TPU v7x, 128 devices: a whole 4x4x4 slice. The times are simulated.
128 devices in a mesh: rep: 2 (over core), dp: 64 (over x, y, z).
Axes of the slice: x: 4, y: 4, z: 4, core: 2. Of those that a mesh axis runs over, the one named last changes fastest.
Arguments:
- x: bfloat16 [128, 1024, 1280], P(('rep', 'dp')), parts along dimension 0
- dy: bfloat16 [128, 1024, 1280], P(('rep', 'dp')), parts along dimension 0
- w_gate: bfloat16 [2, 1280, 4096], replicated
- w_up: bfloat16 [2, 1280, 4096], replicated
- w_down: bfloat16 [2, 4096, 1280], replicated
- m_w_gate: float32 [2, 1280, 4096], P(None, 'dp')
- m_w_up: float32 [2, 1280, 4096], P(None, 'dp')
- m_w_down: float32 [2, 4096, 1280], P(None, 'dp')
- v_w_gate: float32 [2, 1280, 4096], P(None, 'dp')
- v_w_up: float32 [2, 1280, 4096], P(None, 'dp')
- v_w_down: float32 [2, 4096, 1280], P(None, 'dp')
Outputs:
- output 1: bfloat16 [4, 1280, 4096], P('rep'), parts along dimension 0
- output 2: bfloat16 [4, 1280, 4096], P('rep'), parts along dimension 0
- output 3: bfloat16 [4, 4096, 1280], P('rep'), parts along dimension 0
- output 4: float32 [4, 1280, 4096], P('rep', 'dp'), parts along dimension 0
- output 5: float32 [4, 1280, 4096], P('rep', 'dp'), parts along dimension 0
- output 6: float32 [4, 4096, 1280], P('rep', 'dp'), parts along dimension 0
- output 7: float32 [4, 1280, 4096], P('rep', 'dp'), parts along dimension 0
- output 8: float32 [4, 1280, 4096], P('rep', 'dp'), parts along dimension 0
- output 9: float32 [4, 4096, 1280], P('rep', 'dp'), parts along dimension 0
There are 2 independent parts. A program takes and returns all parts, laid end to end along the dimension named above; an argument that names none is the same for every part.
All inputs are finite; a program needn't handle non-finite values.
Results may differ from a plain program's by a relative error of at most 0.022.
Values are sent between devices in bfloat16 or wider.
A program may use at most 1.5 GiB of HBM per device.

v0:
```python
import jax
import jax.numpy as jnp
from jax import lax

NAMES = ("w_gate", "w_up", "w_down")


def matmul(a, w):
    return jnp.dot(a, w, preferred_element_type=jnp.float32).astype(jnp.bfloat16)


def normed(h):
    wide = h.astype(jnp.float32)
    scale = lax.rsqrt(jnp.mean(wide**2, -1, keepdims=True) + 1e-6)
    return (wide * scale).astype(jnp.bfloat16)


def layer(h, w):
    a = normed(h)
    gate = jnp.dot(a, w["w_gate"], preferred_element_type=jnp.float32)
    up = jnp.dot(a, w["w_up"], preferred_element_type=jnp.float32)
    return h + matmul((jax.nn.silu(gate) * up).astype(jnp.bfloat16), w["w_down"])


def adamw(w, m, v, g):
    m = 0.9 * m + 0.1 * g
    v = 0.95 * v + 0.05 * g * g
    step = m * lax.rsqrt(v + 1e-8) + 0.1 * w
    return (w - 0.02 * step).astype(jnp.bfloat16), m, v


def stack(weights, h):
    for number in range(weights["w_gate"].shape[0]):
        h = layer(h, {name: w[number] for name, w in weights.items()})
    return h


def solution(mesh):
    groups = mesh.shape["rep"]

    def step(x, dy, *arrays):
        weights, m, v = (arrays[i : i + 3] for i in (0, 3, 6))
        x, dy = (t.reshape(groups, -1, *t.shape[1:]) for t in (x, dy))

        def of_a_group(x, dy):
            _, back = jax.vjp(lambda w: stack(w, x), dict(zip(NAMES, weights, strict=True)))
            by_weights = back(dy)[0]
            gradients = [by_weights[name].astype(jnp.float32) for name in NAMES]
            new = [adamw(w.astype(jnp.float32), m, v, g) for w, m, v, g in zip(weights, m, v, gradients, strict=True)]
            return tuple(one[which] for which in range(3) for one in new)

        return tuple(t.reshape(-1, *t.shape[2:]) for t in jax.vmap(of_a_group)(x, dy))

    return step
```

profile of v0, /device:TPU:0, one launch (start us, length us, event | category | flops | bytes accessed | tf_op | source)
XLA Modules:
  0.0 2419.8 jit_solution(1531446790707027202)
XLA Ops:
  7.2 2.3 fusion.67
  9.6 14.6 fusion.42
  24.2 23.5 fusion.40
  47.7 11.0 fusion.53
  58.7 17.2 fusion.71
  76.6 17.4 fusion.29
  94.0 17.4 fusion.32
  111.4 21.8 convolution_bitcast_fusion.1
  133.3 17.5 fusion.64
  150.8 15.0 fusion.9
  165.8 3.3 copy-done.1
  169.1 16.3 fusion.74
  185.4 24.5 %fusion.73 = (f32[1024]{0:T(1024)S(1)}, bf16[1,1,1024,1280]{3,2,1,0:T(8,128)(2,1)}) fusion(bf16[1,1,1024,1280]{3,2,1,0:T(8,128)(2,1)} %copy-done.24, bf16[1024,1280]{1,0:T(8,128)(2,1)} %fusion.74, bf16[2,1280,4096]{2,1,0:T(8,128)(2,1)} %param.3, bf16[1024,4096]{1,0:T(8,128)(2,1)} %fusion.64, f32[1024,4096]{1,0:T(8,128)} %fusion.29), kind=kOutput, calls=%fused_computation.86 | convolution fusion | flops 10770447360 | bytes 43520000 | tf_op jit(solution)/vmap(transpose(jvp()))/dot_general | solution.py:21
  209.9 20.2 convolution_bitcast_fusion
  230.2 19.0 fusion.61
  249.2 21.4 convolution_bitcast_fusion.3
  270.5 20.9 convolution_bitcast_fusion.2
  291.4 912.2 %fusion.153 = (f32[24,4096]{1,0:T(8,128)S(1)}, f32[24,4096]{1,0:T(8,128)S(1)}) fusion(f32[1,1280,4096]{2,1,0:T(8,128)} %convolution_bitcast_fusion.2, f32[1,1280,4096]{2,1,0:T(8,128)} %convolution_bitcast_fusion.3), kind=kCustom, calls=%all-reduce-scatter.5 | all-reduce-scatter fusion | flops 12582913 | bytes 42729984
  1212.9 7.0 collective-permute-start.27
  1222.6 16.2 collective-permute-start.30
  1238.8 4.0 collective-permute-start.31
  1242.8 2.5 collective-permute-start.22
  1246.0 2.8 collective-permute-start.34
  1248.8 2.8 collective-permute-start.35
  1251.6 2.9 collective-permute-start.36
  1254.5 18.2 collective-permute-start.37
  1272.8 3.2 collective-permute-start.38
  1276.0 6.5 collective-permute-start.39
  1284.5 2.0 collective-permute-start.41
  1286.5 2.5 collective-permute-start.42
  1289.0 2.6 collective-permute-start.33
  1293.5 17.0 concatenate.2
  1310.6 35.2 %concatenate.3 = bf16[276,4096]{1,0:T(8,128)(2,1)} concatenate(bf16[12,4096]{1,0:T(8,128)(2,1)} %collective-permute-done.43, bf16[24,4096]{1,0:T(8,128)(2,1)} %collective-permute-done.42, bf16[24,4096]{1,0:T(8,128)(2,1)} %collective-permute-done.41, bf16[24,4096]{1,0:T(8,128)(2,1)} %collective-permute-done.40, bf16[24,4096]{1,0:T(8,128)(2,1)} %collective-permute-done.39, ...), dimensions={0} | concatenate | bytes 4718592
  1346.9 2.6 fusion.135
  1350.6 18.8 convolution_bitcast_fusion.5
  1369.4 27.8 %convolution_bitcast_fusion.4 = f32[1,1280,4096]{2,1,0:T(8,128)} fusion(f32[1024,4096]{1,0:T(8,128)} %copy-done, f32[1024,4096]{1,0:T(8,128)} %fusion.40, bf16[1024,4096]{1,0:T(8,128)(2,1)} %fusion.61, bf16[1,1024,1280]{2,1,0:T(8,128)(2,1)} %param.2, f32[1024]{0:T(1024)S(1)} %copy-done.19), kind=kOutput, calls=%fused_computation.10 | convolution fusion | flops 10787487744 | bytes 65540096 | tf_op jit(solution)/vmap(transpose(jvp()))/dot_general | solution.py:20
  1397.2 561.8 %fusion.152 = (f32[24,4096]{1,0:T(8,128)S(1)}, f32[24,4096]{1,0:T(8,128)S(1)}) fusion(f32[1,1280,4096]{2,1,0:T(8,128)} %convolution_bitcast_fusion.4, f32[1,1280,4096]{2,1,0:T(8,128)} %convolution_bitcast_fusion.5), kind=kCustom, calls=%all-reduce-scatter.4 | all-reduce-scatter fusion | flops 12582913 | bytes 42729984
  1961.7 5.8 collective-permute-start.1
  1967.6 9.8 collective-permute-start.2
  1978.7 2.3 collective-permute-start.4
  1981.0 4.5 collective-permute-start.5
  1985.6 3.7 collective-permute-start.6
  1989.3 3.3 collective-permute-start.7
  1992.6 9.7 collective-permute-start.8
  2002.4 10.1 collective-permute-start.9
  2012.5 2.0 collective-permute-start
  2015.1 11.4 collective-permute-start.12
  2026.5 11.5 collective-permute-start.13
  2038.1 2.0 collective-permute-start.14
  2040.0 2.2 collective-permute-start.15
  2042.2 10.7 collective-permute-start.16
  2054.9 15.8 collective-permute-start.18
  2070.7 5.7 collective-permute-start.19
  2076.4 7.1 collective-permute-start.20
  2083.5 2.0 collective-permute-start.11
  2085.5 33.9 %concatenate = bf16[276,4096]{1,0:T(8,128)(2,1)} concatenate(bf16[12,4096]{1,0:T(8,128)(2,1)} %copy-done.15, bf16[24,4096]{1,0:T(8,128)(2,1)} %collective-permute-done.9, bf16[24,4096]{1,0:T(8,128)(2,1)} %collective-permute-done.8, bf16[24,4096]{1,0:T(8,128)(2,1)} %collective-permute-done.7, bf16[24,4096]{1,0:T(8,128)(2,1)S(1)} %collective-permute-done.6, ...), dimensions={0} | concatenate | bytes 4718592
  2119.5 35.2 %concatenate.1 = bf16[276,4096]{1,0:T(8,128)(2,1)} concatenate(bf16[12,4096]{1,0:T(8,128)(2,1)} %copy-done.14, bf16[24,4096]{1,0:T(8,128)(2,1)} %collective-permute-done.20, bf16[24,4096]{1,0:T(8,128)(2,1)} %collective-permute-done.19, bf16[24,4096]{1,0:T(8,128)(2,1)} %collective-permute-done.18, bf16[24,4096]{1,0:T(8,128)(2,1)} %collective-permute-done.17, ...), dimensions={0} | concatenate | bytes 4718592
  2156.7 2.6 fusion.136
  2162.4 2.9 fusion.138
  2170.7 22.7 copy.15
  2193.4 82.7 %all-gather.10.cloned.1.call-done = bf16[1,2,1280,4096]{3,1,0,2:T(2,128)(2,1)} async-done(((bf16[1,2,20,4096]{3,1,0,2:T(2,128)(2,1)}), bf16[1,2,1280,4096]{3,1,0,2:T(2,128)(2,1)}) %all-gather.10.cloned.1.call-update) | async-done | bytes 20971536 | tf_op jit(solution)/reshape | solution.py:52
  2276.1 22.7 copy.14
  2298.8 97.1 %all-gather.14.cloned.1.call-done = bf16[1,2,4096,1280]{3,2,1,0:T(8,128)(2,1)} async-done(((bf16[1,2,64,1280]{3,2,1,0:T(8,128)(2,1)}), bf16[1,2,4096,1280]{3,2,1,0:T(8,128)(2,1)}) %all-gather.14.cloned.1.call-update) | async-done | bytes 20971536 | tf_op jit(solution)/reshape | solution.py:52
  2395.8 17.1 copy.57
  (144 shorter events, 35.5 us)
Async XLA Ops:
  7.2 2153.2 %reduce-scatter.23.cloned.1.call-start = ((), (), s32[]{:S(2)}) async-start(), calls=%async_computation.5 | async-start | bytes 21299200
  24.2 23.5 copy-start
  133.3 2028.2 %reduce-scatter.25.cloned.1.call-start = ((), (), s32[]{:S(2)}) async-start(), calls=%async_computation.6 | async-start | bytes 21299200
  185.4 24.5 %copy-start.17 = (f32[1024]{0:T(1024)S(1)}, f32[1024]{0:T(1024)}, u32[]{:S(2)}) copy-start(f32[1024]{0:T(1024)} %copy-done.16) | copy-start | bytes 12292
  185.4 24.5 %copy-start.21 = (f32[1,1,1024]{2,1,0:T(1,128)S(1)}, f32[1,1,1024]{2,1,0:T(1,128)}, u32[]{:S(2)}) copy-start(f32[1,1,1024]{2,1,0:T(1,128)} %copy-done.20) | copy-start | bytes 12292
  230.1 1940.6 %all-gather.12.cloned.1.call-start = ((), (), s32[]{:S(2)}) async-start(), calls=%async_computation.3 | async-start | bytes 21299200 | tf_op jit(solution)/reshape | solution.py:52
  249.2 21.4 copy-start.2
  249.2 21.4 copy-start.19
  291.4 1000.2 %copy-start.22 = (u32[128]{0:T(128)S(1)}, u32[128]{0:T(128)}, u32[]{:S(2)}) copy-start(u32[128]{0:T(128)} %constant.62) | copy-start | bytes 1540
  1203.7 7.9 collective-permute-start.32
  1205.7 7.2 collective-permute-start.43
  1207.7 12.2 collective-permute-start.23
  1209.0 12.2 collective-permute-start.24
  1210.3 12.3 collective-permute-start.25
  1211.6 27.2 %collective-permute-start.26 = (bf16[24,4096]{1,0:T(8,128)(2,1)S(1)}, bf16[24,4096]{1,0:T(8,128)(2,1)S(1)}, u32[]{:S(2)}, u32[]{:S(2)}) collective-permute-start(bf16[24,4096]{1,0:T(8,128)(2,1)S(1)} %convert.124), channel_id=1, source_target_pairs={{0,5},{1,6},{2,7},{3,8},{4,9},{5,10},{6,11},{7,12},{8,13},{9,14},{... | collective-permute-start | bytes 589832
  1212.9 29.9 %collective-permute-start.27 = (bf16[24,4096]{1,0:T(8,128)(2,1)S(1)}, bf16[24,4096]{1,0:T(8,128)(2,1)S(1)}, u32[]{:S(2)}, u32[]{:S(2)}) collective-permute-start(bf16[24,4096]{1,0:T(8,128)(2,1)S(1)} %convert.124), channel_id=1, source_target_pairs={{0,6},{1,7},{2,8},{3,9},{4,10},{5,11},{6,12},{7,13},{8,14},{9,15},... | collective-permute-start | bytes 589832
  1219.9 26.1 %collective-permute-start.28 = (bf16[24,4096]{1,0:T(8,128)(2,1)S(1)}, bf16[24,4096]{1,0:T(8,128)(2,1)S(1)}, u32[]{:S(2)}, u32[]{:S(2)}) collective-permute-start(bf16[24,4096]{1,0:T(8,128)(2,1)S(1)} %convert.124), channel_id=1, source_target_pairs={{0,7},{1,8},{2,9},{3,10},{4,11},{5,12},{6,13},{7,14},{8,15},{9,16}... | collective-permute-start | bytes 589832
  1221.2 27.6 %collective-permute-start.29 = (bf16[24,4096]{1,0:T(8,128)(2,1)S(1)}, bf16[24,4096]{1,0:T(8,128)(2,1)S(1)}, u32[]{:S(2)}, u32[]{:S(2)}) collective-permute-start(bf16[24,4096]{1,0:T(8,128)(2,1)S(1)} %convert.124), channel_id=1, source_target_pairs={{0,8},{1,9},{2,10},{3,11},{4,12},{5,13},{6,14},{7,15},{8,16},{9,17... | collective-permute-start | bytes 589832
  1222.5 70.8 %copy-start.3 = (bf16[24,4096]{1,0:T(8,128)(2,1)}, bf16[24,4096]{1,0:T(8,128)(2,1)S(1)}, u32[]{:S(2)}) copy-start(bf16[24,4096]{1,0:T(8,128)(2,1)S(1)} %collective-permute-done.25) | copy-start | bytes 589828
  1222.6 29.0 %collective-permute-start.30 = (bf16[24,4096]{1,0:T(8,128)(2,1)S(1)}, bf16[24,4096]{1,0:T(8,128)(2,1)S(1)}, u32[]{:S(2)}, u32[]{:S(2)}) collective-permute-start(bf16[24,4096]{1,0:T(8,128)(2,1)S(1)} %convert.124), channel_id=1, source_target_pairs={{0,9},{1,10},{2,11},{3,12},{4,13},{5,14},{6,15},{7,16},{8,17},{9,1... | collective-permute-start | bytes 589832
  1238.8 54.6 %copy-start.4 = (bf16[24,4096]{1,0:T(8,128)(2,1)}, bf16[24,4096]{1,0:T(8,128)(2,1)S(1)}, u32[]{:S(2)}) copy-start(bf16[24,4096]{1,0:T(8,128)(2,1)S(1)} %collective-permute-done.26) | copy-start | bytes 589828
  1238.8 15.7 collective-permute-start.31
  1242.8 50.6 %copy-start.5 = (bf16[24,4096]{1,0:T(8,128)(2,1)}, bf16[24,4096]{1,0:T(8,128)(2,1)S(1)}, u32[]{:S(2)}) copy-start(bf16[24,4096]{1,0:T(8,128)(2,1)S(1)} %collective-permute-done.27) | copy-start | bytes 589828
  1242.8 29.9 %collective-permute-start.22 = (bf16[24,4096]{1,0:T(8,128)(2,1)S(1)}, bf16[24,4096]{1,0:T(8,128)(2,1)S(1)}, u32[]{:S(2)}, u32[]{:S(2)}) collective-permute-start(bf16[24,4096]{1,0:T(8,128)(2,1)S(1)} %convert.124), channel_id=1, source_target_pairs={{0,1},{1,2},{2,3},{3,4},{4,5},{5,6},{6,7},{7,8},{8,9},{9,10},{10,1... | collective-permute-start | bytes 589832
  1246.0 47.4 %copy-start.6 = (bf16[24,4096]{1,0:T(8,128)(2,1)}, bf16[24,4096]{1,0:T(8,128)(2,1)S(1)}, u32[]{:S(2)}) copy-start(bf16[24,4096]{1,0:T(8,128)(2,1)S(1)} %collective-permute-done.28) | copy-start | bytes 589828
  1246.0 30.0 %collective-permute-start.34 = (bf16[24,4096]{1,0:T(8,128)(2,1)}, bf16[24,4096]{1,0:T(8,128)(2,1)S(1)}, u32[]{:S(2)}, u32[]{:S(2)}) collective-permute-start(bf16[24,4096]{1,0:T(8,128)(2,1)} %convert.125), channel_id=1, source_target_pairs={{0,2},{1,3},{2,4},{3,5},{4,6},{5,7},{6,8},{7,9},{8,10},{9,11},{10,... | collective-permute-start | bytes 589832
  1248.8 44.6 %copy-start.7 = (bf16[24,4096]{1,0:T(8,128)(2,1)}, bf16[24,4096]{1,0:T(8,128)(2,1)S(1)}, u32[]{:S(2)}) copy-start(bf16[24,4096]{1,0:T(8,128)(2,1)S(1)} %collective-permute-done.29) | copy-start | bytes 589828
  1248.8 33.7 %collective-permute-start.35 = (bf16[24,4096]{1,0:T(8,128)(2,1)}, bf16[24,4096]{1,0:T(8,128)(2,1)S(1)}, u32[]{:S(2)}, u32[]{:S(2)}) collective-permute-start(bf16[24,4096]{1,0:T(8,128)(2,1)} %convert.125), channel_id=1, source_target_pairs={{0,3},{1,4},{2,5},{3,6},{4,7},{5,8},{6,9},{7,10},{8,11},{9,12},{10... | collective-permute-start | bytes 589832
  1251.6 41.8 %copy-start.8 = (bf16[24,4096]{1,0:T(8,128)(2,1)}, bf16[24,4096]{1,0:T(8,128)(2,1)S(1)}, u32[]{:S(2)}) copy-start(bf16[24,4096]{1,0:T(8,128)(2,1)S(1)} %collective-permute-done.30) | copy-start | bytes 589828
  1251.6 32.9 %collective-permute-start.36 = (bf16[24,4096]{1,0:T(8,128)(2,1)}, bf16[24,4096]{1,0:T(8,128)(2,1)S(1)}, u32[]{:S(2)}, u32[]{:S(2)}) collective-permute-start(bf16[24,4096]{1,0:T(8,128)(2,1)} %convert.125), channel_id=1, source_target_pairs={{0,4},{1,5},{2,6},{3,7},{4,8},{5,9},{6,10},{7,11},{8,12},{9,13},{1... | collective-permute-start | bytes 589832
  1254.5 38.9 %copy-start.10 = (bf16[24,4096]{1,0:T(8,128)(2,1)}, bf16[24,4096]{1,0:T(8,128)(2,1)S(1)}, u32[]{:S(2)}) copy-start(bf16[24,4096]{1,0:T(8,128)(2,1)S(1)} %collective-permute-done.31) | copy-start | bytes 589828
  1254.5 32.0 %collective-permute-start.37 = (bf16[24,4096]{1,0:T(8,128)(2,1)}, bf16[24,4096]{1,0:T(8,128)(2,1)}, u32[]{:S(2)}, u32[]{:S(2)}) collective-permute-start(bf16[24,4096]{1,0:T(8,128)(2,1)} %convert.125), channel_id=1, source_target_pairs={{0,5},{1,6},{2,7},{3,8},{4,9},{5,10},{6,11},{7,12},{8,13},{9,14},{... | collective-permute-start | bytes 589832
  1272.8 16.2 collective-permute-start.38
  1276.0 34.5 %collective-permute-start.39 = (bf16[24,4096]{1,0:T(8,128)(2,1)}, bf16[24,4096]{1,0:T(8,128)(2,1)}, u32[]{:S(2)}, u32[]{:S(2)}) collective-permute-start(bf16[24,4096]{1,0:T(8,128)(2,1)} %convert.125), channel_id=1, source_target_pairs={{0,7},{1,8},{2,9},{3,10},{4,11},{5,12},{6,13},{7,14},{8,15},{9,16}... | collective-permute-start | bytes 589832
  1282.6 28.0 %collective-permute-start.40 = (bf16[24,4096]{1,0:T(8,128)(2,1)}, bf16[24,4096]{1,0:T(8,128)(2,1)}, u32[]{:S(2)}, u32[]{:S(2)}) collective-permute-start(bf16[24,4096]{1,0:T(8,128)(2,1)} %convert.125), channel_id=1, source_target_pairs={{0,8},{1,9},{2,10},{3,11},{4,12},{5,13},{6,14},{7,15},{8,16},{9,17... | collective-permute-start | bytes 589832
  1284.5 26.1 %collective-permute-start.41 = (bf16[24,4096]{1,0:T(8,128)(2,1)}, bf16[24,4096]{1,0:T(8,128)(2,1)}, u32[]{:S(2)}, u32[]{:S(2)}) collective-permute-start(bf16[24,4096]{1,0:T(8,128)(2,1)} %convert.125), channel_id=1, source_target_pairs={{0,9},{1,10},{2,11},{3,12},{4,13},{5,14},{6,15},{7,16},{8,17},{9,1... | collective-permute-start | bytes 589832
  1286.5 24.1 collective-permute-start.42
  1289.0 21.6 collective-permute-start.33
  1350.5 925.6 %all-gather.10.cloned.1.call-start = ((), (), s32[]{:S(2)}) async-start(), calls=%async_computation.2 | async-start | bytes 21299200 | tf_op jit(solution)/reshape | solution.py:52
  1959.1 19.6 collective-permute-start.10
  1960.4 20.6 collective-permute-start.21
  1961.7 23.8 collective-permute-start.1
  1967.6 21.7 collective-permute-start.2
  1977.4 15.2 collective-permute-start.3
  1978.7 74.3 %copy-start.15 = (bf16[12,4096]{1,0:T(8,128)(2,1)}, bf16[12,4096]{1,0:T(8,128)(2,1)S(1)}, u32[]{:S(2)}) copy-start(bf16[12,4096]{1,0:T(8,128)(2,1)S(1)} %collective-permute-done.10) | copy-start | bytes 294916
  1978.7 23.6 collective-permute-start.4
  1981.0 61.2 %copy-start.14 = (bf16[12,4096]{1,0:T(8,128)(2,1)}, bf16[12,4096]{1,0:T(8,128)(2,1)S(1)}, u32[]{:S(2)}) copy-start(bf16[12,4096]{1,0:T(8,128)(2,1)S(1)} %collective-permute-done.21) | copy-start | bytes 294916
  1981.0 31.4 %collective-permute-start.5 = (bf16[24,4096]{1,0:T(8,128)(2,1)S(1)}, bf16[24,4096]{1,0:T(8,128)(2,1)S(1)}, u32[]{:S(2)}, u32[]{:S(2)}) collective-permute-start(bf16[24,4096]{1,0:T(8,128)(2,1)S(1)} %convert.126), channel_id=1, source_target_pairs={{0,6},{1,7},{2,8},{3,9},{4,10},{5,11},{6,12},{7,13},{8,14},{9,15},... | collective-permute-start | bytes 589832
  1985.6 29.5 %collective-permute-start.6 = (bf16[24,4096]{1,0:T(8,128)(2,1)S(1)}, bf16[24,4096]{1,0:T(8,128)(2,1)S(1)}, u32[]{:S(2)}, u32[]{:S(2)}) collective-permute-start(bf16[24,4096]{1,0:T(8,128)(2,1)S(1)} %convert.126), channel_id=1, source_target_pairs={{0,7},{1,8},{2,9},{3,10},{4,11},{5,12},{6,13},{7,14},{8,15},{9,16}... | collective-permute-start | bytes 589832
  1989.3 37.2 %collective-permute-start.7 = (bf16[24,4096]{1,0:T(8,128)(2,1)S(1)}, bf16[24,4096]{1,0:T(8,128)(2,1)}, u32[]{:S(2)}, u32[]{:S(2)}) collective-permute-start(bf16[24,4096]{1,0:T(8,128)(2,1)S(1)} %convert.126), channel_id=1, source_target_pairs={{0,8},{1,9},{2,10},{3,11},{4,12},{5,13},{6,14},{7,15},{8,16},{9,17... | collective-permute-start | bytes 589832
  1992.6 45.5 %collective-permute-start.8 = (bf16[24,4096]{1,0:T(8,128)(2,1)S(1)}, bf16[24,4096]{1,0:T(8,128)(2,1)}, u32[]{:S(2)}, u32[]{:S(2)}) collective-permute-start(bf16[24,4096]{1,0:T(8,128)(2,1)S(1)} %convert.126), channel_id=1, source_target_pairs={{0,9},{1,10},{2,11},{3,12},{4,13},{5,14},{6,15},{7,16},{8,17},{9,1... | collective-permute-start | bytes 589832
  2002.4 37.7 %collective-permute-start.9 = (bf16[24,4096]{1,0:T(8,128)(2,1)S(1)}, bf16[24,4096]{1,0:T(8,128)(2,1)}, u32[]{:S(2)}, u32[]{:S(2)}) collective-permute-start(bf16[24,4096]{1,0:T(8,128)(2,1)S(1)} %convert.126), channel_id=1, source_target_pairs={{0,10},{1,11},{2,12},{3,13},{4,14},{5,15},{6,16},{7,17},{8,18},{9,... | collective-permute-start | bytes 589832
  2012.5 29.8 %collective-permute-start = (bf16[24,4096]{1,0:T(8,128)(2,1)S(1)}, bf16[24,4096]{1,0:T(8,128)(2,1)}, u32[]{:S(2)}, u32[]{:S(2)}) collective-permute-start(bf16[24,4096]{1,0:T(8,128)(2,1)S(1)} %convert.126), channel_id=1, source_target_pairs={{0,1},{1,2},{2,3},{3,4},{4,5},{5,6},{6,7},{7,8},{8,9},{9,10},{10,1... | collective-permute-start | bytes 589832
  2015.1 37.9 %collective-permute-start.12 = (bf16[24,4096]{1,0:T(8,128)(2,1)}, bf16[24,4096]{1,0:T(8,128)(2,1)}, u32[]{:S(2)}, u32[]{:S(2)}) collective-permute-start(bf16[24,4096]{1,0:T(8,128)(2,1)} %convert.127), channel_id=1, source_target_pairs={{0,2},{1,3},{2,4},{3,5},{4,6},{5,7},{6,8},{7,9},{8,10},{9,11},{10,... | collective-permute-start | bytes 589832
  2026.5 28.4 %collective-permute-start.13 = (bf16[24,4096]{1,0:T(8,128)(2,1)}, bf16[24,4096]{1,0:T(8,128)(2,1)}, u32[]{:S(2)}, u32[]{:S(2)}) collective-permute-start(bf16[24,4096]{1,0:T(8,128)(2,1)} %convert.127), channel_id=1, source_target_pairs={{0,3},{1,4},{2,5},{3,6},{4,7},{5,8},{6,9},{7,10},{8,11},{9,12},{10... | collective-permute-start | bytes 589832
  2038.1 32.7 %collective-permute-start.14 = (bf16[24,4096]{1,0:T(8,128)(2,1)}, bf16[24,4096]{1,0:T(8,128)(2,1)}, u32[]{:S(2)}, u32[]{:S(2)}) collective-permute-start(bf16[24,4096]{1,0:T(8,128)(2,1)} %convert.127), channel_id=1, source_target_pairs={{0,4},{1,5},{2,6},{3,7},{4,8},{5,9},{6,10},{7,11},{8,12},{9,13},{1... | collective-permute-start | bytes 589832
  2040.0 36.4 %collective-permute-start.15 = (bf16[24,4096]{1,0:T(8,128)(2,1)}, bf16[24,4096]{1,0:T(8,128)(2,1)}, u32[]{:S(2)}, u32[]{:S(2)}) collective-permute-start(bf16[24,4096]{1,0:T(8,128)(2,1)} %convert.127), channel_id=1, source_target_pairs={{0,5},{1,6},{2,7},{3,8},{4,9},{5,10},{6,11},{7,12},{8,13},{9,14},{... | collective-permute-start | bytes 589832
  2042.2 41.3 %collective-permute-start.16 = (bf16[24,4096]{1,0:T(8,128)(2,1)}, bf16[24,4096]{1,0:T(8,128)(2,1)}, u32[]{:S(2)}, u32[]{:S(2)}) collective-permute-start(bf16[24,4096]{1,0:T(8,128)(2,1)} %convert.127), channel_id=1, source_target_pairs={{0,6},{1,7},{2,8},{3,9},{4,10},{5,11},{6,12},{7,13},{8,14},{9,15},... | collective-permute-start | bytes 589832
  2053.0 66.5 %collective-permute-start.17 = (bf16[24,4096]{1,0:T(8,128)(2,1)}, bf16[24,4096]{1,0:T(8,128)(2,1)}, u32[]{:S(2)}, u32[]{:S(2)}) collective-permute-start(bf16[24,4096]{1,0:T(8,128)(2,1)} %convert.127), channel_id=1, source_target_pairs={{0,7},{1,8},{2,9},{3,10},{4,11},{5,12},{6,13},{7,14},{8,15},{9,16}... | collective-permute-start | bytes 589832
  2054.9 64.5 %collective-permute-start.18 = (bf16[24,4096]{1,0:T(8,128)(2,1)}, bf16[24,4096]{1,0:T(8,128)(2,1)}, u32[]{:S(2)}, u32[]{:S(2)}) collective-permute-start(bf16[24,4096]{1,0:T(8,128)(2,1)} %convert.127), channel_id=1, source_target_pairs={{0,8},{1,9},{2,10},{3,11},{4,12},{5,13},{6,14},{7,15},{8,16},{9,17... | collective-permute-start | bytes 589832
  2070.7 48.7 %collective-permute-start.19 = (bf16[24,4096]{1,0:T(8,128)(2,1)}, bf16[24,4096]{1,0:T(8,128)(2,1)}, u32[]{:S(2)}, u32[]{:S(2)}) collective-permute-start(bf16[24,4096]{1,0:T(8,128)(2,1)} %convert.127), channel_id=1, source_target_pairs={{0,9},{1,10},{2,11},{3,12},{4,13},{5,14},{6,15},{7,16},{8,17},{9,1... | collective-permute-start | bytes 589832
  2076.4 43.0 %collective-permute-start.20 = (bf16[24,4096]{1,0:T(8,128)(2,1)}, bf16[24,4096]{1,0:T(8,128)(2,1)}, u32[]{:S(2)}, u32[]{:S(2)}) collective-permute-start(bf16[24,4096]{1,0:T(8,128)(2,1)} %convert.127), channel_id=1, source_target_pairs={{0,10},{1,11},{2,12},{3,13},{4,14},{5,15},{6,16},{7,17},{8,18},{9,... | collective-permute-start | bytes 589832
  2083.5 35.9 %collective-permute-start.11 = (bf16[24,4096]{1,0:T(8,128)(2,1)}, bf16[24,4096]{1,0:T(8,128)(2,1)}, u32[]{:S(2)}, u32[]{:S(2)}) collective-permute-start(bf16[24,4096]{1,0:T(8,128)(2,1)} %convert.127), channel_id=1, source_target_pairs={{0,1},{1,2},{2,3},{3,4},{4,5},{5,6},{6,7},{7,8},{8,9},{9,10},{10,1... | collective-permute-start | bytes 589832
  2160.3 235.5 %all-gather.14.cloned.1.call-start = ((), (), s32[]{:S(2)}) async-start(), calls=%async_computation.4 | async-start | bytes 21299200 | tf_op jit(solution)/reshape | solution.py:52
  (10 other events, 129.6 us)
Sparse Core Ops, SparseCore 0:
  133.4 447.7 reduce-scatter.22
  584.1 470.4 reduce-scatter.24
  1350.7 677.2 all-gather.11
  2160.5 115.5 all-gather.9
  2278.8 116.9 all-gather.13
where the time goes:
time: 2440 us; the launch traced here: 2420 us
  blocking collectives  1470 us (60%)
  matrix products  298 us (12%)
  starting transfers between devices  213 us (9%)
  local copies, waits for them, and re-layouts  199 us (8%)
  waiting for transfers between devices  180 us (7%)
  other arithmetic  39.7 us (2%)
    unnamed x2, blocking collectives  1470 us
    unnamed x46, starting transfers between devices  212 us
    unnamed x66, local copies, waits for them, and re-layouts  194 us
    reshape x3, waiting for transfers between devices, step(): t.reshape(-1, *t.shape[2:])  180 us
    dot_general x5, matrix products, layer(): up = jnp.dot(a, w['w_up'], preferred_element_type=jnp.float32)  108 us
    dot_general x5, matrix products, matmul(): jnp.dot(a, w, preferred_element_type=jnp.float32).astype(jnp.bfloat16)  95.7 us
    dot_general x5, matrix products, layer(): gate = jnp.dot(a, w['w_gate'], preferred_element_type=jnp.float32)  94.9 us
  transfers between devices with their start and end apart: 49, of which 2 were waited for; matrix products, arithmetic and copies ran while one was open for 77% of the time, Pallas kernels for 0%

commit v1 on v0

v1 whole, which is shorter than its diff:
```python
import jax
import jax.numpy as jnp
from jax import lax
from jax.sharding import PartitionSpec as P

NAMES = ("w_gate", "w_up", "w_down")


def dot(a, b, dims):
    return lax.dot_general(a, b, (dims, ((), ())), preferred_element_type=jnp.float32)


def scale_of(h):
    wide = h.astype(jnp.float32)
    return lax.rsqrt(jnp.mean(wide**2, -1, keepdims=True) + 1e-6)


def hidden(a, w_gate, w_up):
    gate, up = dot(a, w_gate, ((1,), (0,))), dot(a, w_up, ((1,), (0,)))
    return gate, up, (jax.nn.silu(gate) * up).astype(jnp.bfloat16)


def of_hidden(d, gate, up):
    d = d.astype(jnp.float32)
    s = jax.nn.sigmoid(gate)
    d_gate = d * up * (s * (1 + gate * (1 - s)))
    return d_gate.astype(jnp.bfloat16), (d * (gate * s)).astype(jnp.bfloat16)


def of_norm(h, scale, d):
    wide, d = h.astype(jnp.float32), d.astype(jnp.float32)
    along = jnp.mean(wide * d, -1, keepdims=True)
    return (scale * d - wide * (scale * scale * scale) * along).astype(jnp.bfloat16)


def adamw(w, m, v, g):
    m = 0.9 * m + 0.1 * g
    v = 0.95 * v + 0.05 * g * g
    step = m * lax.rsqrt(v + 1e-8) + 0.1 * w
    return (w - 0.02 * step).astype(jnp.bfloat16), m, v


def solution(mesh):
    n = mesh.shape["dp"]

    def step(x, dy, wg, wu, wd, mg, mu, md, vg, vu, vd):
        bf = jnp.bfloat16
        h0, dy = x[0], dy[0]
        s0 = scale_of(h0)
        a0 = (h0.astype(jnp.float32) * s0).astype(bf)
        g0, u0, p0 = hidden(a0, wg[0], wu[0])
        h1 = h0 + dot(p0, wd[0], ((1,), (0,))).astype(bf)
        s1 = scale_of(h1)
        a1 = (h1.astype(jnp.float32) * s1).astype(bf)
        g1, u1, p1 = hidden(a1, wg[1], wu[1])
        down1 = dot(p1, dy, ((0,), (0,))).astype(bf)
        dg1, du1 = of_hidden(dot(dy, wd[1], ((1,), (1,))).astype(bf), g1, u1)
        gate1 = dot(a1, dg1, ((0,), (0,))).astype(bf)
        up1 = dot(a1, du1, ((0,), (0,))).astype(bf)
        da1 = dot(dg1, wg[1], ((1,), (1,))) + dot(du1, wu[1], ((1,), (1,)))
        dh1 = dy + of_norm(h1, s1, da1)
        down0 = dot(p0, dh1, ((0,), (0,))).astype(bf)
        dg0, du0 = of_hidden(dot(dh1, wd[0], ((1,), (1,))).astype(bf), g0, u0)
        gate0 = dot(a0, dg0, ((0,), (0,))).astype(bf)
        up0 = dot(a0, du0, ((0,), (0,))).astype(bf)

        def summed(gate, up, down):
            parts = [t.reshape(n, -1, 1280) for t in (gate, up, down)]
            return lax.psum_scatter(jnp.concatenate(parts, 1), "dp", scatter_dimension=0, tiled=True)[0]

        me = lax.axis_index("dp")
        news = [None, None]
        for layer, grads in ((1, (gate1, up1, down1)), (0, (gate0, up0, down0))):
            total = summed(*grads).astype(jnp.float32)
            out = []
            for i, (w, m, v) in enumerate(((wg, mg, vg), (wu, mu, vu), (wd, md, vd))):
                rows, cols = m.shape[1:]
                g = total[64 * i : 64 * i + 64].reshape(rows, cols)
                mine = lax.dynamic_slice(w[layer], (me * rows, 0), (rows, cols)).astype(jnp.float32)
                out.append(adamw(mine, m[layer], v[layer], g))
            whole = lax.all_gather(jnp.concatenate([o[0].reshape(64, 1280) for o in out]), "dp")
            news[layer] = [(whole[:, 64 * i : 64 * i + 64].reshape(w.shape[1:]), *out[i][1:]) for i, w in enumerate((wg, wu, wd))]
        return tuple(jnp.stack([news[0][i][which], news[1][i][which]]) for which in range(3) for i in range(3))

    seq, whole, rows = P(("rep", "dp")), P(), P(None, "dp", None)
    return jax.shard_map(
        step,
        mesh=mesh,
        in_specs=(seq, seq) + (whole,) * 3 + (rows,) * 6,
        out_specs=(P("rep"),) * 3 + (P("rep", "dp", None),) * 6,
        check_vma=False,
    )
```

time: 2440 us -> 1320 us (0.54)
  blocking collectives: 1470 us -> 0 us
  waiting for transfers between devices: 180 us -> 614 us
  starting transfers between devices: 213 us -> 0.16 us
  other arithmetic: 39.7 us -> 114 us
  local copies, waits for them, and re-layouts: 199 us -> 272 us
    unnamed x2 -> x0, blocking collectives: 1470 us -> none
    reduce_scatter x0 -> x2, waiting for transfers between devices: none -> 355 us  [summed(): lax.psum_scatter(jnp.concatenate(parts, 1), 'dp', scatter_dimension=0, ti...]
    all_gather x0 -> x2, waiting for transfers between devices: none -> 259 us  [step(): lax.all_gather(jnp.concatenate([o[0].reshape(64, 1280) for o in out]), 'dp')]
    unnamed x46 -> x0, starting transfers between devices: 212 us -> none
    unnamed x66 -> x70, local copies, waits for them, and re-layouts: 194 us -> 7.16 us
    reshape x3 -> x0, waiting for transfers between devices: 180 us -> none  [step(): t.reshape(-1, *t.shape[2:])]
    slice x0 -> x11, local copies, waits for them, and re-layouts: none -> 95.1 us  [the longest x2 44.7 us: step(): whole[:, 64 * i:64 * i + 64].reshape(w.shape[1:])]
    reshape x0 -> x8, local copies, waits for them, and re-layouts: none -> 75.6 us  [the longest x4 73.8 us: summed(): parts = [t.reshape(n, -1, 1280) for t in (gate, up, down)]]
  transfers between devices with their start and end apart: 49 -> 4, of which waited for: 2 -> 4; matrix products, arithmetic and copies ran while one was open for 77% -> 16% of each run, Pallas kernels for 0% -> 0%
where the time goes in v1:
time: 1320 us; the launch traced here: 1310 us
  waiting for transfers between devices  614 us (47%)
  matrix products  292 us (22%)
  local copies, waits for them, and re-layouts  272 us (21%)
  other arithmetic  114 us (9%)
  between operations  14.4 us (1%)
    reduce_scatter x2, waiting for transfers between devices, summed(): lax.psum_scatter(jnp.concatenate(parts, 1), 'dp', scatter_dimension=0, ti...  355 us
    dot_general x15, matrix products, dot(): lax.dot_general(a, b, (dims, ((), ())), preferred_element_type=jnp.float32)  292 us
    all_gather x2, waiting for transfers between devices, step(): lax.all_gather(jnp.concatenate([o[0].reshape(64, 1280) for o in out]), 'dp')  259 us
    another operation x4, local copies, waits for them, and re-layouts, step(): jnp.stack([news[0][i][which], news[1][i][which]])  74.1 us
    reshape x4, local copies, waits for them, and re-layouts, summed(): parts = [t.reshape(n, -1, 1280) for t in (gate, up, down)]  73.8 us
    another operation x9, other arithmetic, step(): jnp.stack([news[0][i][which], news[1][i][which]])  48.7 us
    slice x2, local copies, waits for them, and re-layouts, step(): whole[:, 64 * i:64 * i + 64].reshape(w.shape[1:])  44.7 us
    concatenate x2, other arithmetic, summed(): jnp.concatenate(parts, 1)  43.1 us
  transfers between devices with their start and end apart: 4, of which 4 were waited for; matrix products, arithmetic and copies ran while one was open for 16% of the time, Pallas kernels for 0%

profile of v1, /device:TPU:0, one launch (start us, length us, event | category | flops | bytes accessed | tf_op | source)
XLA Modules:
  0.0 1307.1 jit_solution(1665218448325678582)
XLA Ops:
  7.2 2.3 fusion.34
  9.6 18.1 %fusion.24 = f32[1024,4096]{1,0:T(8,128)} fusion(bf16[1,1024,1280]{2,1,0:T(8,128)(2,1)} %param.11, f32[1024]{0:T(1024)S(1)} %add_rsqrt_fusion.1, bf16[2,1280,4096]{2,1,0:T(8,128)(2,1)} %param.13), kind=kOutput, calls=%fused_computation.43 | convolution fusion | flops 10741350400 | bytes 29888512 | tf_op jit(solution)/shard_map/dot_general | solution.py:10
  27.7 23.8 %multiply_convert_fusion.1 = (bf16[1024,4096]{1,0:T(8,128)(2,1)}, f32[1024,4096]{1,0:T(8,128)}) fusion(f32[1024,4096]{1,0:T(8,128)} %fusion.24, bf16[2,1280,4096]{2,1,0:T(8,128)(2,1)} %param.14, bf16[1,1024,1280]{2,1,0:T(8,128)(2,1)S(1)} %copy-done.2, f32[1024]{0:T(1024)S(1)} %add_rsqrt_fusion.1), kind=kOutput, calls=%fused_computation.18 | convolution fusion | flops 10766516224 | bytes 55054336 | tf_op jit(solution)/shard_map/dot_general | solution.py:10
  51.5 16.8 %fusion.36 = (f32[1024]{0:T(1024)S(1)}, bf16[1024,1280]{1,0:T(8,128)(2,1)S(1)}) fusion(bf16[1024,4096]{1,0:T(8,128)(2,1)} %get-tuple-element.75, bf16[2,4096,1280]{2,1,0:T(8,128)(2,1)} %param.15, bf16[1,1024,1280]{2,1,0:T(8,128)(2,1)S(1)} %copy-done.2), kind=kOutput, calls=%fused_computation.55 | convolution fusion | flops 10743970816 | bytes 24121344 | tf_op jit(solution)/shard_map/dot_general | solution.py:10
  69.0 17.2 %fusion.31 = bf16[1024,4096]{1,0:T(8,128)(2,1)} fusion(bf16[1,1024,1280]{2,1,0:T(8,128)(2,1)S(1)} %copy-done.4, bf16[2,4096,1280]{2,1,0:T(8,128)(2,1)} %param.15), kind=kOutput, calls=%fused_computation.50 | convolution fusion | flops 10741612544 | bytes 21495808 | tf_op jit(solution)/shard_map/dot_general | solution.py:10
  86.2 17.2 %fusion.10 = f32[1024,4096]{1,0:T(8,128)} fusion(bf16[1024,1280]{1,0:T(8,128)(2,1)S(1)} %get-tuple-element.78, f32[1024]{0:T(1024)S(1)} %get-tuple-element.74, bf16[2,1280,4096]{2,1,0:T(8,128)(2,1)} %param.13), kind=kOutput, calls=%fused_computation.29 | convolution fusion | flops 10741350400 | bytes 29888512 | tf_op jit(solution)/shard_map/dot_general | solution.py:10
  103.4 32.5 %fusion.1 = (bf16[1024,4096]{1,0:T(8,128)(2,1)}, bf16[1024,4096]{1,0:T(8,128)(2,1)}, f32[1024,4096]{1,0:T(8,128)}) fusion(bf16[1024,4096]{1,0:T(8,128)(2,1)} %fusion.31, f32[1024,4096]{1,0:T(8,128)} %fusion.10, bf16[2,1280,4096]{2,1,0:T(8,128)(2,1)} %param.14, bf16[1024,1280]{1,0:T(8,128)(2,1)} %copy-done.6, f32[1024]{0:T(1024)S(1)} %get-tuple-element.74), kind=kOutput, calls=%fused_computation.10 | convolution fusion | flops 10800070656 | bytes 71831552 | tf_op jit(solution)/shard_map/dot_general | solution.py:10
  136.0 18.4 %fusion.8 = f32[1024,1280]{1,0:T(8,128)} fusion(bf16[1024,4096]{1,0:T(8,128)(2,1)} %get-tuple-element.24, bf16[2,1280,4096]{2,1,0:T(8,128)(2,1)} %param.13), kind=kOutput, calls=%fused_computation.27 | convolution fusion | flops 10737418240 | bytes 24117248 | tf_op jit(solution)/shard_map/dot_general | solution.py:10
  154.4 19.8 %fusion.41 = (f32[1024]{0:T(1024)S(1)}, f32[1024,1280]{1,0:T(8,128)}) fusion(bf16[1024,1280]{1,0:T(8,128)(2,1)} %copy-done.6, f32[1024,1280]{1,0:T(8,128)} %fusion.8, bf16[1024,4096]{1,0:T(8,128)(2,1)} %get-tuple-element.25, bf16[2,1280,4096]{2,1,0:T(8,128)(2,1)} %param.14), kind=kOutput, calls=%fused_computation.60 | convolution fusion | flops 10742660096 | bytes 31985664 | tf_op jit(solution)/shard_map/dot_general | solution.py:10
  174.2 4.3 fusion.54
  178.5 17.4 %fusion.28 = bf16[1024,4096]{1,0:T(8,128)(2,1)} fusion(bf16[1024,1280]{1,0:T(8,128)(2,1)S(1)} %fusion.54, bf16[2,4096,1280]{2,1,0:T(8,128)(2,1)} %param.15), kind=kOutput, calls=%fused_computation.49 | convolution fusion | flops 10741612544 | bytes 21495808 | tf_op jit(solution)/shard_map/dot_general | solution.py:10
  195.9 13.6 %convolution_convert_fusion.3 = bf16[4096,1280]{1,0:T(8,128)(2,1)} fusion(bf16[1024,4096]{1,0:T(8,128)(2,1)S(1)} %bitcast.181, bf16[1024,1280]{1,0:T(8,128)(2,1)S(1)} %fusion.54), kind=kOutput, calls=%fused_computation.24 | convolution fusion | flops 10742661120 | bytes 21495808 | tf_op jit(solution)/shard_map/dot_general | solution.py:10
  209.5 18.8 %convolution_convert_fusion.4 = bf16[1280,4096]{1,0:T(8,128)(2,1)} fusion(bf16[1024,4096]{1,0:T(8,128)(2,1)} %fusion.28, f32[1024,4096]{1,0:T(8,128)} %fusion.24, bf16[1,1024,1280]{2,1,0:T(8,128)(2,1)S(1)} %copy-done.3, f32[1024]{0:T(1024)S(1)} %copy-done.21), kind=kOutput, calls=%fused_computation.25 | convolution fusion | flops 10775953408 | bytes 38277120 | tf_op jit(solution)/shard_map/dot_general | solution.py:10
  228.3 23.6 %convolution_convert_fusion.5 = bf16[1280,4096]{1,0:T(8,128)(2,1)} fusion(f32[1024,4096]{1,0:T(8,128)} %get-tuple-element.76, bf16[1024,4096]{1,0:T(8,128)(2,1)} %fusion.28, f32[1024,4096]{1,0:T(8,128)} %fusion.24, bf16[1,1024,1280]{2,1,0:T(8,128)(2,1)S(1)} %copy-done.3, f32[1024]{0:T(1024)S(1)} %copy-done.21), kind=kOutput, calls=%fused_computation.26 | convolution fusion | flops 10792730624 | bytes 55054336 | tf_op jit(solution)/shard_map/dot_general | solution.py:10
  251.9 18.4 %reshape.276 = bf16[64,64,1280]{2,1,0:T(8,128)(2,1)} reshape(bf16[1280,4096]{1,0:T(8,128)(2,1)} %convolution_convert_fusion.5) | data formatting | bytes 20971520 | tf_op jit(solution)/shard_map/reshape | solution.py:68
  270.3 18.4 %reshape.277 = bf16[64,64,1280]{2,1,0:T(8,128)(2,1)} reshape(bf16[1280,4096]{1,0:T(8,128)(2,1)} %convolution_convert_fusion.4) | data formatting | bytes 20971520 | tf_op jit(solution)/shard_map/reshape | solution.py:68
  288.7 21.4 %pad_maximum_fusion = bf16[64,192,1280]{2,1,0:T(8,128)(2,1)} fusion(bf16[64,64,1280]{2,1,0:T(8,128)(2,1)} %bitcast.178, bf16[64,64,1280]{2,1,0:T(8,128)(2,1)} %reshape.277, bf16[64,64,1280]{2,1,0:T(8,128)(2,1)} %reshape.276), kind=kLoop, calls=%fused_computation | loop fusion | flops 94371840 | bytes 62914560 | tf_op jit(solution)/shard_map/concatenate | solution.py:69
  310.2 1.6 copy-done.7
  311.9 17.3 %convolution_convert_fusion.2 = bf16[1280,4096]{1,0:T(8,128)(2,1)} fusion(bf16[1024,4096]{1,0:T(8,128)(2,1)} %get-tuple-element.24, bf16[1024,1280]{1,0:T(8,128)(2,1)S(1)} %copy-done.7, f32[1024]{0:T(1024)S(1)} %copy-done.18), kind=kOutput, calls=%fused_computation.23 | convolution fusion | flops 10746593280 | bytes 21499904 | tf_op jit(solution)/shard_map/dot_general | solution.py:10
  329.2 18.4 %reshape.279 = bf16[64,64,1280]{2,1,0:T(8,128)(2,1)} reshape(bf16[1280,4096]{1,0:T(8,128)(2,1)} %convolution_convert_fusion.2) | data formatting | bytes 20971520 | tf_op jit(solution)/shard_map/reshape | solution.py:68
  347.6 17.0 %convolution_convert_fusion.1 = bf16[1280,4096]{1,0:T(8,128)(2,1)} fusion(bf16[1024,4096]{1,0:T(8,128)(2,1)} %get-tuple-element.25, bf16[1024,1280]{1,0:T(8,128)(2,1)S(1)} %copy-done.7, f32[1024]{0:T(1024)S(1)} %copy-done.18), kind=kOutput, calls=%fused_computation.22 | convolution fusion | flops 10746593280 | bytes 21499904 | tf_op jit(solution)/shard_map/dot_general | solution.py:10
  364.7 18.6 %reshape.280 = bf16[64,64,1280]{2,1,0:T(8,128)(2,1)} reshape(bf16[1280,4096]{1,0:T(8,128)(2,1)} %convolution_convert_fusion.1) | data formatting | bytes 20971520 | tf_op jit(solution)/shard_map/reshape | solution.py:68
  383.2 20.6 %convolution_convert_fusion = bf16[4096,1280]{1,0:T(8,128)(2,1)} fusion(f32[1024,4096]{1,0:T(8,128)} %get-tuple-element.79, f32[1024,4096]{1,0:T(8,128)} %fusion.10, bf16[1,1024,1280]{2,1,0:T(8,128)(2,1)S(1)} %copy-done.5), kind=kOutput, calls=%fused_computation.21 | convolution fusion | flops 10767826944 | bytes 46661632 | tf_op jit(solution)/shard_map/dot_general | solution.py:10
  403.8 21.7 %pad_maximum_fusion.1 = bf16[64,192,1280]{2,1,0:T(8,128)(2,1)} fusion(bf16[64,64,1280]{2,1,0:T(8,128)(2,1)} %bitcast.179, bf16[64,64,1280]{2,1,0:T(8,128)(2,1)} %reshape.280, bf16[64,64,1280]{2,1,0:T(8,128)(2,1)} %reshape.279), kind=kLoop, calls=%fused_computation.1 | loop fusion | flops 94371840 | bytes 62914560 | tf_op jit(solution)/shard_map/concatenate | solution.py:69
  425.6 13.0 fusion.131
  438.5 13.3 %fusion.132 = (bf16[1,1280,4096]{2,1,0:T(8,128)(2,1)S(1)}, bf16[1,1280,4096]{2,1,0:T(8,128)(2,1)}) fusion(bf16[2,1280,4096]{2,1,0:T(8,128)(2,1)} %param.14), kind=kLoop, calls=%fused_computation.186 | loop fusion | bytes 41943040 | tf_op jit(solution)/shard_map/slice | solution.py:51
  453.6 1.5 fusion.136
  455.1 1.5 fusion.137
  456.6 1.6 fusion.134
  458.2 1.6 fusion.135
  459.8 15.8 %fusion.133 = (bf16[1,4096,1280]{2,1,0:T(8,128)(2,1)}, bf16[1,4096,1280]{2,1,0:T(8,128)(2,1)}) fusion(bf16[2,4096,1280]{2,1,0:T(8,128)(2,1)} %param.15), kind=kLoop, calls=%fused_computation.187 | loop fusion | bytes 41943040 | tf_op jit(solution)/shard_map/slice | solution.py:52
  475.5 96.0 %reduce-scatter.3.cloned.1.call-done = bf16[1,192,1280]{2,1,0:T(8,128)(2,1)} async-done(((bf16[64,192,1280]{2,1,0:T(8,128)(2,1)}), bf16[1,192,1280]{2,1,0:T(8,128)(2,1)}) %reduce-scatter.3.cloned.1.call-update) | async-done | bytes 491536 | tf_op jit(solution)/shard_map/reduce_scatter | solution.py:69
  572.7 259.3 %reduce-scatter.5.cloned.1.call-done = bf16[1,192,1280]{2,1,0:T(8,128)(2,1)} async-done(((bf16[64,192,1280]{2,1,0:T(8,128)(2,1)}), bf16[1,192,1280]{2,1,0:T(8,128)(2,1)}) %reduce-scatter.5.cloned.1.call-update) | async-done | bytes 491536 | tf_op jit(solution)/shard_map/reduce_scatter | solution.py:69
  834.8 3.6 fusion.63
  838.4 1.8 mul.485
  840.2 1.8 mul.488
  842.1 3.4 fusion.61
  845.5 1.8 mul.448
  847.3 1.8 mul.478
  849.3 2.7 fusion.111
  852.0 1.7 fusion.78
  854.6 2.0 dynamic-slice_convert_fusion
  856.6 1.8 reshape.289
  858.5 1.8 reshape.290
  860.3 1.8 mul.517
  862.1 1.8 mul.520
  863.9 1.8 mul.506
  865.7 1.8 mul.510
  867.5 1.7 fusion.95
  869.3 1.8 pad_maximum_fusion.12
  871.2 1.3 copy.43
  873.7 1.3 copy.42
  875.1 1.3 copy.41
  879.0 125.7 %all-gather.5.cloned.1.call-done = bf16[12288,1280]{1,0:T(8,128)(2,1)} async-done(((bf16[192,1280]{1,0:T(8,128)(2,1)}), bf16[12288,1280]{1,0:T(8,128)(2,1)}) %all-gather.5.cloned.1.call-update) | async-done | bytes 31457296 | tf_op jit(solution)/shard_map/all_gather | solution.py:81
  1004.8 22.5 %fusion.129 = (bf16[64,64,1280]{2,1,0:T(8,128)(2,1)}, bf16[64,64,1280]{2,1,0:T(8,128)(2,1)}, bf16[64,64,1280]{2,1,0:T(8,128)(2,1)}) fusion(bf16[64,192,1280]{2,1,0:T(8,128)(2,1)} %bitcast.176), kind=kLoop, calls=%fused_computation.183 | loop fusion | bytes 62914560 | tf_op jit(solution)/shard_map/slice | solution.py:82
  1027.3 133.1 %all-gather.7.cloned.1.call-done = bf16[12288,1280]{1,0:T(8,128)(2,1)} async-done(((bf16[192,1280]{1,0:T(8,128)(2,1)}), bf16[12288,1280]{1,0:T(8,128)(2,1)}) %all-gather.7.cloned.1.call-update) | async-done | bytes 31457296 | tf_op jit(solution)/shard_map/all_gather | solution.py:81
  1160.3 22.2 %fusion.130 = (bf16[64,64,1280]{2,1,0:T(8,128)(2,1)}, bf16[64,64,1280]{2,1,0:T(8,128)(2,1)}, bf16[64,64,1280]{2,1,0:T(8,128)(2,1)}) fusion(bf16[64,192,1280]{2,1,0:T(8,128)(2,1)} %bitcast.177), kind=kLoop, calls=%fused_computation.184 | loop fusion | bytes 62914560 | tf_op jit(solution)/shard_map/slice | solution.py:82
  1182.5 18.5 %stack_reshape.20 = bf16[1,1280,4096]{2,1,0:T(8,128)(2,1)} reshape(bf16[64,64,1280]{2,1,0:T(8,128)(2,1)} %get-tuple-element.19) | data formatting | bytes 20971520 | tf_op jit(solution)/shard_map/stack;reshape | solution.py:83
  1201.0 18.5 %stack_reshape.21 = bf16[1,1280,4096]{2,1,0:T(8,128)(2,1)} reshape(bf16[64,64,1280]{2,1,0:T(8,128)(2,1)} %get-tuple-element.22) | data formatting | bytes 20971520 | tf_op jit(solution)/shard_map/stack;reshape | solution.py:83
  1219.5 18.5 %stack_reshape.18 = bf16[1,1280,4096]{2,1,0:T(8,128)(2,1)} reshape(bf16[64,64,1280]{2,1,0:T(8,128)(2,1)} %get-tuple-element.20) | data formatting | bytes 20971520 | tf_op jit(solution)/shard_map/stack;reshape | solution.py:83
  1238.0 18.6 %stack_reshape.19 = bf16[1,1280,4096]{2,1,0:T(8,128)(2,1)} reshape(bf16[64,64,1280]{2,1,0:T(8,128)(2,1)} %get-tuple-element.23) | data formatting | bytes 20971520 | tf_op jit(solution)/shard_map/stack;reshape | solution.py:83
  1256.7 20.9 %pad_maximum_fusion.4 = bf16[2,4096,1280]{2,1,0:T(8,128)(2,1)} fusion(bf16[1,4096,1280]{2,1,0:T(8,128)(2,1)} %bitcast.175, bf16[1,4096,1280]{2,1,0:T(8,128)(2,1)} %bitcast.174), kind=kLoop, calls=%fused_computation.8 | loop fusion | flops 10485760 | bytes 41943040 | tf_op jit(solution)/shard_map/stack | solution.py:83
  1277.6 14.3 %pad_maximum_fusion.3 = bf16[2,1280,4096]{2,1,0:T(8,128)(2,1)} fusion(bf16[1,1280,4096]{2,1,0:T(8,128)(2,1)} %stack_reshape.21, bf16[1,1280,4096]{2,1,0:T(8,128)(2,1)S(1)} %bitcast.169), kind=kLoop, calls=%fused_computation.7 | loop fusion | flops 10485760 | bytes 41943040 | tf_op jit(solution)/shard_map/stack | solution.py:83
  1292.0 8.3 pad_maximum_fusion.2
  (98 shorter events, 11.6 us)
Async XLA Ops:
  7.2 564.3 %reduce-scatter.3.cloned.1.call-start = ((), (), s32[]{:S(2)}) async-start(), calls=%async_computation.2 | async-start | bytes 31948800 | tf_op jit(solution)/shard_map/reduce_scatter | solution.py:69
  9.6 18.1 %copy-start.20 = (f32[1024]{0:T(1024)}, f32[1024]{0:T(1024)S(1)}, u32[]{:S(2)}) copy-start(f32[1024]{0:T(1024)S(1)} %add_rsqrt_fusion.1) | copy-start | bytes 12292
  9.6 18.1 %copy-start.2 = (bf16[1,1024,1280]{2,1,0:T(8,128)(2,1)S(1)}, bf16[1,1024,1280]{2,1,0:T(8,128)(2,1)}, u32[]{:S(2)}) copy-start(bf16[1,1024,1280]{2,1,0:T(8,128)(2,1)} %param.11) | copy-start | bytes 7864324
  51.5 17.5 %copy-start.4 = (bf16[1,1024,1280]{2,1,0:T(8,128)(2,1)S(1)}, bf16[1,1024,1280]{2,1,0:T(8,128)(2,1)}, u32[]{:S(2)}) copy-start(bf16[1,1024,1280]{2,1,0:T(8,128)(2,1)} %param.12) | copy-start | bytes 7864324
  68.3 17.9 %copy-start.6 = (bf16[1024,1280]{1,0:T(8,128)(2,1)}, bf16[1024,1280]{1,0:T(8,128)(2,1)S(1)}, u32[]{:S(2)}) copy-start(bf16[1024,1280]{1,0:T(8,128)(2,1)S(1)} %get-tuple-element.78) | copy-start | bytes 7864324
  69.0 105.2 %copy-start.17 = (f32[1024]{0:T(1024)}, f32[1024]{0:T(1024)S(1)}, u32[]{:S(2)}) copy-start(f32[1024]{0:T(1024)S(1)} %get-tuple-element.74) | copy-start | bytes 12292
  154.4 19.8 %copy-start.19 = (f32[1024]{0:T(1024)S(1)}, f32[1024]{0:T(1024)}, u32[]{:S(2)}) copy-start(f32[1024]{0:T(1024)} %get-tuple-element.73) | copy-start | bytes 12292
  174.2 21.7 %slice-start.9 = ((s8[8388608]{0:T(1024)(128)(4,1)}), s8[4194304]{0:T(1024)(128)(4,1)S(1)}, s32[]{:S(2)}) async-start(s8[8388608]{0:T(1024)(128)(4,1)} %bitcast.180), calls=%async_computation.15 | async-start | bytes 8388608
  178.5 17.4 %slice-start.10 = ((s8[8388608]{0:T(1024)(128)(4,1)}), s8[4194304]{0:T(1024)(128)(4,1)S(1)}, s32[]{:S(2)}) async-start(s8[8388608]{0:T(1024)(128)(4,1)} %bitcast.180), calls=%async_computation.16 | async-start | bytes 8388608
  195.9 13.6 %copy-start.3 = (bf16[1,1024,1280]{2,1,0:T(8,128)(2,1)S(1)}, bf16[1,1024,1280]{2,1,0:T(8,128)(2,1)}, u32[]{:S(2)}) copy-start(bf16[1,1024,1280]{2,1,0:T(8,128)(2,1)} %param.11) | copy-start | bytes 7864324
  195.9 13.6 %copy-start.21 = (f32[1024]{0:T(1024)S(1)}, f32[1024]{0:T(1024)}, u32[]{:S(2)}) copy-start(f32[1024]{0:T(1024)} %copy-done.20) | copy-start | bytes 12292
  310.1 1.7 copy-start.7
  310.2 1.7 copy-start.18
  310.2 521.8 %reduce-scatter.5.cloned.1.call-start = ((), (), s32[]{:S(2)}) async-start(), calls=%async_computation.3 | async-start | bytes 31948800 | tf_op jit(solution)/shard_map/reduce_scatter | solution.py:69
  364.7 18.6 %copy-start.5 = (bf16[1,1024,1280]{2,1,0:T(8,128)(2,1)S(1)}, bf16[1,1024,1280]{2,1,0:T(8,128)(2,1)}, u32[]{:S(2)}) copy-start(bf16[1,1024,1280]{2,1,0:T(8,128)(2,1)} %param.12) | copy-start | bytes 7864324
  425.5 579.3 %all-gather.5.cloned.1.call-start = ((), (), s32[]{:S(2)}) async-start(), calls=%async_computation.4 | async-start | bytes 31948800 | tf_op jit(solution)/shard_map/all_gather | solution.py:81
  438.5 15.0 %copy-start.13 = (f32[2,20,4096]{2,0,1:T(2,128)S(1)}, f32[2,20,4096]{2,0,1:T(2,128)}, u32[]{:S(2)}) copy-start(f32[2,20,4096]{2,0,1:T(2,128)} %param.17) | copy-start | bytes 1966084
  438.5 16.6 %copy-start.14 = (f32[2,20,4096]{2,0,1:T(2,128)S(1)}, f32[2,20,4096]{2,0,1:T(2,128)}, u32[]{:S(2)}) copy-start(f32[2,20,4096]{2,0,1:T(2,128)} %param.20) | copy-start | bytes 1966084
  438.5 18.1 %copy-start.15 = (f32[2,20,4096]{2,0,1:T(2,128)S(1)}, f32[2,20,4096]{2,0,1:T(2,128)}, u32[]{:S(2)}) copy-start(f32[2,20,4096]{2,0,1:T(2,128)} %param.16) | copy-start | bytes 1966084
  438.5 19.7 %copy-start.16 = (f32[2,20,4096]{2,0,1:T(2,128)S(1)}, f32[2,20,4096]{2,0,1:T(2,128)}, u32[]{:S(2)}) copy-start(f32[2,20,4096]{2,0,1:T(2,128)} %param.19) | copy-start | bytes 1966084
  571.5 277.6 %copy-start = (bf16[1,192,1280]{2,1,0:T(8,128)(2,1)S(1)}, bf16[1,192,1280]{2,1,0:T(8,128)(2,1)}, u32[]{:S(2)}) copy-start(bf16[1,192,1280]{2,1,0:T(8,128)(2,1)} %reduce-scatter.3.cloned.1.call-done) | copy-start | bytes 1474564
  832.0 17.2 %copy-start.1 = (bf16[1,192,1280]{2,1,0:T(8,128)(2,1)S(1)}, bf16[1,192,1280]{2,1,0:T(8,128)(2,1)}, u32[]{:S(2)}) copy-start(bf16[1,192,1280]{2,1,0:T(8,128)(2,1)} %reduce-scatter.5.cloned.1.call-done) | copy-start | bytes 1474564
  853.7 22.7 %copy-start.8 = (f32[1,20,4096]{2,1,0:T(8,128)S(1)}, f32[1,20,4096]{2,1,0:T(8,128)}, u32[]{:S(2)}) copy-start(f32[1,20,4096]{2,1,0:T(8,128)} %get-tuple-element.90) | copy-start | bytes 983044
  854.6 305.7 %all-gather.7.cloned.1.call-start = ((), (), s32[]{:S(2)}) async-start(), calls=%async_computation.5 | async-start | bytes 31948800 | tf_op jit(solution)/shard_map/all_gather | solution.py:81
  869.3 8.6 copy-start.9
  869.3 8.6 copy-start.10
  869.3 8.6 copy-start.11
  871.1 6.7 copy-start.12
  1238.0 39.6 %slice-start = ((s8[10485760]{0:T(1024)(128)(4,1)}), s8[2097152]{0:T(1024)(128)(4,1)S(1)}, s32[]{:S(2)}) async-start(s8[10485760]{0:T(1024)(128)(4,1)} %bitcast.168), calls=%async_computation.6 | async-start | bytes 4194304
  1256.7 20.9 %slice-start.1 = ((s8[10485760]{0:T(1024)(128)(4,1)}), s8[4194304]{0:T(1024)(128)(4,1)S(1)}, s32[]{:S(2)}) async-start(s8[10485760]{0:T(1024)(128)(4,1)} %bitcast.168), calls=%async_computation.7 | async-start | bytes 8388608
  1256.7 20.9 %slice-start.2 = ((s8[10485760]{0:T(1024)(128)(4,1)}), s8[4194304]{0:T(1024)(128)(4,1)S(1)}, s32[]{:S(2)}) async-start(s8[10485760]{0:T(1024)(128)(4,1)} %bitcast.168), calls=%async_computation.8 | async-start | bytes 8388608
  1256.7 35.3 %slice-start.3 = ((s8[10485760]{0:T(1024)(128)(4,1)}), s8[4194304]{0:T(1024)(128)(4,1)S(1)}, s32[]{:S(2)}) async-start(s8[10485760]{0:T(1024)(128)(4,1)} %bitcast.170), calls=%async_computation.9 | async-start | bytes 8388608
  1256.7 35.3 %slice-start.4 = ((s8[10485760]{0:T(1024)(128)(4,1)}), s8[4194304]{0:T(1024)(128)(4,1)S(1)}, s32[]{:S(2)}) async-start(s8[10485760]{0:T(1024)(128)(4,1)} %bitcast.170), calls=%async_computation.10 | async-start | bytes 8388608
  1256.7 35.3 %slice-start.6 = ((s8[10485760]{0:T(1024)(128)(4,1)}), s8[4194304]{0:T(1024)(128)(4,1)S(1)}, s32[]{:S(2)}) async-start(s8[10485760]{0:T(1024)(128)(4,1)} %bitcast.172), calls=%async_computation.12 | async-start | bytes 8388608
  1256.7 35.3 %slice-start.7 = ((s8[10485760]{0:T(1024)(128)(4,1)}), s8[4194304]{0:T(1024)(128)(4,1)S(1)}, s32[]{:S(2)}) async-start(s8[10485760]{0:T(1024)(128)(4,1)} %bitcast.172), calls=%async_computation.13 | async-start | bytes 8388608
  1277.6 14.4 %slice-start.5 = ((s8[10485760]{0:T(1024)(128)(4,1)}), s8[2097152]{0:T(1024)(128)(4,1)S(1)}, s32[]{:S(2)}) async-start(s8[10485760]{0:T(1024)(128)(4,1)} %bitcast.170), calls=%async_computation.11 | async-start | bytes 4194304
  1277.6 14.4 %slice-start.8 = ((s8[10485760]{0:T(1024)(128)(4,1)}), s8[2097152]{0:T(1024)(128)(4,1)S(1)}, s32[]{:S(2)}) async-start(s8[10485760]{0:T(1024)(128)(4,1)} %bitcast.172), calls=%async_computation.14 | async-start | bytes 4194304
Sparse Core Ops, SparseCore 0:
  310.3 261.1 reduce-scatter.2
  576.3 255.6 reduce-scatter.4
  854.7 150.0 all-gather.4
  1008.1 152.2 all-gather.6

commit v2 on v1

v2 whole, which is shorter than its diff:
```python
import functools
import jax, jax.numpy as jnp
from jax import lax
from jax.experimental import pallas as pl
from jax.experimental.pallas import tpu as pltpu
from jax.sharding import PartitionSpec as P

AXES = ("x", "y", "z")
STRIDE = {"x": 16, "y": 4, "z": 1}
ORDERS = (("x", "y", "z"), ("y", "z", "x"), ("z", "x", "y"))
BF, F32 = jnp.bfloat16, jnp.float32
ROWS = 3840


def comm_kernel(n_super, U, g, m, v, w, wall, m_out, v_out,
                recv1, send2, recv2, own, sa, b1s, b1r, b2s, b2r, sb, c1s, c1r, c2s, c2r,
                mb, vb, wb, mo, vo, wn, ssem, rsem, lsem):
    me = lax.axis_index("dp")
    pos = {"x": me // 16, "y": (me // 4) % 4, "z": me % 4}
    low = (U // 2 + 15) // 16 * 16
    halves = (pl.ds(0, 2), pl.ds(2, 2))
    row_halves = (pl.ds(0, low), pl.ds(low, U - low))

    def peer(axis, by):
        return {"dp": me + ((pos[axis] + by) % 4 - pos[axis]) * STRIDE[axis]}

    barrier = pltpu.get_barrier_semaphore()
    for axis in AXES:
        for by in (1, 3):
            pl.semaphore_signal(barrier, inc=1, device_id=peer(axis, by), device_id_type=pl.DeviceIdType.MESH)
    pl.semaphore_wait(barrier, 6)

    def part(ref, fixed, rows):
        return ref.at[tuple(fixed.get(axis, slice(None)) for axis in AXES) + (rows, slice(None))]

    def remote(kind, slot, c, way, src, dst, axis):
        return pltpu.make_async_remote_copy(
            src_ref=src, dst_ref=dst, send_sem=ssem.at[kind, slot, c, way], recv_sem=rsem.at[kind, slot, c, way],
            device_id=peer(axis, (1, 3)[way]), device_id_type=pl.DeviceIdType.MESH)

    def local(kind, slot, c, src, dst):
        return pltpu.make_async_copy(src, dst, lsem.at[kind, slot, c])

    class Chunk:
        def __init__(self, c, j):
            self.c, self.slot = c, j % 2
            self.A, self.B, self.C = ORDERS[c]
            self.rest = tuple(axis for axis in AXES if axis != self.A)
            self.ib = self.rest.index(self.B)
            self.rows = pl.ds(pl.multiple_of((3 * j + c) * U, 16), U)
            self.a, self.b, self.c3 = (pos[axis] for axis in ORDERS[c])

        def unit(self, b, i):
            return (b, i) if self.ib == 0 else (i, b)

        def row_part(self, rows):
            return pl.ds(self.rows.start + rows.start, rows.size)

        def a1(self):
            s, c = self.slot, self.c
            return [remote(0, s, c, way, part(g, {self.A: (self.a + 2) % 4, self.rest[0]: halves[way]}, self.rows),
                           recv1.at[s, c, halves[way]], self.A) for way in (0, 1)]

        def load2(self):
            s, c = self.slot, self.c
            return [local(way, s, c, part(g, {self.A: (self.a + (1, 3)[way]) % 4}, self.rows), send2.at[s, c, way]) for way in (0, 1)]

        def load_own(self):
            return [local(2, self.slot, self.c, part(g, {self.A: self.a}, self.rows), own.at[self.slot, self.c])]

        def a2(self):
            s, c = self.slot, self.c
            return [remote(1, s, c, way, send2.at[s, c, way], recv2.at[s, c, way], self.A) for way in (0, 1)]

        def b1(self):
            s, c = self.slot, self.c
            return [remote(2, s, c, way, b1s.at[s, c, halves[way]], b1r.at[s, c, halves[way]], self.B) for way in (0, 1)]

        def b2(self):
            s, c = self.slot, self.c
            return [remote(3, s, c, way, b2s.at[s, c, way], b2r.at[s, c, way], self.B) for way in (0, 1)]

        def c1(self):
            s, c = self.slot, self.c
            return [remote(4, s, c, way, c1s.at[s, c, row_halves[way]], c1r.at[s, c, row_halves[way]], self.C) for way in (0, 1)]

        def c2(self):
            s, c = self.slot, self.c
            return [remote(5, s, c, way, c2s.at[s, c, way], c2r.at[s, c, way], self.C) for way in (0, 1)]

        def load_step(self):
            s, c = self.slot, self.c
            return [local(3 + i, s, c, ref.at[self.rows], buf.at[s, c]) for i, (ref, buf) in enumerate(((m, mb), (v, vb), (w, wb)))]

        def store_step(self):
            s, c = self.slot, self.c
            mine = part(wall, {self.A: self.a, self.B: self.b, self.C: self.c3}, self.rows)
            pairs = ((mo.at[s, c], m_out.at[self.rows]), (vo.at[s, c], v_out.at[self.rows]), (wn.at[s, c], mine))
            return [local(6 + i, s, c, src, dst) for i, (src, dst) in enumerate(pairs)]

        def gather(self, which):
            s, c = self.slot, self.c
            if which < 2:
                axis, here, fixed, kind = self.C, self.c3, {self.A: self.a, self.B: self.b}, 6
            elif which < 4:
                axis, here, fixed, kind = self.B, self.b, {self.A: self.a}, 8
            else:
                axis, here, fixed, kind = self.A, self.a, {}, 10
            if which % 2 == 0:
                block = part(wall, fixed | {axis: here}, self.rows)
                src = wn.at[s, c] if which == 0 else block
                return [remote(kind, s, c, way, src, block, axis) for way in (0, 1)]
            out = []
            for way in (0, 1):
                block = fixed | {axis: (here + (3, 1)[way]) % 4}
                rows = self.rows
                if which == 1:
                    rows = self.row_part(row_halves[way])
                elif which == 3:
                    block[self.C] = halves[way]
                else:
                    block[self.rest[0]] = halves[way]
                half = part(wall, block, rows)
                out.append(remote(kind + 1, s, c, way, half, half, axis))
            return out

    def start(copies):
        for copy in copies:
            copy.start()

    def wait(copies):
        for copy in copies:
            copy.wait()

    def loop(n, body, unroll=1):
        lax.fori_loop(0, n, lambda i, _: (body(i), None)[1], None, unroll=unroll)

    def stage0(k):
        start(k.a1())
        start(k.load2())

    def stage1(k):
        wait(k.load2())
        wait(k.a1())
        s, c = k.slot, k.c

        def body(i):
            for way in (0, 1):
                at = (s, c, 2 * way + i // 4, i % 4)
                to = (s, c, way, 2 * way + i // 4, i % 4)
                send2[to] = (send2[to].astype(F32) + recv1[at].astype(F32)).astype(BF)

        loop(8, body)
        start(k.a2())
        start(k.load_own())

    def stage2(k):
        wait(k.load_own())
        wait(k.a2())
        s, c = k.slot, k.c

        def body(i):
            at = (i // 4, i % 4)
            total = own[(s, c) + at].astype(F32) + recv2[(s, c, 0) + at].astype(F32) + recv2[(s, c, 1) + at].astype(F32)
            sa[(s, c) + at] = total

        loop(16, body)
        far = (k.b + 2) % 4

        def pack(i):
            b1s[s, c, i] = sa[(s, c) + k.unit(far, i)].astype(BF)

        loop(4, pack)
        start(k.b1())

    def stage3(k):
        wait(k.b1())
        s, c = k.slot, k.c
        near = ((k.b + 1) % 4, (k.b + 3) % 4)

        def body(i):
            for way in (0, 1):
                b2s[s, c, way, 2 * way + i] = (sa[(s, c) + k.unit(near[way], 2 * way + i)] + b1r[s, c, 2 * way + i].astype(F32)).astype(BF)
                b2s[s, c, way, 2 - 2 * way + i] = sa[(s, c) + k.unit(near[way], 2 - 2 * way + i)].astype(BF)

        loop(2, body)
        start(k.b2())

    def stage4(k):
        wait(k.b2())
        s, c = k.slot, k.c

        def body(i):
            sb[s, c, i] = sa[(s, c) + k.unit(k.b, i)] + b2r[s, c, 0, i].astype(F32) + b2r[s, c, 1, i].astype(F32)

        loop(4, body)
        c1s[s, c] = sb[s, c, (k.c3 + 2) % 4].astype(BF)
        start(k.c1())

    def stage5(k):
        wait(k.c1())
        s, c = k.slot, k.c
        near = ((k.c3 + 1) % 4, (k.c3 + 3) % 4)
        for way in (0, 1):
            add, keep = row_halves[way], row_halves[1 - way]
            c2s[s, c, way, add] = (sb[s, c, near[way], add] + c1r[s, c, add].astype(F32)).astype(BF)
            c2s[s, c, way, keep] = sb[s, c, near[way], keep].astype(BF)
        start(k.c2())
        start(k.load_step())

    def stage6(k):
        wait(k.load_step())
        wait(k.c2())
        s, c = k.slot, k.c
        total = sb[s, c, k.c3] + c2r[s, c, 0].astype(F32) + c2r[s, c, 1].astype(F32)
        grad = total.astype(BF).astype(F32)
        first = 0.9 * mb[s, c] + 0.1 * grad
        second = 0.95 * vb[s, c] + 0.05 * grad * grad
        old = wb[s, c].astype(F32)
        mo[s, c] = first
        vo[s, c] = second
        wn[s, c] = (old - 0.02 * (first * lax.rsqrt(second + 1e-8) + 0.1 * old)).astype(BF)
        start(k.gather(0))
        start(k.store_step())

    def stage7(k):
        wait(k.gather(0))
        start(k.gather(1))

    def stage8(k):
        wait(k.store_step())
        wait(k.gather(1))
        start(k.gather(2))

    def later(n):
        def stage(k):
            wait(k.gather(n - 1))
            start(k.gather(n))
        return stage

    def stage12(k):
        wait(k.gather(5))

    stages = (stage0, stage1, stage2, stage3, stage4, stage5, stage6, stage7, stage8, later(3), later(4), later(5), stage12)

    def iteration(s):
        for number in reversed(range(len(stages))):
            j = s - number

            @pl.when((j >= 0) & (j < n_super))
            def _():
                for c in range(3):
                    stages[number](Chunk(c, j))

    loop(n_super + len(stages) - 1, iteration)


def comm(g, m, v, w, U, n_super, collective_id=0):
    rows = g.shape[3]
    hbm = pl.BlockSpec(memory_space=pl.ANY)
    V, two = pltpu.VMEM, (2, 3)
    scratch = [
        V(two + (4, 4, U, 128), BF), V(two + (2, 4, 4, U, 128), BF), V(two + (2, 4, 4, U, 128), BF), V(two + (4, 4, U, 128), BF),
        V(two + (4, 4, U, 128), F32),
        V(two + (4, U, 128), BF), V(two + (4, U, 128), BF), V(two + (2, 4, U, 128), BF), V(two + (2, 4, U, 128), BF), V(two + (4, U, 128), F32),
        V(two + (U, 128), BF), V(two + (U, 128), BF), V(two + (2, U, 128), BF), V(two + (2, U, 128), BF),
        V(two + (U, 128), F32), V(two + (U, 128), F32), V(two + (U, 128), BF), V(two + (U, 128), F32), V(two + (U, 128), F32), V(two + (U, 128), BF),
        pltpu.SemaphoreType.DMA((12, 2, 3, 2)), pltpu.SemaphoreType.DMA((12, 2, 3, 2)), pltpu.SemaphoreType.DMA((9, 2, 3)),
    ]
    return pl.pallas_call(
        functools.partial(comm_kernel, n_super, U),
        out_shape=(jax.ShapeDtypeStruct(g.shape, BF), jax.ShapeDtypeStruct(m.shape, F32), jax.ShapeDtypeStruct(v.shape, F32)),
        in_specs=[hbm] * 4, out_specs=(hbm,) * 3, scratch_shapes=scratch,
        compiler_params=pltpu.CompilerParams(collective_id=collective_id, has_side_effects=True, vmem_limit_bytes=48 * 2**20),
        name="sum_step_gather",
    )(g, m, v, w)


def dot(a, b, dims):
    return lax.dot_general(a, b, (dims, ((), ())), preferred_element_type=F32)


def scale_of(h):
    wide = h.astype(F32)
    return lax.rsqrt(jnp.mean(wide**2, -1, keepdims=True) + 1e-6)


def hidden(a, w_gate, w_up):
    gate, up = dot(a, w_gate, ((1,), (0,))), dot(a, w_up, ((1,), (0,)))
    return gate, up, (jax.nn.silu(gate) * up).astype(BF)


def of_hidden(d, gate, up):
    d = d.astype(F32)
    s = jax.nn.sigmoid(gate)
    d_gate = d * up * (s * (1 + gate * (1 - s)))
    return d_gate.astype(BF), (d * (gate * s)).astype(BF)


def of_norm(h, scale, d):
    wide, d = h.astype(F32), d.astype(F32)
    along = jnp.mean(wide * d, -1, keepdims=True)
    return (scale * d - wide * (scale * scale * scale) * along).astype(BF)


def down_kernel(p_ref, d_ref, *refs):
    out = refs[-1]
    for ct in range(2):
        @pl.loop(0, 8)
        def _(i):
            rows = pl.ds(pl.multiple_of(i * 512, 512), 512)
            r = jnp.dot(p_ref[rows, :], d_ref[:, ct * 128 : ct * 128 + 128], preferred_element_type=F32)
            out[pl.ds(i * 8, 8), ct * 64 : ct * 64 + 64, :] = r.reshape(8, 64, 128).astype(BF)


def down_gradient(p_t, d, at, g=None):
    tokens = d.shape[0]
    whole = pl.BlockSpec((4096, tokens), lambda i: (0, 0))
    return pl.pallas_call(
        down_kernel,
        grid=(5,),
        out_shape=jax.ShapeDtypeStruct((64, ROWS, 128), BF),
        in_specs=[whole, pl.BlockSpec((tokens, 256), lambda i: (0, i))] + [pl.BlockSpec(memory_space=pl.ANY)] * (g is not None),
        out_specs=pl.BlockSpec((64, 128, 128), lambda i: (0, at // 128 + i, 0)),
        input_output_aliases={} if g is None else {2: 0},
        cost_estimate=pl.CostEstimate(flops=2 * 4096 * 1280 * 1024, bytes_accessed=22 * 10**6, transcendentals=0),
        name="down_gradient",
    )(p_t, d, *([] if g is None else [g]))


def mixed(even, odd):
    row = lax.broadcasted_iota(jnp.int32, even.shape, 1)
    return (jnp.where(row < 4, even, pltpu.roll(odd, 4, 1)), jnp.where(row < 4, pltpu.roll(even, 4, 1), odd))


def gate_up_kernel(a_ref, dg_ref, du_ref, _, out):
    @pl.loop(0, 4)
    def _(i):
        rows = pl.ds(pl.multiple_of(i * 256, 256), 256)
        for at, d in ((0, dg_ref), (32, du_ref)):
            r = jnp.dot(a_ref[rows, :], d[...], preferred_element_type=F32)
            for ct in range(2):
                out[pl.ds(i * 16, 16), at + 16 * ct : at + 16 * ct + 16, :] = r[:, ct * 128 : ct * 128 + 128].reshape(16, 16, 128).astype(BF)
    last = [jnp.dot(a_ref[1024:, :], d[...], preferred_element_type=F32) for d in (dg_ref, du_ref)]
    tiles = [mixed(*(r[:, ct * 128 : ct * 128 + 128].reshape(32, 8, 128) for r in last)) for ct in range(2)]
    for odd in range(2):
        both = jnp.concatenate([tiles[0][odd], tiles[1][odd]], 1).astype(BF)
        for pair in range(32):
            out[2 * pair + odd, 64:80, :] = both[pair]


def gate_up_gradients(a_t, dg, du, at, g):
    tokens = dg.shape[0]
    slab = pl.BlockSpec((tokens, 256), lambda i: (0, i))
    return pl.pallas_call(
        gate_up_kernel,
        grid=(16,),
        out_shape=jax.ShapeDtypeStruct((64, ROWS, 128), BF),
        in_specs=[pl.BlockSpec((1280, tokens), lambda i: (0, 0)), slab, slab, pl.BlockSpec(memory_space=pl.ANY)],
        out_specs=pl.BlockSpec((64, 80, 128), lambda i: (0, at // 80 + i, 0)),
        input_output_aliases={3: 0},
        cost_estimate=pl.CostEstimate(flops=4 * 4096 * 1280 * 1024, bytes_accessed=40 * 10**6, transcendentals=0),
        name="gate_up_gradients",
    )(a_t, dg, du, g)


def unpack_kernel(w_ref, gate, up, down):
    for d in range(4):
        for ct in range(10):
            down[0, 64 * d : 64 * d + 64, ct * 128 : ct * 128 + 128] = w_ref[d, 64 * ct : 64 * ct + 64, :]

    @pl.loop(0, 16)
    def _(slab):
        base = pl.multiple_of(640 + 80 * slab, 16)
        mix = [w_ref[d, pl.ds(base + 64, 16), :].astype(F32) for d in range(4)]
        for ct in range(2):
            tiles = [mixed(*(mix[2 * pair + odd][8 * ct : 8 * ct + 8][None] for odd in range(2))) for pair in range(2)]
            for which, out in enumerate((gate, up)):
                own = [w_ref[d, pl.ds(base + 32 * which + 16 * ct, 16), :].astype(F32) for d in range(4)]
                rows = jnp.concatenate([own[0], tiles[0][which][0], own[1], own[2], tiles[1][which][0], own[3]], 0)
                out[0, :, pl.ds(pl.multiple_of(slab * 256 + ct * 128, 128), 128)] = rows.astype(BF)


def unpack(wall):
    shapes = ((2, 1280, 4096), (2, 1280, 4096), (2, 4096, 1280))
    return pl.pallas_call(
        unpack_kernel,
        grid=(2, 16),
        out_shape=tuple(jax.ShapeDtypeStruct(s, BF) for s in shapes),
        in_specs=[pl.BlockSpec((4, ROWS // 2, 128), lambda l, i: (i, l, 0))],
        out_specs=tuple(pl.BlockSpec((1, s[1] // 16, s[2]), lambda l, i: (1 - l, i, 0)) for s in shapes),
        cost_estimate=pl.CostEstimate(flops=10**6, bytes_accessed=126 * 10**6, transcendentals=0),
        name="unpack",
    )(wall)


def row_order(w_t):
    pairs = w_t.reshape(32, 40, -1)
    own = jnp.concatenate([pairs[:, :16], pairs[:, 24:]], 1)
    return jnp.concatenate([own.reshape(1024, -1), pairs[:, 16:24].reshape(256, -1)], 0)


def to_units(odd, gate, up, down):
    whole, left = [], []
    for t in (gate, up):
        t = jnp.where(odd, jnp.roll(t, -4, 0), t)
        whole.append(t[:16].reshape(16, 16, 2, 128).transpose(1, 2, 0, 3).reshape(16, 32, 128))
        left.append(t[16:].reshape(4, 16, 2, 128).transpose(1, 2, 0, 3))
    slabs = jnp.concatenate(whole + [jnp.concatenate(left, 2).reshape(16, 16, 128)], 1)
    return jnp.concatenate([down.reshape(64, 10, 128).transpose(1, 0, 2).reshape(640, 128), slabs.reshape(1280, 128)], 0)


def from_units(odd, units):
    slabs = units[640:].reshape(16, 80, 128)
    left = slabs[:, 64:].reshape(16, 2, 2, 4, 128)
    out = []
    for i in range(2):
        whole = slabs[:, 32 * i : 32 * i + 32].reshape(16, 2, 16, 128).transpose(2, 0, 1, 3).reshape(16, 4096)
        t = jnp.concatenate([whole, left[:, :, i].transpose(2, 0, 1, 3).reshape(4, 4096)], 0)
        out.append(jnp.where(odd, jnp.roll(t, 4, 0), t))
    return out + [units[:640].reshape(10, 64, 128).transpose(1, 0, 2).reshape(64, 1280)]


def solution(mesh):
    def step(x, dy, *arrays):
        weights, ms, vs = arrays[:3], arrays[3:6], arrays[6:]
        wg, wu, wd = weights
        h0, dy = x[0], dy[0]
        s0 = scale_of(h0)
        a0 = (h0.astype(F32) * s0).astype(BF)
        g0, u0, p0 = hidden(a0, wg[0], wu[0])
        h1 = h0 + dot(p0, wd[0], ((1,), (0,))).astype(BF)
        s1 = scale_of(h1)
        a1 = (h1.astype(F32) * s1).astype(BF)
        g1, u1, p1 = hidden(a1, wg[1], wu[1])
        grads = down_gradient(p1.T, dy, 0)
        dg1, du1 = of_hidden(dot(dy, wd[1], ((1,), (1,))).astype(BF), g1, u1)
        grads = gate_up_gradients(row_order(a1.T), dg1, du1, 640, grads)
        da1 = dot(dg1, wg[1], ((1,), (1,))) + dot(du1, wu[1], ((1,), (1,)))
        dh1 = dy + of_norm(h1, s1, da1)
        grads = down_gradient(p0.T, dh1, 1920, grads)
        dg0, du0 = of_hidden(dot(dh1, wd[0], ((1,), (1,))).astype(BF), g0, u0)
        grads = gate_up_gradients(row_order(a0.T), dg0, du0, 2560, grads)

        me = lax.axis_index("dp")
        odd = me % 2 == 1
        own = [lax.dynamic_slice_in_dim(w, me * (w.shape[1] // 64), w.shape[1] // 64, 1) for w in weights]
        mine = [jnp.concatenate([to_units(odd, *(t[layer] for t in three)) for layer in (1, 0)], 0) for three in (ms, vs, own)]
        wall, *moments = comm(grads.reshape(4, 4, 4, ROWS, 128), *mine, 80, 16)
        new = list(unpack(wall.reshape(64, ROWS, 128)))
        for t in moments:
            layers = [from_units(odd, t[1920 * (1 - layer) :][:1920]) for layer in (0, 1)]
            new += [jnp.stack(pair) for pair in zip(*layers, strict=True)]
        return tuple(new)

    seq, whole, rows = P(("rep", "dp")), P(), P(None, "dp", None)
    return jax.shard_map(
        step,
        mesh=mesh,
        in_specs=(seq, seq) + (whole,) * 3 + (rows,) * 6,
        out_specs=(P("rep"),) * 3 + (P("rep", "dp", None),) * 6,
        check_vma=False,
    )
```

time: 1320 us -> 1040 us (0.79)
  Pallas kernels: 0 us -> 675 us
  waiting for transfers between devices: 614 us -> 0 us
  local copies, waits for them, and re-layouts: 272 us -> 105 us
  matrix products: 292 us -> 181 us
  other arithmetic: 114 us -> 66 us
    pallas_call x0 -> x6, Pallas kernels: none -> 675 us  [the longest x1 461 us: comm(): pl.pallas_call(functools.partial(comm_kernel, n_super, U), out_shape=(jax...]
    reduce_scatter x2 -> x0, waiting for transfers between devices: 355 us -> none  [summed(): lax.psum_scatter(jnp.concatenate(parts, 1), 'dp', scatter_dimension=0, ti...]
    all_gather x2 -> x0, waiting for transfers between devices: 259 us -> none  [step(): lax.all_gather(jnp.concatenate([o[0].reshape(64, 1280) for o in out]), 'dp')]
    dot_general x15 -> x9, matrix products: 292 us -> 181 us  [dot(): return lax.dot_general(a, b, (dims, ((), ())), preferred_element_type=F32)]
    slice x11 -> x63, local copies, waits for them, and re-layouts: 95.1 us -> 17 us  [the longest x14 6.9 us: to_units(): t = jnp.where(odd, jnp.roll(t, -4, 0), t)]
    another operation x4 -> x10, local copies, waits for them, and re-layouts: 74.1 us -> 0.68 us  [the longest x6 0.44 us: to_units(): down.reshape(64, 10, 128).transpose(1, 0, 2).reshape(640, 128)]
    reshape x8 -> x38, local copies, waits for them, and re-layouts: 75.6 us -> 4.91 us  [the longest x12 2.18 us: to_units(): t[:16].reshape(16, 16, 2, 128).transpose(1, 2, 0, 3).reshape(16, 32, 128)]
    dot_general x0 -> x4, local copies, waits for them, and re-layouts: none -> 69.8 us  [dot(): return lax.dot_general(a, b, (dims, ((), ())), preferred_element_type=F32)]
  transfers between devices with their start and end apart: 4 -> 0, of which waited for: 4 -> 0; matrix products, arithmetic and copies ran while one was open for 16% -> 0% of each run, Pallas kernels for 0% -> 0%
where the time goes in v2:
time: 1040 us; the launch traced here: 1030 us
  Pallas kernels  675 us (65%)
  matrix products  181 us (17%)
  local copies, waits for them, and re-layouts  105 us (10%)
  other arithmetic  66 us (6%)
    pallas_call x1, Pallas kernels, comm(): pl.pallas_call(functools.partial(comm_kernel, n_super, U), out_shape=(jax...  461 us
    dot_general x9, matrix products, dot(): return lax.dot_general(a, b, (dims, ((), ())), preferred_element_type=F32)  181 us
    pallas_call x2, Pallas kernels, down_gradient(): pl.pallas_call(down_kernel, grid=(5,), out_shape=jax.ShapeDtypeStruct((64...  80.3 us
    pallas_call x2, Pallas kernels, gate_up_gradients(): pl.pallas_call(gate_up_kernel, grid=(16,), out_shape=jax.ShapeDtypeStruct...  77.3 us
    dot_general x4, local copies, waits for them, and re-layouts, dot(): return lax.dot_general(a, b, (dims, ((), ())), preferred_element_type=F32)  69.8 us
    pallas_call x1, Pallas kernels, unpack(): pl.pallas_call(unpack_kernel, grid=(2, 16), out_shape=tuple((jax.ShapeDty...  56.5 us
    convert_element_type x2, other arithmetic, hidden(): return (gate, up, (jax.nn.silu(gate) * up).astype(BF))  30 us

profile of v2, /device:TPU:0, one launch (start us, length us, event | category | flops | bytes accessed | tf_op | source)
XLA Modules:
  0.0 1029.6 jit_solution(11876095106006500182)
XLA Ops:
  0.6 2.3 fusion.48
  3.0 3.7 fusion.68
  6.7 3.0 copy.99
  10.2 1.8 pad_maximum_fusion.a_ref
  11.9 17.1 %fusion.31 = f32[1024,4096]{1,0:T(8,128)} fusion(bf16[2,1280,4096]{2,1,0:T(8,128)(2,1)} %param.13, bf16[1,1024,1280]{2,1,0:T(8,128)(2,1)S(1)} %copy-done.2, f32[1024]{0:T(1024)S(1)} %add_rsqrt_fusion.1), kind=kOutput, calls=%fused_computation.44 | convolution fusion | flops 10741350400 | bytes 29888512 | tf_op jit(solution)/shard_map/dot_general | solution.py:280
  29.1 17.1 %fusion.29 = f32[1024,4096]{1,0:T(8,128)} fusion(bf16[2,1280,4096]{2,1,0:T(8,128)(2,1)} %param.14, bf16[1,1024,1280]{2,1,0:T(8,128)(2,1)S(1)} %copy-done.2, f32[1024]{0:T(1024)S(1)} %add_rsqrt_fusion.1), kind=kOutput, calls=%fused_computation.42 | convolution fusion | flops 10741350400 | bytes 29888512 | tf_op jit(solution)/shard_map/dot_general | solution.py:280
  46.2 23.3 %fusion.50 = (f32[1024]{0:T(1024)S(1)}, bf16[1024,1280]{1,0:T(8,128)(2,1)S(1)}) fusion(bf16[2,4096,1280]{2,1,0:T(8,128)(2,1)} %param.15, f32[1024,4096]{1,0:T(8,128)} %fusion.29, f32[1024,4096]{1,0:T(8,128)} %fusion.31, bf16[1,1024,1280]{2,1,0:T(8,128)(2,1)S(1)} %copy-done.2), kind=kOutput, calls=%fused_computation.65 | convolution fusion | flops 10769136640 | bytes 49287168 | tf_op jit(solution)/shard_map/dot_general | solution.py:280
  69.5 0.7 multiply_multiply_fusion
  70.2 17.4 %fusion.17 = f32[1024,4096]{1,0:T(8,128)} fusion(bf16[2,1280,4096]{2,1,0:T(8,128)(2,1)} %param.13, bf16[1024,1280]{1,0:T(8,128)(2,1)S(1)} %get-tuple-element.100, f32[1024]{0:T(1024)S(1)} %get-tuple-element.98), kind=kOutput, calls=%fused_computation.30 | convolution fusion | flops 10741350400 | bytes 29888512 | tf_op jit(solution)/shard_map/dot_general | solution.py:280
  87.6 17.2 %fusion.21 = f32[1024,4096]{1,0:T(8,128)} fusion(bf16[2,1280,4096]{2,1,0:T(8,128)(2,1)} %param.14, bf16[1024,1280]{1,0:T(8,128)(2,1)S(1)} %get-tuple-element.100, f32[1024]{0:T(1024)S(1)} %get-tuple-element.98), kind=kOutput, calls=%fused_computation.34 | convolution fusion | flops 10741350400 | bytes 29888512 | tf_op jit(solution)/shard_map/dot_general | solution.py:280
  104.7 25.2 %fusion.2 = (bf16[1024,4096]{1,0:T(8,128)(2,1)}, bf16[1024,4096]{1,0:T(8,128)(2,1)}) fusion(f32[1024,4096]{1,0:T(8,128)} %fusion.17, f32[1024,4096]{1,0:T(8,128)} %fusion.21, bf16[2,4096,1280]{2,1,0:T(8,128)(2,1)} %param.15, bf16[1,1024,1280]{2,1,0:T(8,128)(2,1)S(1)} %copy-done.1), kind=kOutput, calls=%fused_computation.6 | convolution fusion | flops 10800332800 | bytes 63438848 | tf_op jit(solution)/shard_map/dot_general | solution.py:280
  129.9 18.2 %fusion.15 = f32[1024,1280]{1,0:T(8,128)} fusion(bf16[1024,4096]{1,0:T(8,128)(2,1)} %get-tuple-element.24.dg_ref, bf16[2,1280,4096]{2,1,0:T(8,128)(2,1)} %param.13), kind=kOutput, calls=%fused_computation.28 | convolution fusion | flops 10737418240 | bytes 24117248 | tf_op jit(solution)/shard_map/dot_general | solution.py:280
  148.1 17.4 %fusion.56 = f32[1024,1280]{1,0:T(8,128)S(1)} fusion(f32[1024,1280]{1,0:T(8,128)} %fusion.15, bf16[1024,4096]{1,0:T(8,128)(2,1)} %get-tuple-element.23.du_ref, bf16[2,1280,4096]{2,1,0:T(8,128)(2,1)} %param.14), kind=kOutput, calls=%fused_computation.72 | convolution fusion | flops 10738728960 | bytes 29360128 | tf_op jit(solution)/shard_map/dot_general | solution.py:280
  165.6 2.3 fusion.77
  167.9 2.8 fusion.67.d_ref
  170.7 28.0 %fusion.5 = (bf16[1024,4096]{1,0:T(8,128)(2,1)}, bf16[1024,4096]{1,0:T(8,128)(2,1)}) fusion(f32[1024,4096]{1,0:T(8,128)} %fusion.31, f32[1024,4096]{1,0:T(8,128)} %fusion.29, bf16[1024,1280]{1,0:T(8,128)(2,1)} %fusion.67.d_ref, bf16[2,4096,1280]{2,1,0:T(8,128)(2,1)} %param.15), kind=kOutput, calls=%fused_computation.9 | convolution fusion | flops 10800332800 | bytes 63438848 | tf_op jit(solution)/shard_map/dot_general | solution.py:280
  198.7 17.5 %copy.101 = f32[1024,4096]{0,1:T(8,128)} copy(f32[1024,4096]{1,0:T(8,128)} %fusion.29) | data formatting | bytes 33554432 | tf_op jit(solution)/shard_map/dot_general | solution.py:280
  216.2 17.4 %copy.100 = f32[1024,4096]{0,1:T(8,128)} copy(f32[1024,4096]{1,0:T(8,128)} %fusion.31) | data formatting | bytes 33554432 | tf_op jit(solution)/shard_map/dot_general | solution.py:280
  233.6 15.0 %fusion.10.p_ref = bf16[4096,1024]{1,0:T(8,128)(2,1)} fusion(f32[1024,4096]{0,1:T(8,128)} %copy.101, f32[1024,4096]{0,1:T(8,128)} %copy.100), kind=kLoop, calls=%fused_computation.18 | loop fusion | flops 25165824 | bytes 41943040 | tf_op jit(solution)/shard_map/convert_element_type | solution.py:290
  248.6 3.0 copy.102
  252.1 1.7 pad_maximum_fusion.1.a_ref
  253.8 17.4 %copy.104 = f32[1024,4096]{0,1:T(8,128)} copy(f32[1024,4096]{1,0:T(8,128)} %fusion.21) | data formatting | bytes 33554432 | tf_op jit(solution)/shard_map/dot_general | solution.py:280
  271.2 17.4 %copy.103 = f32[1024,4096]{0,1:T(8,128)} copy(f32[1024,4096]{1,0:T(8,128)} %fusion.17) | data formatting | bytes 33554432 | tf_op jit(solution)/shard_map/dot_general | solution.py:280
  288.7 15.0 %fusion.6.p_ref = bf16[4096,1024]{1,0:T(8,128)(2,1)} fusion(f32[1024,4096]{0,1:T(8,128)} %copy.104, f32[1024,4096]{0,1:T(8,128)} %copy.103), kind=kLoop, calls=%fused_computation.11 | loop fusion | flops 25165824 | bytes 41943040 | tf_op jit(solution)/shard_map/convert_element_type | solution.py:290
  303.7 40.2 %down_gradient.2._ = bf16[64,3840,128]{2,1,0:T(8,128)(2,1)} custom-call(bf16[4096,1024]{1,0:T(8,128)(2,1)} %fusion.6.p_ref, bf16[1024,1280]{1,0:T(8,128)(2,1)} %bitcast.383), custom_call_target="tpu_custom_call" | custom-call | flops 10737418240 | bytes 22000000 | tf_op jit(solution)/shard_map/down_gradient/pallas_call | solution.py:319
  343.9 38.5 %gate_up_gradients.2.refs_0_ = bf16[64,3840,128]{2,1,0:T(8,128)(2,1)} custom-call(bf16[1280,1024]{1,0:T(8,128)(2,1)} %pad_maximum_fusion.1.a_ref, bf16[1024,4096]{1,0:T(8,128)(2,1)} %get-tuple-element.24.dg_ref, bf16[1024,4096]{1,0:T(8,128)(2,1)} %get-tuple-element.23.du_ref, bf16[64,3840,128]{2,1,0:T(8,128)(2,1)} %down_gradient.2._), custom_call_target="tpu_custom_call", output_to_operand_aliasing={{}: (3, {})} | custom-call | flops 21474836480 | bytes 40000000 | tf_op jit(solution)/shard_map/gate_up_gradients/pallas_call | solution.py:355
  382.4 40.1 %down_gradient.3._ = bf16[64,3840,128]{2,1,0:T(8,128)(2,1)} custom-call(bf16[4096,1024]{1,0:T(8,128)(2,1)} %fusion.10.p_ref, bf16[1024,1280]{1,0:T(8,128)(2,1)} %fusion.67.d_ref, bf16[64,3840,128]{2,1,0:T(8,128)(2,1)} %gate_up_gradients.2.refs_0_), custom_call_target="tpu_custom_call", output_to_operand_aliasing={{}: (2, {})} | custom-call | flops 10737418240 | bytes 22000000 | tf_op jit(solution)/shard_map/down_gradient/pallas_call | solution.py:319
  422.5 38.8 %gate_up_gradients.3 = bf16[64,3840,128]{2,1,0:T(8,128)(2,1)} custom-call(bf16[1280,1024]{1,0:T(8,128)(2,1)} %pad_maximum_fusion.a_ref, bf16[1024,4096]{1,0:T(8,128)(2,1)} %get-tuple-element.22.dg_ref, bf16[1024,4096]{1,0:T(8,128)(2,1)} %get-tuple-element.21.du_ref, bf16[64,3840,128]{2,1,0:T(8,128)(2,1)} %down_gradient.3._), custom_call_target="tpu_custom_call", output_to_operand_aliasing={{}: (3, {})} | custom-call | flops 21474836480 | bytes 40000000 | tf_op jit(solution)/shard_map/gate_up_gradients/pallas_call | solution.py:355
  461.6 0.6 fusion.102
  462.4 1.4 fusion.101
  464.4 0.4 fusion.99
  464.9 0.7 fusion.98
  465.9 0.4 maximum_select_fusion
  467.5 1.2 fusion.97
  468.7 0.8 copy.115
  469.6 1.2 maximum_select_fusion.1
  471.0 0.7 copy.268
  472.6 1.0 pad_maximum_fusion.7
  473.7 2.4 pad_maximum_fusion.4.m
  476.3 0.6 fusion.92
  477.0 0.5 fusion.91
  477.5 0.5 fusion.94
  478.2 0.6 fusion.95
  478.9 0.4 maximum_select_fusion.6
  480.6 1.1 fusion.90
  482.3 0.6 maximum_select_fusion.4
  484.4 1.4 pad_maximum_fusion.5.v
  485.8 0.9 dynamic-slice_bitcast_fusion.10
  486.7 1.1 dynamic-slice_bitcast_fusion.6
  487.8 0.9 dynamic-slice_bitcast_fusion.11
  488.8 1.1 dynamic-slice_bitcast_fusion.7
  489.9 1.5 fusion.73
  492.0 1.0 constant_dynamic-slice_fusion
  494.1 461.1 %sum_step_gather.1 = (bf16[4,4,4,3840,128]{4,3,2,1,0:T(8,128)(2,1)}, f32[3840,128]{1,0:T(8,128)S(1)}, f32[3840,128]{1,0:T(8,128)S(1)}) custom-call(bf16[4,4,4,3840,128]{4,3,2,1,0:T(8,128)(2,1)} %bitcast.381, f32[3840,128]{1,0:T(8,128)} %pad_maximum_fusion.4.m, f32[3840,128]{1,0:T(8,128)} %pad_maximum_fusion.5.v, bf16[3840,128]{1,0:T(8,128)(2,1)S(1)} %pad_maximum_fusion.6.w), custom_call_target="tpu_custom_call" | custom-call | tf_op jit(solution)/shard_map/sum_step_gather/pallas_call | solution.py:270
  955.2 1.3 copy-done
  956.5 56.5 %unpack.1 = (bf16[2,1280,4096]{2,1,0:T(8,128)(2,1)}, bf16[2,1280,4096]{2,1,0:T(8,128)(2,1)}, bf16[2,4096,1280]{2,1,0:T(8,128)(2,1)}) custom-call(bf16[64,3840,128]{2,1,0:T(8,128)(2,1)} %bitcast.382), custom_call_target="tpu_custom_call" | custom-call | flops 1000000 | bytes 126000000 | tf_op jit(solution)/shard_map/unpack/pallas_call | solution.py:386
  1013.0 1.4 fusion.85
  1015.7 1.4 pad_maximum_fusion.11
  1018.3 1.4 pad_maximum_fusion.12
  1019.7 1.1 fusion.84
  1021.4 0.9 pad_maximum_fusion.13
  1023.7 1.4 pad_maximum_fusion.14
  1026.3 1.4 pad_maximum_fusion.15
  1028.3 0.9 pad_maximum_fusion.16
  (180 shorter events, 15.5 us)
Async XLA Ops:
  9.7 2.2 copy-start.2
  69.5 18.0 %copy-start.3 = (bf16[1024,1280]{1,0:T(8,128)(2,1)}, bf16[1024,1280]{1,0:T(8,128)(2,1)S(1)}, u32[]{:S(2)}) copy-start(bf16[1024,1280]{1,0:T(8,128)(2,1)S(1)} %get-tuple-element.100) | copy-start | bytes 7864324
  87.6 17.2 %copy-start.1 = (bf16[1,1024,1280]{2,1,0:T(8,128)(2,1)S(1)}, bf16[1,1024,1280]{2,1,0:T(8,128)(2,1)}, u32[]{:S(2)}) copy-start(bf16[1,1024,1280]{2,1,0:T(8,128)(2,1)} %param.12) | copy-start | bytes 7864324
  148.1 17.4 %copy-start.4 = (bf16[1024,1280]{1,0:T(8,128)(2,1)S(1)}, bf16[1024,1280]{1,0:T(8,128)(2,1)}, u32[]{:S(2)}) copy-start(bf16[1024,1280]{1,0:T(8,128)(2,1)} %copy-done.3) | copy-start | bytes 7864324
  165.6 2.3 copy-start.9
  422.5 38.8 %copy-start.5 = (f32[2,20,4096]{2,0,1:T(2,128)S(1)}, f32[2,20,4096]{2,0,1:T(2,128)}, u32[]{:S(2)}) copy-start(f32[2,20,4096]{2,0,1:T(2,128)} %param.17) | copy-start | bytes 1966084
  422.5 41.6 %copy-start.6 = (f32[2,20,4096]{2,0,1:T(2,128)S(1)}, f32[2,20,4096]{2,0,1:T(2,128)}, u32[]{:S(2)}) copy-start(f32[2,20,4096]{2,0,1:T(2,128)} %param.16) | copy-start | bytes 1966084
  467.4 8.7 copy-start.7
  468.7 8.8 copy-start.8
  955.2 1.3 copy-start

commit v3 on v2

--- a/solution.py
+++ b/solution.py
@@ -9,12 +9,200 @@
 STRIDE = {"x": 16, "y": 4, "z": 1}
 ORDERS = (("x", "y", "z"), ("y", "z", "x"), ("z", "x", "y"))
 BF, F32 = jnp.bfloat16, jnp.float32
+D, FF, TOKENS = 1280, 4096, 1024
 ROWS = 3840
-
-
-def comm_kernel(n_super, U, g, m, v, w, wall, m_out, v_out,
+U, SUPER = 80, 16
+
+
+def dot(a, b, dims):
+    return lax.dot_general(a, b, (dims, ((), ())), preferred_element_type=F32)
+
+
+class Refs:
+    def __init__(self, operands, buffers):
+        (self.a_hbm, self.at_hbm, self.dy_hbm, self.h_hbm, self.wg, self.wu, self.wd) = operands
+        (self.a, self.at, self.d, self.ws, self.wds, self.p, self.dgu, self.da, self.out, self.sem) = buffers
+
+    def slabs(self, i):
+        slot, layer = i % 2, 1 - i // 8
+        cols = pl.ds(pl.multiple_of(i % 8 * 512, 512), 512)
+        pairs = ((self.wg.at[layer, :, cols], self.ws.at[slot, 0]), (self.wu.at[layer, :, cols], self.ws.at[slot, 1]),
+                 (self.wd.at[layer, cols, :], self.wds.at[slot]))
+        return [pltpu.make_async_copy(src, dst, self.sem.at[slot, n]) for n, (src, dst) in enumerate(pairs)]
+
+    def states(self, slot):
+        return [pltpu.make_async_copy(self.a_hbm.at[slot], self.a, self.sem.at[0, 3]),
+                pltpu.make_async_copy(self.at_hbm.at[slot], self.at, self.sem.at[1, 3])]
+
+    def whole(self, src):
+        return pltpu.make_async_copy(src, self.d, self.sem.at[0, 4])
+
+    def put(self, g, row, n):
+        rows = pl.ds(pl.multiple_of(row, 16), n)
+        return [pltpu.make_async_copy(self.out.at[:, :, :, 0:n, :], g.at[:, :, :, rows, :], self.sem.at[1, 4])]
+
+
+def tasks_begin(r):
+    for copy in r.states(0) + r.slabs(0) + [r.whole(r.dy_hbm)]:
+        copy.start()
+    r.whole(r.dy_hbm).wait()
+
+
+def tasks(r, g, s):
+    slot, at = s // 8, s % 8
+
+    @pl.when(at < 5)
+    def _():
+        first = (3 * at + 1) // 2
+
+        @pl.when(at == 0)
+        def _():
+            for copy in r.states(slot):
+                copy.wait()
+
+        def one(f, _):
+            columns_task(r, g, slot, f, f > first)
+
+        lax.fori_loop(first, (3 * at + 4) // 2, one, None)
+
+    @pl.when((at == 5) & (slot == 0))
+    def _():
+        for copy in r.states(1):
+            copy.start()
+
+    @pl.when((at == 5) | (at == 6))
+    def _():
+        down_task(r, g, slot, at - 5, 512)
+
+    @pl.when(at == 7)
+    def _():
+        down_task(r, g, slot, 2, 256)
+
+        @pl.when(slot == 0)
+        def _():
+            next_layer(r)
+
+
+def tasks_done(r, g, s):
+    slot, at = s // 8, s % 8
+
+    @pl.when(at < 5)
+    def _():
+        for copy in r.put(g, 1920 * slot + 160 * ((3 * at + 2) // 2), 160):
+            copy.wait()
+
+    @pl.when((at == 5) | (at == 6))
+    def _():
+        for copy in r.put(g, 1920 * slot + 1280 + 256 * (at - 5), 256):
+            copy.wait()
+
+    @pl.when(at == 7)
+    def _():
+        for copy in r.put(g, 1920 * slot + 1792, 128):
+            copy.wait()
+
+
+def columns_task(r, g, slot, f, more):
+    i = 8 * slot + f
+    b = i % 2
+    for copy in r.slabs(i):
+        copy.wait()
+
+    @pl.when(i < 15)
+    def _():
+        for copy in r.slabs(i + 1):
+            copy.start()
+
+    cols = pl.ds(pl.multiple_of(f * 512, 512), 512)
+
+    @pl.loop(0, TOKENS // 256)
+    def _(t):
+        rows = pl.ds(pl.multiple_of(t * 256, 256), 256)
+        gate = dot(r.a[rows, :], r.ws[b, 0], ((1,), (0,)))
+        up = dot(r.a[rows, :], r.ws[b, 1], ((1,), (0,)))
+        dp = dot(r.d[rows, :], r.wds[b], ((1,), (1,))).astype(BF).astype(F32)
+        sig = jax.nn.sigmoid(gate)
+        silu = gate * sig
+        r.p[rows, cols] = (silu * up).astype(BF)
+        r.dgu[rows, 0:512] = (dp * up * (sig * (1 + gate * (1 - sig)))).astype(BF)
+        r.dgu[rows, 512:1024] = (dp * silu).astype(BF)
+
+    @pl.when(more)
+    def _():
+        for copy in r.put(g, 1920 * slot + 160 * (f - 1), 160):
+            copy.wait()
+
+    @pl.loop(0, 4)
+    def _(k):
+        rows = pl.ds(pl.multiple_of(k * 320, 64), 320)
+        of_gate = dot(r.at[rows, :], r.dgu[:, 0:512], ((1,), (0,)))
+        of_up = dot(r.at[rows, :], r.dgu[:, 512:1024], ((1,), (0,)))
+        low = lax.broadcasted_iota(jnp.int32, (8, 128), 0) < 4
+        for pair in range(8):
+            row = 40 * pair
+            for half in range(2):
+                parts = ([], [])
+                for ct in (2 * half, 2 * half + 1):
+                    tile = slice(128 * ct, 128 * ct + 128)
+                    gm, um = of_gate[row + 16 : row + 24, tile], of_up[row + 16 : row + 24, tile]
+                    parts[0].extend((of_gate[row : row + 16, tile], of_up[row : row + 16, tile], jnp.where(low, gm, pltpu.roll(um, 4, 0))))
+                    parts[1].extend((of_gate[row + 24 : row + 40, tile], of_up[row + 24 : row + 40, tile], jnp.where(low, pltpu.roll(gm, 4, 0), um)))
+                for odd in range(2):
+                    r.out[k, pair // 2, pair % 2 * 2 + odd, 80 * half : 80 * half + 80, :] = jnp.concatenate(parts[odd], 0).astype(BF)
+
+    for copy in r.put(g, 1920 * slot + 160 * f, 160):
+        copy.start()
+
+    @pl.when(slot == 0)
+    def _():
+        @pl.loop(0, TOKENS // 256)
+        def _(t):
+            rows = pl.ds(pl.multiple_of(t * 256, 256), 256)
+            more = dot(r.dgu[rows, 0:512], r.ws[b, 0], ((1,), (1,))) + dot(r.dgu[rows, 512:1024], r.ws[b, 1], ((1,), (1,)))
+
+            @pl.when(f == 0)
+            def _():
+                r.da[rows, :] = more
+
+            @pl.when(f > 0)
+            def _():
+                r.da[rows, :] += more
+
+
+def down_task(r, g, slot, t, width):
+    cols = pl.ds(pl.multiple_of(t * 512, 512), width)
+
+    @pl.loop(0, 8)
+    def _(k):
+        of_down = dot(r.p[:, pl.ds(pl.multiple_of(k * 512, 512), 512)], r.d[:, cols], ((0,), (0,)))
+        for ct in range(width // 128):
+            part = of_down[:, 128 * ct : 128 * ct + 128].reshape(2, 4, 64, 128).astype(BF)
+            r.out[k // 2, pl.ds(k % 2 * 2, 2), :, 64 * ct : 64 * ct + 64, :] = part
+
+    for copy in r.put(g, 1920 * slot + 1280 + 256 * t, width // 2):
+        copy.start()
+
+
+def next_layer(r):
+    h = pltpu.make_async_copy(r.h_hbm, r.p.at[:, 0:D], r.sem.at[0, 5])
+    h.start()
+    h.wait()
+
+    @pl.loop(0, TOKENS // 128)
+    def _(t):
+        rows = pl.ds(pl.multiple_of(t * 128, 128), 128)
+        wide = r.p[rows, 0:D].astype(F32)
+        d = r.da[rows, :].astype(BF).astype(F32)
+        scale = lax.rsqrt(jnp.mean(wide * wide, -1, keepdims=True) + 1e-6)
+        along = jnp.mean(wide * d, -1, keepdims=True)
+        through = (scale * d - wide * (scale * scale * scale) * along).astype(BF)
+        r.d[rows, :] = (r.d[rows, :].astype(F32) + through.astype(F32)).astype(BF)
+
+
+def comm_kernel(refs, g, m, v, w, wall, m_out, v_out,
                 recv1, send2, recv2, own, sa, b1s, b1r, b2s, b2r, sb, c1s, c1r, c2s, c2r,
                 mb, vb, wb, mo, vo, wn, ssem, rsem, lsem):
+    n_super = SUPER
     me = lax.axis_index("dp")
     pos = {"x": me // 16, "y": (me // 4) % 4, "z": me % 4}
     low = (U // 2 + 15) // 16 * 16
@@ -244,22 +432,38 @@
     stages = (stage0, stage1, stage2, stage3, stage4, stage5, stage6, stage7, stage8, later(3), later(4), later(5), stage12)
 
     def iteration(s):
+        @pl.when(s < n_super)
+        def _():
+            tasks(refs, g, s)
+
         for number in reversed(range(len(stages))):
             j = s - number
 
             @pl.when((j >= 0) & (j < n_super))
             def _():
+                if number == 0:
+                    tasks_done(refs, g, s)
                 for c in range(3):
                     stages[number](Chunk(c, j))
 
+    tasks_begin(refs)
     loop(n_super + len(stages) - 1, iteration)
 
 
-def comm(g, m, v, w, U, n_super, collective_id=0):
-    rows = g.shape[3]
+COMM_SCRATCH = 23
+
+
+def whole_kernel(*refs):
+    ins, outs, scratch = refs[:10], refs[10:14], refs[14:]
+    m, v, w = ins[7:]
+    wall, m_out, v_out, g = outs
+    comm_kernel(Refs(ins[:7], scratch[COMM_SCRATCH:]), g, m, v, w, wall, m_out, v_out, *scratch[:COMM_SCRATCH])
+
+
+def backward_and_step(a, at, dy, h, wg, wu, wd, m, v, w):
     hbm = pl.BlockSpec(memory_space=pl.ANY)
     V, two = pltpu.VMEM, (2, 3)
-    scratch = [
+    comm_scratch = [
         V(two + (4, 4, U, 128), BF), V(two + (2, 4, 4, U, 128), BF), V(two + (2, 4, 4, U, 128), BF), V(two + (4, 4, U, 128), BF),
         V(two + (4, 4, U, 128), F32),
         V(two + (4, U, 128), BF), V(two + (4, U, 128), BF), V(two + (2, 4, U, 128), BF), V(two + (2, 4, U, 128), BF), V(two + (4, U, 128), F32),
@@ -267,122 +471,50 @@
         V(two + (U, 128), F32), V(two + (U, 128), F32), V(two + (U, 128), BF), V(two + (U, 128), F32), V(two + (U, 128), F32), V(two + (U, 128), BF),
         pltpu.SemaphoreType.DMA((12, 2, 3, 2)), pltpu.SemaphoreType.DMA((12, 2, 3, 2)), pltpu.SemaphoreType.DMA((9, 2, 3)),
     ]
+    task_scratch = [
+        V((TOKENS, D), BF), V((D, TOKENS), BF), V((TOKENS, D), BF), V((2, 2, D, 512), BF), V((2, 512, D), BF),
+        V((TOKENS, FF), BF), V((TOKENS, 1024), BF), V((TOKENS, D), F32), V((4, 4, 4, 256, 128), BF), pltpu.SemaphoreType.DMA((2, 6)),
+    ]
+    units = jax.ShapeDtypeStruct((4, 4, 4, ROWS, 128), BF)
+    moment = jax.ShapeDtypeStruct((ROWS, 128), F32)
     return pl.pallas_call(
-        functools.partial(comm_kernel, n_super, U),
-        out_shape=(jax.ShapeDtypeStruct(g.shape, BF), jax.ShapeDtypeStruct(m.shape, F32), jax.ShapeDtypeStruct(v.shape, F32)),
-        in_specs=[hbm] * 4, out_specs=(hbm,) * 3, scratch_shapes=scratch,
-        compiler_params=pltpu.CompilerParams(collective_id=collective_id, has_side_effects=True, vmem_limit_bytes=48 * 2**20),
-        name="sum_step_gather",
-    )(g, m, v, w)
-
-
-def dot(a, b, dims):
-    return lax.dot_general(a, b, (dims, ((), ())), preferred_element_type=F32)
-
-
-def scale_of(h):
-    wide = h.astype(F32)
-    return lax.rsqrt(jnp.mean(wide**2, -1, keepdims=True) + 1e-6)
-
-
-def hidden(a, w_gate, w_up):
-    gate, up = dot(a, w_gate, ((1,), (0,))), dot(a, w_up, ((1,), (0,)))
-    return gate, up, (jax.nn.silu(gate) * up).astype(BF)
-
-
-def of_hidden(d, gate, up):
-    d = d.astype(F32)
-    s = jax.nn.sigmoid(gate)
-    d_gate = d * up * (s * (1 + gate * (1 - s)))
-    return d_gate.astype(BF), (d * (gate * s)).astype(BF)
-
-
-def of_norm(h, scale, d):
-    wide, d = h.astype(F32), d.astype(F32)
-    along = jnp.mean(wide * d, -1, keepdims=True)
-    return (scale * d - wide * (scale * scale * scale) * along).astype(BF)
-
-
-def down_kernel(p_ref, d_ref, *refs):
-    out = refs[-1]
-    for ct in range(2):
-        @pl.loop(0, 8)
-        def _(i):
-            rows = pl.ds(pl.multiple_of(i * 512, 512), 512)
-            r = jnp.dot(p_ref[rows, :], d_ref[:, ct * 128 : ct * 128 + 128], preferred_element_type=F32)
-            out[pl.ds(i * 8, 8), ct * 64 : ct * 64 + 64, :] = r.reshape(8, 64, 128).astype(BF)
-
-
-def down_gradient(p_t, d, at, g=None):
-    tokens = d.shape[0]
-    whole = pl.BlockSpec((4096, tokens), lambda i: (0, 0))
-    return pl.pallas_call(
-        down_kernel,
-        grid=(5,),
-        out_shape=jax.ShapeDtypeStruct((64, ROWS, 128), BF),
-        in_specs=[whole, pl.BlockSpec((tokens, 256), lambda i: (0, i))] + [pl.BlockSpec(memory_space=pl.ANY)] * (g is not None),
-        out_specs=pl.BlockSpec((64, 128, 128), lambda i: (0, at // 128 + i, 0)),
-        input_output_aliases={} if g is None else {2: 0},
-        cost_estimate=pl.CostEstimate(flops=2 * 4096 * 1280 * 1024, bytes_accessed=22 * 10**6, transcendentals=0),
-        name="down_gradient",
-    )(p_t, d, *([] if g is None else [g]))
-
-
-def mixed(even, odd):
-    row = lax.broadcasted_iota(jnp.int32, even.shape, 1)
-    return (jnp.where(row < 4, even, pltpu.roll(odd, 4, 1)), jnp.where(row < 4, pltpu.roll(even, 4, 1), odd))
-
-
-def gate_up_kernel(a_ref, dg_ref, du_ref, _, out):
-    @pl.loop(0, 4)
-    def _(i):
-        rows = pl.ds(pl.multiple_of(i * 256, 256), 256)
-        for at, d in ((0, dg_ref), (32, du_ref)):
-            r = jnp.dot(a_ref[rows, :], d[...], preferred_element_type=F32)
-            for ct in range(2):
-                out[pl.ds(i * 16, 16), at + 16 * ct : at + 16 * ct + 16, :] = r[:, ct * 128 : ct * 128 + 128].reshape(16, 16, 128).astype(BF)
-    last = [jnp.dot(a_ref[1024:, :], d[...], preferred_element_type=F32) for d in (dg_ref, du_ref)]
-    tiles = [mixed(*(r[:, ct * 128 : ct * 128 + 128].reshape(32, 8, 128) for r in last)) for ct in range(2)]
-    for odd in range(2):
-        both = jnp.concatenate([tiles[0][odd], tiles[1][odd]], 1).astype(BF)
-        for pair in range(32):
-            out[2 * pair + odd, 64:80, :] = both[pair]
-
-
-def gate_up_gradients(a_t, dg, du, at, g):
-    tokens = dg.shape[0]
-    slab = pl.BlockSpec((tokens, 256), lambda i: (0, i))
-    return pl.pallas_call(
-        gate_up_kernel,
-        grid=(16,),
-        out_shape=jax.ShapeDtypeStruct((64, ROWS, 128), BF),
-        in_specs=[pl.BlockSpec((1280, tokens), lambda i: (0, 0)), slab, slab, pl.BlockSpec(memory_space=pl.ANY)],
-        out_specs=pl.BlockSpec((64, 80, 128), lambda i: (0, at // 80 + i, 0)),
-        input_output_aliases={3: 0},
-        cost_estimate=pl.CostEstimate(flops=4 * 4096 * 1280 * 1024, bytes_accessed=40 * 10**6, transcendentals=0),
-        name="gate_up_gradients",
-    )(a_t, dg, du, g)
+        whole_kernel,
+        out_shape=(units, moment, moment, units),
+        in_specs=[hbm] * 10,
+        out_specs=(hbm,) * 4,
+        scratch_shapes=comm_scratch + task_scratch,
+        compiler_params=pltpu.CompilerParams(collective_id=0, has_side_effects=True, vmem_limit_bytes=67043328),
+        name="backward_and_step",
+    )(a, at, dy, h, wg, wu, wd, m, v, w)[:3]
 
 
 def unpack_kernel(w_ref, gate, up, down):
+    low = lax.broadcasted_iota(jnp.int32, (8, 128), 0) < 4
     for d in range(4):
         for ct in range(10):
-            down[0, 64 * d : 64 * d + 64, ct * 128 : ct * 128 + 128] = w_ref[d, 64 * ct : 64 * ct + 64, :]
+            down[0, 64 * d : 64 * d + 64, ct * 128 : ct * 128 + 128] = w_ref[d, 1280 + 64 * ct : 1344 + 64 * ct, :]
 
     @pl.loop(0, 16)
     def _(slab):
-        base = pl.multiple_of(640 + 80 * slab, 16)
-        mix = [w_ref[d, pl.ds(base + 64, 16), :].astype(F32) for d in range(4)]
+        rows = pl.ds(pl.multiple_of(80 * slab, 16), 80)
+        units = [w_ref[d, rows, :].astype(F32) for d in range(4)]
         for ct in range(2):
-            tiles = [mixed(*(mix[2 * pair + odd][8 * ct : 8 * ct + 8][None] for odd in range(2))) for pair in range(2)]
+            own = [u[40 * ct : 40 * ct + 40] for u in units]
+            tile = pl.ds(pl.multiple_of(slab * 256 + ct * 128, 128), 128)
             for which, out in enumerate((gate, up)):
-                own = [w_ref[d, pl.ds(base + 32 * which + 16 * ct, 16), :].astype(F32) for d in range(4)]
-                rows = jnp.concatenate([own[0], tiles[0][which][0], own[1], own[2], tiles[1][which][0], own[3]], 0)
-                out[0, :, pl.ds(pl.multiple_of(slab * 256 + ct * 128, 128), 128)] = rows.astype(BF)
+                parts = []
+                for even, odd in ((own[0], own[1]), (own[2], own[3])):
+                    left, right = even[32:40], odd[32:40]
+                    if which == 0:
+                        right = pltpu.roll(right, 4, 0)
+                    else:
+                        left = pltpu.roll(left, 4, 0)
+                    parts += [even[16 * which : 16 * which + 16], jnp.where(low, left, right), odd[16 * which : 16 * which + 16]]
+                out[0, :, tile] = jnp.concatenate(parts, 0).astype(BF)
 
 
 def unpack(wall):
-    shapes = ((2, 1280, 4096), (2, 1280, 4096), (2, 4096, 1280))
+    shapes = ((2, D, FF), (2, D, FF), (2, FF, D))
     return pl.pallas_call(
         unpack_kernel,
         grid=(2, 16),
@@ -394,64 +526,45 @@
     )(wall)
 
 
-def row_order(w_t):
-    pairs = w_t.reshape(32, 40, -1)
-    own = jnp.concatenate([pairs[:, :16], pairs[:, 24:]], 1)
-    return jnp.concatenate([own.reshape(1024, -1), pairs[:, 16:24].reshape(256, -1)], 0)
-
-
 def to_units(odd, gate, up, down):
-    whole, left = [], []
-    for t in (gate, up):
-        t = jnp.where(odd, jnp.roll(t, -4, 0), t)
-        whole.append(t[:16].reshape(16, 16, 2, 128).transpose(1, 2, 0, 3).reshape(16, 32, 128))
-        left.append(t[16:].reshape(4, 16, 2, 128).transpose(1, 2, 0, 3))
-    slabs = jnp.concatenate(whole + [jnp.concatenate(left, 2).reshape(16, 16, 128)], 1)
-    return jnp.concatenate([down.reshape(64, 10, 128).transpose(1, 0, 2).reshape(640, 128), slabs.reshape(1280, 128)], 0)
+    gate, up = (jnp.where(odd, jnp.roll(t, -4, 1), t) for t in (gate, up))
+    tiles = jnp.concatenate([gate[:, :16], up[:, :16], gate[:, 16:], up[:, 16:]], 1)
+    tiles = tiles.reshape(2, 40, 32, 128).transpose(0, 2, 1, 3).reshape(2, 1280, 128)
+    units = jnp.concatenate([tiles, down.reshape(2, 64, 10, 128).transpose(0, 2, 1, 3).reshape(2, 640, 128)], 1)
+    return units[::-1].reshape(ROWS, 128)
 
 
 def from_units(odd, units):
-    slabs = units[640:].reshape(16, 80, 128)
-    left = slabs[:, 64:].reshape(16, 2, 2, 4, 128)
-    out = []
-    for i in range(2):
-        whole = slabs[:, 32 * i : 32 * i + 32].reshape(16, 2, 16, 128).transpose(2, 0, 1, 3).reshape(16, 4096)
-        t = jnp.concatenate([whole, left[:, :, i].transpose(2, 0, 1, 3).reshape(4, 4096)], 0)
-        out.append(jnp.where(odd, jnp.roll(t, 4, 0), t))
-    return out + [units[:640].reshape(10, 64, 128).transpose(1, 0, 2).reshape(64, 1280)]
+    units = units.reshape(2, 1920, 128)[::-1]
+    tiles = units[:, :1280].reshape(2, 32, 40, 128).transpose(0, 2, 1, 3).reshape(2, 40, FF)
+    gate = jnp.concatenate([tiles[:, :16], tiles[:, 32:36]], 1)
+    up = jnp.concatenate([tiles[:, 16:32], tiles[:, 36:]], 1)
+    down = units[:, 1280:].reshape(2, 10, 64, 128).transpose(0, 2, 1, 3).reshape(2, 64, D)
+    return [jnp.where(odd, jnp.roll(t, 4, 1), t) for t in (gate, up)] + [down]
+
+
+def normed(h):
+    wide = h.astype(F32)
+    return (wide * lax.rsqrt(jnp.mean(wide**2, -1, keepdims=True) + 1e-6)).astype(BF)
 
 
 def solution(mesh):
     def step(x, dy, *arrays):
         weights, ms, vs = arrays[:3], arrays[3:6], arrays[6:]
         wg, wu, wd = weights
-        h0, dy = x[0], dy[0]
-        s0 = scale_of(h0)
-        a0 = (h0.astype(F32) * s0).astype(BF)
-        g0, u0, p0 = hidden(a0, wg[0], wu[0])
+        h0 = x[0]
+        a0 = normed(h0)
+        gate, up = (dot(a0, w[0], ((1,), (0,))) for w in (wg, wu))
+        p0 = (jax.nn.silu(gate) * up).astype(BF)
         h1 = h0 + dot(p0, wd[0], ((1,), (0,))).astype(BF)
-        s1 = scale_of(h1)
-        a1 = (h1.astype(F32) * s1).astype(BF)
-        g1, u1, p1 = hidden(a1, wg[1], wu[1])
-        grads = down_gradient(p1.T, dy, 0)
-        dg1, du1 = of_hidden(dot(dy, wd[1], ((1,), (1,))).astype(BF), g1, u1)
-        grads = gate_up_gradients(row_order(a1.T), dg1, du1, 640, grads)
-        da1 = dot(dg1, wg[1], ((1,), (1,))) + dot(du1, wu[1], ((1,), (1,)))
-        dh1 = dy + of_norm(h1, s1, da1)
-        grads = down_gradient(p0.T, dh1, 1920, grads)
-        dg0, du0 = of_hidden(dot(dh1, wd[0], ((1,), (1,))).astype(BF), g0, u0)
-        grads = gate_up_gradients(row_order(a0.T), dg0, du0, 2560, grads)
+        a = jnp.stack([normed(h1), a0])
 
         me = lax.axis_index("dp")
         odd = me % 2 == 1
         own = [lax.dynamic_slice_in_dim(w, me * (w.shape[1] // 64), w.shape[1] // 64, 1) for w in weights]
-        mine = [jnp.concatenate([to_units(odd, *(t[layer] for t in three)) for layer in (1, 0)], 0) for three in (ms, vs, own)]
-        wall, *moments = comm(grads.reshape(4, 4, 4, ROWS, 128), *mine, 80, 16)
-        new = list(unpack(wall.reshape(64, ROWS, 128)))
-        for t in moments:
-            layers = [from_units(odd, t[1920 * (1 - layer) :][:1920]) for layer in (0, 1)]
-            new += [jnp.stack(pair) for pair in zip(*layers, strict=True)]
-        return tuple(new)
+        units = [to_units(odd, *three) for three in (ms, vs, own)]
+        wall, *moments = backward_and_step(a, a.transpose(0, 2, 1), dy[0], h1, wg, wu, wd, *units)
+        return tuple(unpack(wall.reshape(64, ROWS, 128))) + tuple(t for units in moments for t in from_units(odd, units))
 
     seq, whole, rows = P(("rep", "dp")), P(), P(None, "dp", None)
     return jax.shard_map(

time: 1040 us -> 721 us (0.69)
  matrix products: 181 us -> 54.1 us
  Pallas kernels: 675 us -> 593 us
  local copies, waits for them, and re-layouts: 105 us -> 43.3 us
  other arithmetic: 66 us -> 23.8 us
    dot_general x9 -> x3, matrix products: 181 us -> 54.1 us  [dot(): return lax.dot_general(a, b, (dims, ((), ())), preferred_element_type=F32)]
    pallas_call x5 -> x1, Pallas kernels: 619 us -> 537 us  [backward_and_step(): pl.pallas_call(whole_kernel, out_shape=(units, moment, moment, units), in...]
    dot_general x4 -> x0, local copies, waits for them, and re-layouts: 69.8 us -> none  [dot(): return lax.dot_general(a, b, (dims, ((), ())), preferred_element_type=F32)]
    convert_element_type x2 -> x1, other arithmetic: 30 us -> 1.98 us  [normed(): (wide * lax.rsqrt(jnp.mean(wide ** 2, -1, keepdims=True) + 1e-06)).astype...]
    slice x63 -> x44, local copies, waits for them, and re-layouts: 17 us -> 4.75 us  [the longest x4 1.67 us: from_units(): units[:, :1280].reshape(2, 32, 40, 128).transpose(0, 2, 1, 3)]
where the time goes in v3:
time: 721 us; the launch traced here: 716 us
  Pallas kernels  593 us (82%)
  matrix products  54.1 us (8%)
  local copies, waits for them, and re-layouts  43.3 us (6%)
  other arithmetic  23.8 us (3%)
    pallas_call x1, Pallas kernels, backward_and_step(): pl.pallas_call(whole_kernel, out_shape=(units, moment, moment, units), in...  537 us
    pallas_call x1, Pallas kernels, unpack(): pl.pallas_call(unpack_kernel, grid=(2, 16), out_shape=tuple((jax.ShapeDty...  55.8 us
    dot_general x3, matrix products, dot(): return lax.dot_general(a, b, (dims, ((), ())), preferred_element_type=F32)  54.1 us

profile of v3, /device:TPU:0, one launch (start us, length us, event | category | flops | bytes accessed | tf_op | source)
XLA Modules:
  0.0 715.8 jit_solution(7640185572805459267)
XLA Ops:
  0.7 2.3 multiply_reduce_fusion
  3.0 1.0 constant_dynamic-slice_fusion
  4.0 0.2 reshape.147
  4.2 0.1 copy.47
  4.3 1.2 constant_dynamic-slice_fusion.2
  5.6 0.1 slice.194
  5.6 0.3 copy.66
  5.9 1.2 constant_dynamic-slice_fusion.1
  7.2 0.1 slice.197
  7.3 0.3 copy.64
  7.5 1.4 broadcast_select_fusion
  9.0 0.2 slice.199
  9.3 0.2 slice.196
  9.5 1.2 pad_maximum_fusion.6
  10.7 0.5 reshape.145
  11.2 0.4 copy.46
  11.8 1.0 rev.13
  12.8 0.3 slice-done
  13.1 0.2 slice-done.1
  13.3 0.2 slice-done.3
  13.5 2.2 maximum_select_fusion
  15.8 0.7 pad_maximum_fusion.3
  16.6 1.1 reshape.135
  17.8 1.8 copy.40
  19.6 0.2 copy-done.7
  19.8 1.5 maximum_select_fusion.2
  21.5 0.7 pad_maximum_fusion.4
  22.2 1.1 reshape.140
  23.4 1.8 copy.42
  25.2 1.3 reshape.137
  26.5 0.2 copy.41
  26.7 0.1 pad_maximum_fusion.1
  26.9 1.4 rev.11
  28.3 0.1 reshape.142
  28.4 0.2 copy.43
  28.6 1.0 copy-done.4
  29.6 1.4 pad_maximum_fusion.2
  31.0 3.1 rev.12
  34.1 2.0 multiply_convert_fusion.2
  36.1 17.3 %fusion.4 = f32[1024,4096]{1,0:T(8,128)} fusion(bf16[2,1280,4096]{2,1,0:T(8,128)(2,1)} %refs_4_.1, bf16[1,1024,1280]{2,1,0:T(8,128)(2,1)S(1)} %copy-done.1, f32[1024]{0:T(1024)S(1)} %add_rsqrt_fusion.1), kind=kOutput, calls=%fused_computation.5 | convolution fusion | flops 10741350400 | bytes 29888512 | tf_op jit(solution)/shard_map/dot_general | solution.py:18
  53.4 19.9 %multiply_convert_fusion.6.clone.5 = bf16[1024,4096]{1,0:T(8,128)(2,1)} fusion(f32[1024,4096]{1,0:T(8,128)} %fusion.4, bf16[2,1280,4096]{2,1,0:T(8,128)(2,1)} %refs_5_.1, bf16[1,1024,1280]{2,1,0:T(8,128)(2,1)S(1)} %copy-done.1, f32[1024]{0:T(1024)S(1)} %add_rsqrt_fusion.1), kind=kOutput, calls=%fused_computation.clone.clone.clone.clone.clone.clone.clone.clone.2 | convolution fusion | flops 10766516224 | bytes 38277120 | tf_op jit(solution)/shard_map/dot_general | solution.py:18
  73.3 16.9 %fusion.9 = (f32[1024]{0:T(1024)S(1)}, bf16[1024,1280]{1,0:T(8,128)(2,1)S(1)}) fusion(bf16[2,4096,1280]{2,1,0:T(8,128)(2,1)} %refs_6_.1, bf16[1,1024,1280]{2,1,0:T(8,128)(2,1)S(1)} %copy-done.1, bf16[1024,4096]{1,0:T(8,128)(2,1)} %multiply_convert_fusion.6.clone.5), kind=kOutput, calls=%fused_computation.12 | convolution fusion | flops 10743970816 | bytes 24121344 | tf_op jit(solution)/shard_map/dot_general | solution.py:18
  90.3 1.5 copy-done
  91.7 0.5 fusion.17
  92.2 1.2 copy-done.2
  93.5 4.8 fusion.29
  98.2 7.9 %copy.48.refs_1_ = bf16[2,1280,1024]{2,1,0:T(8,128)(2,1)} copy(bf16[2,1280,1024]{1,2,0:T(8,128)(2,1)} %get-tuple-element.21) | data formatting | bytes 10485760 | tf_op jit(solution)/shard_map/transpose | solution.py:566
  106.1 537.1 %backward_and_step.1 = (bf16[4,4,4,3840,128]{4,3,2,1,0:T(8,128)(2,1)}, f32[3840,128]{1,0:T(8,128)}, f32[3840,128]{1,0:T(8,128)}, bf16[4,4,4,3840,128]{4,3,2,1,0:T(8,128)(2,1)}) custom-call(bf16[2,1024,1280]{2,1,0:T(8,128)(2,1)} %get-tuple-element.22.refs_0_, bf16[2,1280,1024]{2,1,0:T(8,128)(2,1)} %copy.48.refs_1_, bf16[1024,1280]{1,0:T(8,128)(2,1)} %bitcast.116, ...), custom_call_target="tpu_custom_call" | custom-call | tf_op jit(solution)/shard_map/backward_and_step/pallas_call | solution.py:480
  643.2 55.8 %unpack.1 = (bf16[2,1280,4096]{2,1,0:T(8,128)(2,1)}, bf16[2,1280,4096]{2,1,0:T(8,128)(2,1)}, bf16[2,4096,1280]{2,1,0:T(8,128)(2,1)}) custom-call(bf16[64,3840,128]{2,1,0:T(8,128)(2,1)} %bitcast.104), custom_call_target="tpu_custom_call" | custom-call | flops 1000000 | bytes 126000000 | tf_op jit(solution)/shard_map/unpack/pallas_call | solution.py:518
  699.0 1.1 slice.207
  700.1 1.4 slice.202
  701.5 0.1 slice.171
  701.6 1.3 copy.49
  703.0 2.0 reshape.153
  705.0 0.9 copy.62
  706.0 1.2 maximum_select_fusion.5
  707.2 1.2 maximum_select_fusion.4
  708.4 0.1 slice.208
  708.5 0.1 slice.179
  708.6 1.3 copy.51
  709.9 2.0 reshape.158
  712.0 0.9 copy.61
  712.9 1.2 maximum_select_fusion.7
  714.1 1.2 maximum_select_fusion.6
  (53 shorter events, 1.0 us)
Async XLA Ops:
  11.7 1.2 copy-start.5
  11.7 1.5 slice-start
  11.7 1.6 slice-start.1
  11.7 1.6 slice-start.2
  11.7 1.8 slice-start.3
  17.7 1.9 copy-start.6
  17.7 1.9 slice-start.4
  17.7 1.9 slice-start.5
  17.8 2.0 copy-start.7
  17.8 2.1 slice-start.6
  17.8 2.1 slice-start.7
  25.2 1.5 copy-start.3
  26.8 1.5 copy-start.9
  28.3 1.3 copy-start.4
  31.0 3.1 copy-start.1
  90.2 1.5 copy-start
  91.7 1.7 copy-start.2
  705.9 2.5 copy-start.8

commit v4 on v3

v4 whole, which is shorter than its diff:
```python
import jax
import jax.numpy as jnp
from jax import lax
from jax.experimental import pallas as pl
from jax.experimental.pallas import tpu as pltpu
from jax.sharding import PartitionSpec as P

AXES = ("x", "y", "z")
STRIDE = {"x": 16, "y": 4, "z": 1}
ORDERS = (("x", "y", "z"), ("y", "z", "x"), ("z", "x", "y"))
BF, F32 = jnp.bfloat16, jnp.float32
D, FF, TOKENS = 1280, 4096, 1024
ROWS = 3840
U, SUPER = 80, 16


def dot(a, b, dims):
    return lax.dot_general(a, b, (dims, ((), ())), preferred_element_type=F32)


def loop(n, body, unroll=1):
    lax.fori_loop(0, n, lambda i, _: (body(i), None)[1], None, unroll=unroll)


def start(copies):
    for copy in copies:
        copy.start()


def wait(copies):
    for copy in copies:
        copy.wait()


class Refs:
    def __init__(self, operands, buffers):
        self.x, self.dy, self.wg, self.wu, self.wd, self.h = operands
        self.a, self.d, self.ws, self.wds, self.p, self.dgu, self.da, self.out, self.sem = buffers
        self.state = self.p.at[:, FF - D :]

    def slabs(self, i):
        slot, layer = i % 2, i // 8 % 2
        cols = pl.ds(pl.multiple_of(i % 8 * 512, 512), 512)
        pairs = ((self.wg.at[layer, :, cols], self.ws.at[slot, 0]), (self.wu.at[layer, :, cols], self.ws.at[slot, 1]),
                 (self.wd.at[layer, cols, :], self.wds.at[slot]))
        return [pltpu.make_async_copy(src, dst, self.sem.at[slot, n]) for n, (src, dst) in enumerate(pairs)]

    def next_slabs(self, i):
        wait(self.slabs(i))

        @pl.when(i < 23)
        def _():
            start(self.slabs(i + 1))

    def copy(self, n, src, dst):
        return [pltpu.make_async_copy(src, dst, self.sem.at[n // 4, 3 + n % 4])]

    def load_x(self):
        return self.copy(0, self.x, self.state)

    def load_dy(self):
        return self.copy(1, self.dy, self.d)

    def keep_h(self):
        return self.copy(2, self.state, self.h)

    def back_h(self):
        return self.copy(3, self.h, self.state)

    def load_a(self):
        return self.copy(4, self.x, self.a)

    def put(self, g, row, n):
        return self.copy(5, self.out.at[:, :, :, 0:n, :], g.at[:, :, :, pl.ds(pl.multiple_of(row, 16), n), :])


def normed(h):
    wide = h.astype(F32)
    return (wide * lax.rsqrt(jnp.mean(wide * wide, -1, keepdims=True) + 1e-6)).astype(BF)


def token_blocks(size, body):
    loop(TOKENS // size, lambda t: body(pl.ds(pl.multiple_of(t * size, size), size)))


def add_to(ref, rows, first, more):
    @pl.when(first)
    def _():
        ref[rows, :] = more

    @pl.when(jnp.logical_not(first))
    def _():
        ref[rows, :] += more


def forward(r):
    start(r.load_x() + r.slabs(0) + r.load_dy())
    wait(r.load_x())

    def norm(rows):
        r.a[rows, :] = normed(r.state[rows, :])

    token_blocks(128, norm)

    def task(f):
        r.next_slabs(f)
        b = f % 2

        def block(rows):
            gate = dot(r.a[rows, :], r.ws[b, 0], ((1,), (0,)))
            up = dot(r.a[rows, :], r.ws[b, 1], ((1,), (0,)))
            p = (gate * jax.nn.sigmoid(gate) * up).astype(BF)
            add_to(r.da, rows, f == 0, dot(p, r.wds[b], ((1,), (0,))))

        token_blocks(256, block)

    loop(8, task)

    def end(rows):
        h = (r.state[rows, :].astype(F32) + r.da[rows, :].astype(BF).astype(F32)).astype(BF)
        r.state[rows, :] = h
        r.a[rows, :] = normed(h)

    token_blocks(128, end)
    start(r.keep_h())
    wait(r.load_dy())


def tasks(r, g, s):
    slot, at = s // 8, s % 8

    @pl.when(at < 5)
    def _():
        first = (3 * at + 1) // 2

        @pl.when(s == 1)
        def _():
            wait(r.keep_h())

        @pl.when(s == 8)
        def _():
            wait(r.load_a())

            def norm(rows):
                r.a[rows, :] = normed(r.a[rows, :])

            token_blocks(128, norm)

        def one(f, _):
            columns_task(r, g, slot, f, f > first)

        lax.fori_loop(first, (3 * at + 4) // 2, one, None)

    @pl.when(s == 5)
    def _():
        start(r.load_a())

    @pl.when((at == 5) | (at == 6))
    def _():
        down_task(r, g, slot, at - 5, 512)

    @pl.when(at == 7)
    def _():
        down_task(r, g, slot, 2, 256)

        @pl.when(slot == 0)
        def _():
            next_layer(r)


def tasks_done(r, g, s):
    slot, at = s // 8, s % 8

    @pl.when(at < 5)
    def _():
        wait(r.put(g, 1920 * slot + 160 * ((3 * at + 2) // 2), 160))

    @pl.when((at == 5) | (at == 6))
    def _():
        wait(r.put(g, 1920 * slot + 1280 + 256 * (at - 5), 256))

    @pl.when(at == 7)
    def _():
        wait(r.put(g, 1920 * slot + 1792, 128))


def columns_task(r, g, slot, f, more):
    i = 8 + 8 * slot + f
    b = i % 2
    r.next_slabs(i)
    cols = pl.ds(pl.multiple_of(f * 512, 512), 512)

    def block(rows):
        gate = dot(r.a[rows, :], r.ws[b, 0], ((1,), (0,)))
        up = dot(r.a[rows, :], r.ws[b, 1], ((1,), (0,)))
        dp = dot(r.d[rows, :], r.wds[b], ((1,), (1,))).astype(BF).astype(F32)
        sig = jax.nn.sigmoid(gate)
        silu = gate * sig
        r.p[rows, cols] = (silu * up).astype(BF)
        r.dgu[rows, 0:512] = (dp * up * (sig * (1 + gate * (1 - sig)))).astype(BF)
        r.dgu[rows, 512:1024] = (dp * silu).astype(BF)

    token_blocks(256, block)

    @pl.when(more)
    def _():
        wait(r.put(g, 1920 * slot + 160 * (f - 1), 160))

    def gradients(k):
        a = r.a[:, pl.ds(pl.multiple_of(k * 640, 640), 640)]
        of_gate = dot(a, r.dgu[:, 0:512], ((0,), (0,)))
        of_up = dot(a, r.dgu[:, 512:1024], ((0,), (0,)))
        low = lax.broadcasted_iota(jnp.int32, (8, 128), 0) < 4
        for pair in range(16):
            row = 40 * pair
            for half in range(2):
                parts = ([], [])
                for ct in (2 * half, 2 * half + 1):
                    tile = slice(128 * ct, 128 * ct + 128)
                    gm, um = of_gate[row + 16 : row + 24, tile], of_up[row + 16 : row + 24, tile]
                    parts[0].extend((of_gate[row : row + 16, tile], of_up[row : row + 16, tile], jnp.where(low, gm, pltpu.roll(um, 4, 0))))
                    parts[1].extend((of_gate[row + 24 : row + 40, tile], of_up[row + 24 : row + 40, tile], jnp.where(low, pltpu.roll(gm, 4, 0), um)))
                for odd in range(2):
                    at = (2 * k + pair // 8, pair // 2 % 4, pair % 2 * 2 + odd)
                    r.out[at + (slice(80 * half, 80 * half + 80),)] = jnp.concatenate(parts[odd], 0).astype(BF)

    loop(2, gradients)
    start(r.put(g, 1920 * slot + 160 * f, 160))

    @pl.when(slot == 0)
    def _():
        def block(rows):
            more = dot(r.dgu[rows, 0:512], r.ws[b, 0], ((1,), (1,))) + dot(r.dgu[rows, 512:1024], r.ws[b, 1], ((1,), (1,)))
            add_to(r.da, rows, f == 0, more)

        token_blocks(256, block)


def down_task(r, g, slot, t, width):
    cols = pl.ds(pl.multiple_of(t * 512, 512), width)

    def block(k):
        of_down = dot(r.p[:, pl.ds(pl.multiple_of(k * 512, 512), 512)], r.d[:, cols], ((0,), (0,)))
        for ct in range(width // 128):
            part = of_down[:, 128 * ct : 128 * ct + 128].reshape(2, 4, 64, 128).astype(BF)
            r.out[k // 2, pl.ds(k % 2 * 2, 2), :, 64 * ct : 64 * ct + 64, :] = part

    loop(8, block)
    start(r.put(g, 1920 * slot + 1280 + 256 * t, width // 2))


def next_layer(r):
    start(r.back_h())
    wait(r.back_h())

    def block(rows):
        wide = r.state[rows, :].astype(F32)
        d = r.da[rows, :].astype(BF).astype(F32)
        scale = lax.rsqrt(jnp.mean(wide * wide, -1, keepdims=True) + 1e-6)
        along = jnp.mean(wide * d, -1, keepdims=True)
        through = (scale * d - wide * (scale * scale * scale) * along).astype(BF)
        r.d[rows, :] = (r.d[rows, :].astype(F32) + through.astype(F32)).astype(BF)

    token_blocks(128, block)


def comm_kernel(r, g, params, moments, wall, moments_out,
                recv1, send2, recv2, own, sa, b1s, b1r, b2s, b2r, sb, c1s, c1r, c2s, c2r,
                gm, gw, gn, dm, dw, dn, wn, ssem, rsem, lsem):
    n_super = SUPER
    me = lax.axis_index("dp")
    pos = {"x": me // 16, "y": (me // 4) % 4, "z": me % 4}
    low = (U // 2 + 15) // 16 * 16
    halves = (pl.ds(0, 2), pl.ds(2, 2))
    row_halves = (pl.ds(0, low), pl.ds(low, U - low))

    def peer(axis, by):
        return {"dp": me + ((pos[axis] + by) % 4 - pos[axis]) * STRIDE[axis]}

    barrier = pltpu.get_barrier_semaphore()
    for axis in AXES:
        for by in (1, 3):
            pl.semaphore_signal(barrier, inc=1, device_id=peer(axis, by), device_id_type=pl.DeviceIdType.MESH)
    forward(r)
    pl.semaphore_wait(barrier, 6)

    def part(ref, fixed, rows):
        return ref.at[tuple(fixed.get(axis, slice(None)) for axis in AXES) + (rows, slice(None))]

    def remote(kind, slot, c, way, src, dst, axis):
        return pltpu.make_async_remote_copy(
            src_ref=src, dst_ref=dst, send_sem=ssem.at[kind, slot, c, way], recv_sem=rsem.at[kind, slot, c, way],
            device_id=peer(axis, (1, 3)[way]), device_id_type=pl.DeviceIdType.MESH)

    def local(kind, slot, c, src, dst):
        return pltpu.make_async_copy(src, dst, lsem.at[kind, slot, c])

    class Chunk:
        def __init__(self, c, j):
            self.c, self.slot = c, j % 2
            self.A, self.B, self.C = ORDERS[c]
            self.rest = tuple(axis for axis in AXES if axis != self.A)
            self.ib = self.rest.index(self.B)
            self.rows = pl.ds(pl.multiple_of((3 * j + c) * U, 16), U)
            self.k, self.layer = (3 * j + c) % 24, 1 - (3 * j + c) // 24
            self.a, self.b, self.c3 = (pos[axis] for axis in ORDERS[c])

        def unit(self, b, i):
            return (b, i) if self.ib == 0 else (i, b)

        def row_part(self, rows):
            return pl.ds(self.rows.start + rows.start, rows.size)

        def a1(self):
            s, c = self.slot, self.c
            return [remote(0, s, c, way, part(g, {self.A: (self.a + 2) % 4, self.rest[0]: halves[way]}, self.rows),
                           recv1.at[s, c, halves[way]], self.A) for way in (0, 1)]

        def load2(self):
            s, c = self.slot, self.c
            return [local(way, s, c, part(g, {self.A: (self.a + (1, 3)[way]) % 4}, self.rows), send2.at[s, c, way]) for way in (0, 1)]

        def load_own(self):
            return [local(2, self.slot, self.c, part(g, {self.A: self.a}, self.rows), own.at[self.slot, self.c])]

        def a2(self):
            s, c = self.slot, self.c
            return [remote(1, s, c, way, send2.at[s, c, way], recv2.at[s, c, way], self.A) for way in (0, 1)]

        def b1(self):
            s, c = self.slot, self.c
            return [remote(2, s, c, way, b1s.at[s, c, halves[way]], b1r.at[s, c, halves[way]], self.B) for way in (0, 1)]

        def b2(self):
            s, c = self.slot, self.c
            return [remote(3, s, c, way, b2s.at[s, c, way], b2r.at[s, c, way], self.B) for way in (0, 1)]

        def c1(self):
            s, c = self.slot, self.c
            return [remote(4, s, c, way, c1s.at[s, c, row_halves[way]], c1r.at[s, c, row_halves[way]], self.C) for way in (0, 1)]

        def c2(self):
            s, c = self.slot, self.c
            return [remote(5, s, c, way, c2s.at[s, c, way], c2r.at[s, c, way], self.C) for way in (0, 1)]

        def of_columns(self, out):
            s, c = self.slot, self.c
            cols = pl.ds(pl.multiple_of(self.k * 256, 256), 256)
            pairs = []
            for i in range(4):
                which = i // 2 * 3 + i % 2
                if out:
                    pairs.append((gn.at[s, c, i], moments_out[which].at[self.layer, :, cols]))
                else:
                    pairs.append((moments[which].at[self.layer, :, cols], gm.at[s, c, i]))
            if not out:
                rows = pl.ds(pl.multiple_of(me // 2 * 40, 8), 40)
                pairs += [(params[i].at[self.layer, rows, cols], gw.at[s, c, i]) for i in range(2)]
            return [local((10 if out else 3) + i, s, c, *pair) for i, pair in enumerate(pairs)]

        def of_down(self, out, q):
            s, c = self.slot, self.c
            tile = 5 * (self.k - 16) // 4
            pairs = []
            for n, (first, rows, at) in enumerate(((16 * q, 64 - 16 * q, 0), (0, 16 + 16 * q, 64 - 16 * q))):
                cols = pl.ds(pl.multiple_of((tile + n) * 128, 128), 128)
                there, here = pl.ds(first, rows), pl.ds(at, rows)
                for i in range(2):
                    if out:
                        pairs.append((dn.at[s, c, i, here], moments_out[3 * i + 2].at[self.layer, there, cols]))
                    else:
                        pairs.append((moments[3 * i + 2].at[self.layer, there, cols], dm.at[s, c, i, here]))
                if not out:
                    mine = pl.ds(pl.multiple_of(me * 64 + first, 16), rows)
                    pairs.append((params[2].at[self.layer, mine, cols], dw.at[s, c, here]))
            return [local((10 if out else 3) + i, s, c, *pair) for i, pair in enumerate(pairs)]

        def step_copies(self, out, act):
            @pl.when(self.k < 16)
            def _():
                act(self.of_columns(out))

            for q in range(4):
                @pl.when((self.k >= 16) & (self.k % 4 == q))
                def _():
                    act(self.of_down(out, q))

        def store_new(self):
            mine = part(wall, {self.A: self.a, self.B: self.b, self.C: self.c3}, self.rows)
            return [local(9, self.slot, self.c, wn.at[self.slot, self.c], mine)]

        def gather(self, which):
            s, c = self.slot, self.c
            if which < 2:
                axis, here, fixed, kind = self.C, self.c3, {self.A: self.a, self.B: self.b}, 6
            elif which < 4:
                axis, here, fixed, kind = self.B, self.b, {self.A: self.a}, 8
            else:
                axis, here, fixed, kind = self.A, self.a, {}, 10
            if which % 2 == 0:
                block = part(wall, fixed | {axis: here}, self.rows)
                src = wn.at[s, c] if which == 0 else block
                return [remote(kind, s, c, way, src, block, axis) for way in (0, 1)]
            out = []
            for way in (0, 1):
                block = fixed | {axis: (here + (3, 1)[way]) % 4}
                rows = self.rows
                if which == 1:
                    rows = self.row_part(row_halves[way])
                elif which == 3:
                    block[self.C] = halves[way]
                else:
                    block[self.rest[0]] = halves[way]
                half = part(wall, block, rows)
                out.append(remote(kind + 1, s, c, way, half, half, axis))
            return out

    def stage0(k):
        start(k.a1())
        start(k.load2())

    def stage1(k):
        wait(k.load2())
        wait(k.a1())
        s, c = k.slot, k.c

        def body(i):
            for way in (0, 1):
                at = (s, c, 2 * way + i // 4, i % 4)
                to = (s, c, way, 2 * way + i // 4, i % 4)
                send2[to] = (send2[to].astype(F32) + recv1[at].astype(F32)).astype(BF)

        loop(8, body)
        start(k.a2())
        start(k.load_own())

    def stage2(k):
        wait(k.load_own())
        wait(k.a2())
        s, c = k.slot, k.c

        def body(i):
            at = (i // 4, i % 4)
            total = own[(s, c) + at].astype(F32) + recv2[(s, c, 0) + at].astype(F32) + recv2[(s, c, 1) + at].astype(F32)
            sa[(s, c) + at] = total

        loop(16, body)
        far = (k.b + 2) % 4

        def pack(i):
            b1s[s, c, i] = sa[(s, c) + k.unit(far, i)].astype(BF)

        loop(4, pack)
        start(k.b1())

    def stage3(k):
        wait(k.b1())
        s, c = k.slot, k.c
        near = ((k.b + 1) % 4, (k.b + 3) % 4)

        def body(i):
            for way in (0, 1):
                b2s[s, c, way, 2 * way + i] = (sa[(s, c) + k.unit(near[way], 2 * way + i)] + b1r[s, c, 2 * way + i].astype(F32)).astype(BF)
                b2s[s, c, way, 2 - 2 * way + i] = sa[(s, c) + k.unit(near[way], 2 - 2 * way + i)].astype(BF)

        loop(2, body)
        start(k.b2())

    def stage4(k):
        wait(k.b2())
        s, c = k.slot, k.c

        def body(i):
            sb[s, c, i] = sa[(s, c) + k.unit(k.b, i)] + b2r[s, c, 0, i].astype(F32) + b2r[s, c, 1, i].astype(F32)

        loop(4, body)
        c1s[s, c] = sb[s, c, (k.c3 + 2) % 4].astype(BF)
        start(k.c1())

    def stage5(k):
        wait(k.c1())
        s, c = k.slot, k.c
        near = ((k.c3 + 1) % 4, (k.c3 + 3) % 4)
        for way in (0, 1):
            add, keep = row_halves[way], row_halves[1 - way]
            c2s[s, c, way, add] = (sb[s, c, near[way], add] + c1r[s, c, add].astype(F32)).astype(BF)
            c2s[s, c, way, keep] = sb[s, c, near[way], keep].astype(BF)
        start(k.c2())
        k.step_copies(False, start)

    def adamw(old, first, second, grad):
        first = 0.9 * first + 0.1 * grad
        second = 0.95 * second + 0.05 * grad * grad
        return old - 0.02 * (first * lax.rsqrt(second + 1e-8) + 0.1 * old), first, second

    def step_columns(k, grad):
        s, c = k.slot, k.c
        low = lax.broadcasted_iota(jnp.int32, (8, 128), 0) < 4
        odd = me % 2 == 1
        unit = []
        for ct in range(2):
            tile = slice(128 * ct, 128 * ct + 128)
            mix = grad[40 * ct + 32 : 40 * ct + 40]
            turned = pltpu.roll(mix, 4, 0)
            whole, left = [], []
            for i in range(2):
                rest = jnp.where(odd, (turned, mix)[i], (mix, turned)[i])
                rows = jnp.concatenate([grad[40 * ct + 16 * i : 40 * ct + 16 * i + 16], rest], 0)
                rows = jnp.where(odd, pltpu.roll(rows, 4, 0), rows)
                pair = gw[s, c, i, :, tile].astype(F32)
                old = jnp.where(odd, pltpu.roll(pair[16:40], 20, 0), pair[0:24])
                new, first, second = adamw(old, gm[s, c, i, :, tile], gm[s, c, 2 + i, :, tile], rows)
                gn[s, c, i, :, tile] = first
                gn[s, c, 2 + i, :, tile] = second
                new = jnp.where(odd, pltpu.roll(new, 20, 0), new)
                whole.append(new[:16])
                turn = pltpu.roll(new[16:], 4, 0)
                left.append(jnp.where(odd, (turn, new[16:])[i], (new[16:], turn)[i]))
            unit += whole + [jnp.where(low, *left)]
        wn[s, c] = jnp.concatenate(unit, 0).astype(BF)

    def stage6(k):
        k.step_copies(False, wait)
        wait(k.c2())
        s, c = k.slot, k.c
        total = sb[s, c, k.c3] + c2r[s, c, 0].astype(F32) + c2r[s, c, 1].astype(F32)
        grad = total.astype(BF).astype(F32)

        @pl.when(k.k < 16)
        def _():
            step_columns(k, grad)

        @pl.when(k.k >= 16)
        def _():
            new, dn[s, c, 0], dn[s, c, 1] = adamw(dw[s, c].astype(F32), dm[s, c, 0], dm[s, c, 1], grad)
            wn[s, c] = new.astype(BF)

        start(k.gather(0))
        start(k.store_new())
        k.step_copies(True, start)

    def stage7(k):
        wait(k.gather(0))
        start(k.gather(1))

    def stage8(k):
        wait(k.store_new())
        k.step_copies(True, wait)
        wait(k.gather(1))
        start(k.gather(2))

    def later(n):
        def stage(k):
            wait(k.gather(n - 1))
            start(k.gather(n))
        return stage

    def stage12(k):
        wait(k.gather(5))

    stages = (stage0, stage1, stage2, stage3, stage4, stage5, stage6, stage7, stage8, later(3), later(4), later(5), stage12)

    def iteration(s):
        @pl.when(s < n_super)
        def _():
            tasks(r, g, s)

        for number in reversed(range(len(stages))):
            j = s - number

            @pl.when((j >= 0) & (j < n_super))
            def _():
                if number == 0:
                    tasks_done(r, g, s)
                for c in range(3):
                    stages[number](Chunk(c, j))

    loop(n_super + len(stages) - 1, iteration)


def whole_kernel(*refs):
    (x, dy), params, moments = refs[:2], refs[2:5], refs[5:11]
    wall, moments_out, g, h = refs[11], refs[12:18], refs[18], refs[19]
    scratch, n = refs[20:], COMM_SCRATCH
    comm_kernel(Refs((x, dy, *params, h), scratch[n:]), g, params, moments, wall, moments_out, *scratch[:n])


COMM_SCRATCH = 24


def whole_step(x, dy, params, moments):
    hbm = pl.BlockSpec(memory_space=pl.ANY)
    V, two = pltpu.VMEM, (2, 3)
    comm_scratch = [
        V(two + (4, 4, U, 128), BF), V(two + (2, 4, 4, U, 128), BF), V(two + (2, 4, 4, U, 128), BF), V(two + (4, 4, U, 128), BF),
        V(two + (4, 4, U, 128), F32),
        V(two + (4, U, 128), BF), V(two + (4, U, 128), BF), V(two + (2, 4, U, 128), BF), V(two + (2, 4, U, 128), BF), V(two + (4, U, 128), F32),
        V(two + (U, 128), BF), V(two + (U, 128), BF), V(two + (2, U, 128), BF), V(two + (2, U, 128), BF),
        V(two + (4, 24, 256), F32), V(two + (2, 40, 256), BF), V(two + (4, 24, 256), F32),
        V(two + (2, U, 128), F32), V(two + (U, 128), BF), V(two + (2, U, 128), F32), V(two + (U, 128), BF),
        pltpu.SemaphoreType.DMA((12, 2, 3, 2)), pltpu.SemaphoreType.DMA((12, 2, 3, 2)), pltpu.SemaphoreType.DMA((14, 2, 3)),
    ]
    assert len(comm_scratch) == COMM_SCRATCH
    task_scratch = [
        V((TOKENS, D), BF), V((TOKENS, D), BF), V((2, 2, D, 512), BF), V((2, 512, D), BF),
        V((TOKENS, FF), BF), V((TOKENS, 1024), BF), V((TOKENS, D), F32), V((4, 4, 4, 256, 128), BF), pltpu.SemaphoreType.DMA((2, 7)),
    ]
    units = jax.ShapeDtypeStruct((4, 4, 4, ROWS, 128), BF)
    outs = pl.pallas_call(
        whole_kernel,
        out_shape=(units, *(jax.ShapeDtypeStruct(t.shape, F32) for t in moments), units, jax.ShapeDtypeStruct(x.shape, BF)),
        in_specs=[hbm] * 11,
        out_specs=(hbm,) * 9,
        scratch_shapes=comm_scratch + task_scratch,
        compiler_params=pltpu.CompilerParams(collective_id=0, has_side_effects=True, vmem_limit_bytes=67043328),
        name="whole_step",
    )(x, dy, *params, *moments)
    return outs[0], outs[1:7]


UNPACK = 8


def unpack_kernel(w_ref, gate, up, down):
    low = lax.broadcasted_iota(jnp.int32, (8, 128), 0) < 4

    def of_device(d):
        for ct in range(10):
            down[0, pl.ds(pl.multiple_of(64 * d, 64), 64), ct * 128 : ct * 128 + 128] = w_ref[d, 1280 + 64 * ct : 1344 + 64 * ct, :]

    loop(UNPACK, of_device)

    def slab(n):
        rows = pl.ds(pl.multiple_of(80 * n, 16), 80)
        units = [w_ref[d, rows, :].astype(F32) for d in range(UNPACK)]
        for ct in range(2):
            own = [u[40 * ct : 40 * ct + 40] for u in units]
            tile = pl.ds(pl.multiple_of(n * 256 + ct * 128, 128), 128)
            for which, out in enumerate((gate, up)):
                parts = []
                for even, odd in zip(own[::2], own[1::2], strict=True):
                    left, right = even[32:40], odd[32:40]
                    if which == 0:
                        right = pltpu.roll(right, 4, 0)
                    else:
                        left = pltpu.roll(left, 4, 0)
                    parts += [even[16 * which : 16 * which + 16], jnp.where(low, left, right), odd[16 * which : 16 * which + 16]]
                out[0, :, tile] = jnp.concatenate(parts, 0).astype(BF)

    loop(16, slab)


def unpack(wall):
    shapes = ((2, D, FF), (2, D, FF), (2, FF, D))
    blocks = 64 // UNPACK
    return pl.pallas_call(
        unpack_kernel,
        grid=(2, blocks),
        out_shape=tuple(jax.ShapeDtypeStruct(s, BF) for s in shapes),
        in_specs=[pl.BlockSpec((UNPACK, ROWS // 2, 128), lambda l, i: (i, l, 0))],
        out_specs=tuple(pl.BlockSpec((1, s[1] // blocks, s[2]), lambda l, i: (1 - l, i, 0)) for s in shapes),
        cost_estimate=pl.CostEstimate(flops=10**6, bytes_accessed=126 * 10**6, transcendentals=0),
        name="unpack",
    )(wall)


def solution(mesh):
    def step(x, dy, *arrays):
        moments = [jnp.pad(t, ((0, 0), (0, -t.shape[1] % 8), (0, 0))) for t in arrays[3:]]
        wall, new = whole_step(x[0], dy[0], arrays[:3], moments)
        return (*unpack(wall.reshape(64, ROWS, 128)), *(t[:, : old.shape[1]] for t, old in zip(new, arrays[3:], strict=True)))

    seq, whole, rows = P(("rep", "dp")), P(), P(None, "dp", None)
    return jax.shard_map(
        step,
        mesh=mesh,
        in_specs=(seq, seq) + (whole,) * 3 + (rows,) * 6,
        out_specs=(P("rep"),) * 3 + (P("rep", "dp", None),) * 6,
        check_vma=False,
    )
```

time: 721 us -> 649 us (0.900)
  matrix products: 54.1 us -> 0 us
  Pallas kernels: 593 us -> 629 us
  local copies, waits for them, and re-layouts: 43.3 us -> 18.9 us
  other arithmetic: 23.8 us -> 0 us
    dot_general x3 -> x0, matrix products: 54.1 us -> none  [dot(): return lax.dot_general(a, b, (dims, ((), ())), preferred_element_type=F32)]
    pallas_call x2, Pallas kernels: 593 us -> 629 us  [the longest x1 581 us: whole_step(): pl.pallas_call(whole_kernel, out_shape=(units, *(jax.ShapeDtypeStruct(t.s...]
    transpose x9 -> x0, local copies, waits for them, and re-layouts: 15.1 us -> none  [the longest x1 7.88 us: step(): a.transpose(0, 2, 1)]
    unnamed x24 -> x18, local copies, waits for them, and re-layouts: 4.56 us -> 15.2 us
    reshape x10 -> x0, local copies, waits for them, and re-layouts: 10 us -> none  [the longest x2 3.93 us: from_units(): units[:, :1280].reshape(2, 32, 40, 128).transpose(0, 2, 1, 3)]
    select_n x7 -> x0, other arithmetic: 9.94 us -> none  [the longest x3 5.13 us: to_units(): gate, up = (jnp.where(odd, jnp.roll(t, -4, 1), t) for t in (gate, up))]
where the time goes in v4:
time: 649 us
  Pallas kernels  629 us (97%)
  local copies, waits for them, and re-layouts  18.9 us (3%)
    pallas_call x1, Pallas kernels, whole_step(): pl.pallas_call(whole_kernel, out_shape=(units, *(jax.ShapeDtypeStruct(t.s...  581 us
    pallas_call x1, Pallas kernels, unpack(): pl.pallas_call(unpack_kernel, grid=(2, blocks), out_shape=tuple((jax.Shap...  47.7 us
    unnamed x18, local copies, waits for them, and re-layouts  15.2 us

profile of v4, /device:TPU:0, one launch (start us, length us, event | category | flops | bytes accessed | tf_op | source)
XLA Modules:
  0.0 648.7 jit_solution(6645693384092416284)
XLA Ops:
  0.6 1.5 copy.20
  2.1 0.9 pad.13.refs_5_
  3.0 1.5 copy.21
  4.5 0.9 pad.14.refs_6_
  5.5 1.5 copy.22
  6.9 0.9 pad.15.refs_8_
  7.9 1.5 copy.23
  9.3 0.9 pad.16.refs_9_
  10.3 581.4 %whole_step.1 = (bf16[4,4,4,3840,128]{4,3,2,1,0:T(8,128)(2,1)}, f32[2,24,4096]{2,1,0:T(8,128)}, f32[2,24,4096]{2,1,0:T(8,128)}, f32[2,64,1280]{2,1,0:T(8,128)}, ...) custom-call(bf16[1024,1280]{1,0:T(8,128)(2,1)} %bitcast.8, ...), custom_call_target="tpu_custom_call" | custom-call | tf_op jit(solution)/shard_map/whole_step/pallas_call | solution.py:609
  591.7 2.5 copy.24
  594.2 0.0 copy-start.2
  594.2 0.0 copy-start.1
  594.2 0.0 copy-start
  594.2 0.0 copy-start.3
  594.2 47.7 %unpack.1 = (bf16[2,1280,4096]{2,1,0:T(8,128)(2,1)}, bf16[2,1280,4096]{2,1,0:T(8,128)(2,1)}, bf16[2,4096,1280]{2,1,0:T(8,128)(2,1)}) custom-call(bf16[64,3840,128]{2,1,0:T(8,128)(2,1)} %bitcast.7), custom_call_target="tpu_custom_call" | custom-call | flops 1000000 | bytes 126000000 | tf_op jit(solution)/shard_map/unpack/pallas_call | solution.py:656
  641.9 0.0 copy-done.2
  641.9 1.3 copy.25
  643.2 0.0 copy-done.1
  643.2 1.3 copy.26
  644.5 0.0 copy-done
  644.5 1.3 copy.27
  645.9 2.0 copy.30
  647.9 0.0 copy-done.3
  647.9 0.8 copy.31
Async XLA Ops:
  594.2 47.7 %copy-start.2 = (f32[2,24,4096]{2,1,0:T(8,128)S(1)}, f32[2,24,4096]{2,1,0:T(8,128)}, u32[]{:S(2)}) copy-start(f32[2,24,4096]{2,1,0:T(8,128)} %get-tuple-element.24) | copy-start | bytes 2359300
  594.2 49.0 %copy-start.1 = (f32[2,24,4096]{2,1,0:T(8,128)S(1)}, f32[2,24,4096]{2,1,0:T(8,128)}, u32[]{:S(2)}) copy-start(f32[2,24,4096]{2,1,0:T(8,128)} %get-tuple-element.26) | copy-start | bytes 2359300
  594.2 50.4 %copy-start = (f32[2,24,4096]{2,1,0:T(8,128)S(1)}, f32[2,24,4096]{2,1,0:T(8,128)}, u32[]{:S(2)}) copy-start(f32[2,24,4096]{2,1,0:T(8,128)} %get-tuple-element.27) | copy-start | bytes 2359300
  594.2 53.7 %copy-start.3 = (f32[2,64,1280]{2,1,0:T(8,128)S(1)}, f32[2,64,1280]{2,1,0:T(8,128)}, u32[]{:S(2)}) copy-start(f32[2,64,1280]{2,1,0:T(8,128)} %get-tuple-element.55) | copy-start | bytes 1966084

commit v5 on v4

--- a/solution.py
+++ b/solution.py
@@ -1,3 +1,5 @@
+import functools
+
 import jax
 import jax.numpy as jnp
 from jax import lax
@@ -34,26 +36,27 @@
 
 class Refs:
     def __init__(self, operands, buffers):
-        self.x, self.dy, self.wg, self.wu, self.wd, self.h = operands
+        self.x, self.dy, self.wg, self.wu, self.wd, self.h, self.kept = operands
         self.a, self.d, self.ws, self.wds, self.p, self.dgu, self.da, self.out, self.sem = buffers
         self.state = self.p.at[:, FF - D :]
 
     def slabs(self, i):
-        slot, layer = i % 2, i // 8 % 2
-        cols = pl.ds(pl.multiple_of(i % 8 * 512, 512), 512)
-        pairs = ((self.wg.at[layer, :, cols], self.ws.at[slot, 0]), (self.wu.at[layer, :, cols], self.ws.at[slot, 1]),
-                 (self.wd.at[layer, cols, :], self.wds.at[slot]))
+        slot, layer = i % 2, (i // 8 + 1) // 2 % 2
+        pairs = [(self.wd.at[layer, pl.ds(pl.multiple_of(i % 8 * 512, 512), 512), :], self.wds.at[slot])]
+        for n in range(4):
+            cols = pl.ds(pl.multiple_of(i % 8 * 512 + n // 2 * 256, 256), 256)
+            pairs.append(((self.wg, self.wu)[n % 2].at[layer, :, cols], self.ws.at[slot, :, 256 * n : 256 * n + 256]))
         return [pltpu.make_async_copy(src, dst, self.sem.at[slot, n]) for n, (src, dst) in enumerate(pairs)]
 
     def next_slabs(self, i):
         wait(self.slabs(i))
 
-        @pl.when(i < 23)
+        @pl.when(i < 31)
         def _():
             start(self.slabs(i + 1))
 
     def copy(self, n, src, dst):
-        return [pltpu.make_async_copy(src, dst, self.sem.at[n // 4, 3 + n % 4])]
+        return [pltpu.make_async_copy(src, dst, self.sem.at[n // 6, 5 + n % 6])]
 
     def load_x(self):
         return self.copy(0, self.x, self.state)
@@ -70,8 +73,14 @@
     def load_a(self):
         return self.copy(4, self.x, self.a)
 
-    def put(self, g, row, n):
-        return self.copy(5, self.out.at[:, :, :, 0:n, :], g.at[:, :, :, pl.ds(pl.multiple_of(row, 16), n), :])
+    def keep(self, f):
+        return self.copy(5 + f % 2, self.dgu.at[f % 2], self.kept.at[f])
+
+    def back(self, f):
+        return self.copy(7 + f % 2, self.kept.at[f], self.dgu.at[f % 2])
+
+    def put(self, g, row, n, at=0, sem=0):
+        return self.copy(9 + sem, self.out.at[:, :, :, pl.ds(pl.multiple_of(at, 16), n), :], g.at[:, :, :, pl.ds(pl.multiple_of(row, 16), n), :])
 
 
 def normed(h):
@@ -93,6 +102,11 @@
         ref[rows, :] += more
 
 
+def gate_and_up(r, rows, b, half):
+    both = dot(r.a[rows, :], r.ws[b, :, 512 * half : 512 * half + 512], ((1,), (0,)))
+    return both[:, :256], both[:, 256:]
+
+
 def forward(r):
     start(r.load_x() + r.slabs(0) + r.load_dy())
     wait(r.load_x())
@@ -107,10 +121,11 @@
         b = f % 2
 
         def block(rows):
-            gate = dot(r.a[rows, :], r.ws[b, 0], ((1,), (0,)))
-            up = dot(r.a[rows, :], r.ws[b, 1], ((1,), (0,)))
-            p = (gate * jax.nn.sigmoid(gate) * up).astype(BF)
-            add_to(r.da, rows, f == 0, dot(p, r.wds[b], ((1,), (0,))))
+            p = []
+            for half in range(2):
+                gate, up = gate_and_up(r, rows, b, half)
+                p.append((gate * jax.nn.sigmoid(gate) * up).astype(BF))
+            add_to(r.da, rows, f == 0, dot(jnp.concatenate(p, 1), r.wds[b], ((1,), (0,))))
 
         token_blocks(256, block)
 
@@ -129,42 +144,53 @@
 def tasks(r, g, s):
     slot, at = s // 8, s % 8
 
-    @pl.when(at < 5)
-    def _():
-        first = (3 * at + 1) // 2
-
-        @pl.when(s == 1)
+    @pl.when(s == 1)
+    def _():
+        wait(r.keep_h())
+
+    @pl.when(s == 8)
+    def _():
+        wait(r.load_a())
+
+        def norm(rows):
+            r.a[rows, :] = normed(r.a[rows, :])
+
+        token_blocks(128, norm)
+
+    def one(n, _):
+        @pl.when(n % 2 == 0)
         def _():
-            wait(r.keep_h())
-
-        @pl.when(s == 8)
-        def _():
-            wait(r.load_a())
-
-            def norm(rows):
-                r.a[rows, :] = normed(r.a[rows, :])
-
-            token_blocks(128, norm)
-
-        def one(f, _):
-            columns_task(r, g, slot, f, f > first)
-
-        lax.fori_loop(first, (3 * at + 4) // 2, one, None)
-
-    @pl.when(s == 5)
-    def _():
-        start(r.load_a())
-
-    @pl.when((at == 5) | (at == 6))
-    def _():
-        down_task(r, g, slot, at - 5, 512)
-
-    @pl.when(at == 7)
-    def _():
-        down_task(r, g, slot, 2, 256)
-
+            hidden_task(r, slot, n // 2)
+
+        columns_task(r, g, slot, n, n % 3)
+
+    lax.fori_loop(jnp.minimum(3 * at, 16), jnp.minimum(3 * at + 3, 16), one, None)
+
+    @pl.when(at == 5)
+    def _():
         @pl.when(slot == 0)
         def _():
+            start(r.load_a())
+            wait(r.keep(7))
+            start(r.back(0))
+            start(r.back(1))
+
+        wait(r.put(g, 1920 * slot + 1200, 80))
+
+    @pl.when((at == 5) | (at == 6))
+    def _():
+        down_task(r, g, slot, at - 5, 512)
+
+    @pl.when(at == 7)
+    def _():
+        down_task(r, g, slot, 2, 256)
+
+    @pl.when((at >= 5) & (slot == 0))
+    def _():
+        lax.fori_loop(3 * (at - 5), jnp.minimum(3 * (at - 4), 8), lambda f, _: da_task(r, f), None)
+
+        @pl.when(at == 7)
+        def _():
             next_layer(r)
 
 
@@ -173,7 +199,8 @@
 
     @pl.when(at < 5)
     def _():
-        wait(r.put(g, 1920 * slot + 160 * ((3 * at + 2) // 2), 160))
+        for n in range(3):
+            wait(r.put(g, 1920 * slot + 80 * (3 * at + n), 80, 80 * n, n))
 
     @pl.when((at == 5) | (at == 6))
     def _():
@@ -184,56 +211,73 @@
         wait(r.put(g, 1920 * slot + 1792, 128))
 
 
-def columns_task(r, g, slot, f, more):
-    i = 8 + 8 * slot + f
+def hidden_task(r, slot, f):
+    i = 8 + 16 * slot + f
     b = i % 2
     r.next_slabs(i)
-    cols = pl.ds(pl.multiple_of(f * 512, 512), 512)
+
+    @pl.when((slot == 0) & (f > 0))
+    def _():
+        wait(r.keep(f - 1))
 
     def block(rows):
-        gate = dot(r.a[rows, :], r.ws[b, 0], ((1,), (0,)))
-        up = dot(r.a[rows, :], r.ws[b, 1], ((1,), (0,)))
         dp = dot(r.d[rows, :], r.wds[b], ((1,), (1,))).astype(BF).astype(F32)
-        sig = jax.nn.sigmoid(gate)
-        silu = gate * sig
-        r.p[rows, cols] = (silu * up).astype(BF)
-        r.dgu[rows, 0:512] = (dp * up * (sig * (1 + gate * (1 - sig)))).astype(BF)
-        r.dgu[rows, 512:1024] = (dp * silu).astype(BF)
+        for half in range(2):
+            gate, up = gate_and_up(r, rows, b, half)
+            sig = jax.nn.sigmoid(gate)
+            silu = gate * sig
+            d = dp[:, 256 * half : 256 * half + 256]
+            r.p[rows, pl.ds(pl.multiple_of(f * 512 + 256 * half, 256), 256)] = (silu * up).astype(BF)
+            r.dgu[b, rows, 512 * half : 512 * half + 256] = (d * up * (sig * (1 + gate * (1 - sig)))).astype(BF)
+            r.dgu[b, rows, 512 * half + 256 : 512 * half + 512] = (d * silu).astype(BF)
 
     token_blocks(256, block)
 
-    @pl.when(more)
-    def _():
-        wait(r.put(g, 1920 * slot + 160 * (f - 1), 160))
+    @pl.when(slot == 0)
+    def _():
+        start(r.keep(f))
+
+
+def columns_task(r, g, slot, n, region):
+    b = n // 2 % 2
+    cols = pl.ds(pl.multiple_of(n % 2 * 512, 512), 512)
 
     def gradients(k):
-        a = r.a[:, pl.ds(pl.multiple_of(k * 640, 640), 640)]
-        of_gate = dot(a, r.dgu[:, 0:512], ((0,), (0,)))
-        of_up = dot(a, r.dgu[:, 512:1024], ((0,), (0,)))
+        of_both = dot(r.a[:, pl.ds(pl.multiple_of(k * 640, 640), 640)], r.dgu[b, :, cols], ((0,), (0,)))
         low = lax.broadcasted_iota(jnp.int32, (8, 128), 0) < 4
         for pair in range(16):
             row = 40 * pair
-            for half in range(2):
-                parts = ([], [])
-                for ct in (2 * half, 2 * half + 1):
-                    tile = slice(128 * ct, 128 * ct + 128)
-                    gm, um = of_gate[row + 16 : row + 24, tile], of_up[row + 16 : row + 24, tile]
-                    parts[0].extend((of_gate[row : row + 16, tile], of_up[row : row + 16, tile], jnp.where(low, gm, pltpu.roll(um, 4, 0))))
-                    parts[1].extend((of_gate[row + 24 : row + 40, tile], of_up[row + 24 : row + 40, tile], jnp.where(low, pltpu.roll(gm, 4, 0), um)))
-                for odd in range(2):
-                    at = (2 * k + pair // 8, pair // 2 % 4, pair % 2 * 2 + odd)
-                    r.out[at + (slice(80 * half, 80 * half + 80),)] = jnp.concatenate(parts[odd], 0).astype(BF)
+            parts = ([], [])
+            for ct in range(2):
+                gate, up = (of_both[row : row + 40, at + 128 * ct : at + 128 * ct + 128] for at in (0, 256))
+                gm, um = gate[16:24], up[16:24]
+                parts[0].extend((gate[:16], up[:16], jnp.where(low, gm, pltpu.roll(um, 4, 0))))
+                parts[1].extend((gate[24:], up[24:], jnp.where(low, pltpu.roll(gm, 4, 0), um)))
+            for odd in range(2):
+                at = (2 * k + pair // 8, pair // 2 % 4, pair % 2 * 2 + odd)
+                r.out[at + (pl.ds(pl.multiple_of(80 * region, 16), 80),)] = jnp.concatenate(parts[odd], 0).astype(BF)
 
     loop(2, gradients)
-    start(r.put(g, 1920 * slot + 160 * f, 160))
-
-    @pl.when(slot == 0)
-    def _():
-        def block(rows):
-            more = dot(r.dgu[rows, 0:512], r.ws[b, 0], ((1,), (1,))) + dot(r.dgu[rows, 512:1024], r.ws[b, 1], ((1,), (1,)))
-            add_to(r.da, rows, f == 0, more)
-
-        token_blocks(256, block)
+    for m in range(3):
+        @pl.when(region == m)
+        def _():
+            start(r.put(g, 1920 * slot + 80 * n, 80, 80 * m, m))
+
+
+def da_task(r, f):
+    i = 16 + f
+    r.next_slabs(i)
+    wait(r.back(f))
+    b = i % 2
+
+    def block(rows):
+        add_to(r.da, rows, f == 0, dot(r.dgu[b, rows, :], r.ws[b], ((1,), (1,))))
+
+    token_blocks(256, block)
+
+    @pl.when(f < 6)
+    def _():
+        start(r.back(f + 2))
 
 
 def down_task(r, g, slot, t, width):
@@ -266,7 +310,7 @@
 
 def comm_kernel(r, g, params, moments, wall, moments_out,
                 recv1, send2, recv2, own, sa, b1s, b1r, b2s, b2r, sb, c1s, c1r, c2s, c2r,
-                gm, gw, gn, dm, dw, dn, wn, ssem, rsem, lsem):
+                gm, gw, gn, rows24, dm, dw, dn, wn, ssem, rsem, lsem):
     n_super = SUPER
     me = lax.axis_index("dp")
     pos = {"x": me // 16, "y": (me // 4) % 4, "z": me % 4}
@@ -509,9 +553,11 @@
                 rows = jnp.where(odd, pltpu.roll(rows, 4, 0), rows)
                 pair = gw[s, c, i, :, tile].astype(F32)
                 old = jnp.where(odd, pltpu.roll(pair[16:40], 20, 0), pair[0:24])
-                new, first, second = adamw(old, gm[s, c, i, :, tile], gm[s, c, 2 + i, :, tile], rows)
+                new, first, second = adamw(old[:20], gm[s, c, i, :, tile], gm[s, c, 2 + i, :, tile], rows[:20])
                 gn[s, c, i, :, tile] = first
                 gn[s, c, 2 + i, :, tile] = second
+                rows24[ct, i, 0:20] = new
+                new = rows24[ct, i]
                 new = jnp.where(odd, pltpu.roll(new, 20, 0), new)
                 whole.append(new[:16])
                 turn = pltpu.roll(new[16:], 4, 0)
@@ -580,12 +626,12 @@
 
 def whole_kernel(*refs):
     (x, dy), params, moments = refs[:2], refs[2:5], refs[5:11]
-    wall, moments_out, g, h = refs[11], refs[12:18], refs[18], refs[19]
-    scratch, n = refs[20:], COMM_SCRATCH
-    comm_kernel(Refs((x, dy, *params, h), scratch[n:]), g, params, moments, wall, moments_out, *scratch[:n])
-
-
-COMM_SCRATCH = 24
+    wall, moments_out, g, kept = refs[11], refs[12:18], refs[18], refs[19:21]
+    scratch, n = refs[21:], COMM_SCRATCH
+    comm_kernel(Refs((x, dy, *params, *kept), scratch[n:]), g, params, moments, wall, moments_out, *scratch[:n])
+
+
+COMM_SCRATCH = 25
 
 
 def whole_step(x, dy, params, moments):
@@ -596,21 +642,21 @@
         V(two + (4, 4, U, 128), F32),
         V(two + (4, U, 128), BF), V(two + (4, U, 128), BF), V(two + (2, 4, U, 128), BF), V(two + (2, 4, U, 128), BF), V(two + (4, U, 128), F32),
         V(two + (U, 128), BF), V(two + (U, 128), BF), V(two + (2, U, 128), BF), V(two + (2, U, 128), BF),
-        V(two + (4, 24, 256), F32), V(two + (2, 40, 256), BF), V(two + (4, 24, 256), F32),
+        V(two + (4, 20, 256), F32), V(two + (2, 40, 256), BF), V(two + (4, 20, 256), F32), V((2, 2, 24, 128), F32),
         V(two + (2, U, 128), F32), V(two + (U, 128), BF), V(two + (2, U, 128), F32), V(two + (U, 128), BF),
         pltpu.SemaphoreType.DMA((12, 2, 3, 2)), pltpu.SemaphoreType.DMA((12, 2, 3, 2)), pltpu.SemaphoreType.DMA((14, 2, 3)),
     ]
     assert len(comm_scratch) == COMM_SCRATCH
     task_scratch = [
-        V((TOKENS, D), BF), V((TOKENS, D), BF), V((2, 2, D, 512), BF), V((2, 512, D), BF),
-        V((TOKENS, FF), BF), V((TOKENS, 1024), BF), V((TOKENS, D), F32), V((4, 4, 4, 256, 128), BF), pltpu.SemaphoreType.DMA((2, 7)),
+        V((TOKENS, D), BF), V((TOKENS, D), BF), V((2, D, 1024), BF), V((2, 512, D), BF),
+        V((TOKENS, FF), BF), V((2, TOKENS, 1024), BF), V((TOKENS, D), F32), V((4, 4, 4, 256, 128), BF), pltpu.SemaphoreType.DMA((2, 11)),
     ]
     units = jax.ShapeDtypeStruct((4, 4, 4, ROWS, 128), BF)
     outs = pl.pallas_call(
         whole_kernel,
-        out_shape=(units, *(jax.ShapeDtypeStruct(t.shape, F32) for t in moments), units, jax.ShapeDtypeStruct(x.shape, BF)),
+        out_shape=(units, *(jax.ShapeDtypeStruct(t.shape, F32) for t in moments), units, jax.ShapeDtypeStruct(x.shape, BF), jax.ShapeDtypeStruct((8, TOKENS, 1024), BF)),
         in_specs=[hbm] * 11,
-        out_specs=(hbm,) * 9,
+        out_specs=(hbm,) * 10,
         scratch_shapes=comm_scratch + task_scratch,
         compiler_params=pltpu.CompilerParams(collective_id=0, has_side_effects=True, vmem_limit_bytes=67043328),
         name="whole_step",
@@ -621,33 +667,34 @@
 UNPACK = 8
 
 
-def unpack_kernel(w_ref, gate, up, down):
+def unpack_kernel(first, second, third, gate, up, down):
     low = lax.broadcasted_iota(jnp.int32, (8, 128), 0) < 4
 
     def of_device(d):
         for ct in range(10):
-            down[0, pl.ds(pl.multiple_of(64 * d, 64), 64), ct * 128 : ct * 128 + 128] = w_ref[d, 1280 + 64 * ct : 1344 + 64 * ct, :]
+            down[0, pl.ds(pl.multiple_of(64 * d, 64), 64), ct * 128 : ct * 128 + 128] = third[d, 64 * ct : 64 * ct + 64, :]
 
     loop(UNPACK, of_device)
 
     def slab(n):
         rows = pl.ds(pl.multiple_of(80 * n, 16), 80)
-        units = [w_ref[d, rows, :].astype(F32) for d in range(UNPACK)]
-        for ct in range(2):
-            own = [u[40 * ct : 40 * ct + 40] for u in units]
-            tile = pl.ds(pl.multiple_of(n * 256 + ct * 128, 128), 128)
-            for which, out in enumerate((gate, up)):
-                parts = []
-                for even, odd in zip(own[::2], own[1::2], strict=True):
-                    left, right = even[32:40], odd[32:40]
-                    if which == 0:
-                        right = pltpu.roll(right, 4, 0)
-                    else:
-                        left = pltpu.roll(left, 4, 0)
-                    parts += [even[16 * which : 16 * which + 16], jnp.where(low, left, right), odd[16 * which : 16 * which + 16]]
-                out[0, :, tile] = jnp.concatenate(parts, 0).astype(BF)
-
-    loop(16, slab)
+        for at, ref in ((0, first), (2048, second)):
+            units = [ref[d, rows, :].astype(F32) for d in range(UNPACK)]
+            for ct in range(2):
+                own = [u[40 * ct : 40 * ct + 40] for u in units]
+                tile = pl.ds(pl.multiple_of(n * 256 + at + ct * 128, 128), 128)
+                for which, out in enumerate((gate, up)):
+                    parts = []
+                    for even, odd in zip(own[::2], own[1::2], strict=True):
+                        left, right = even[32:40], odd[32:40]
+                        if which == 0:
+                            right = pltpu.roll(right, 4, 0)
+                        else:
+                            left = pltpu.roll(left, 4, 0)
+                        parts += [even[16 * which : 16 * which + 16], jnp.where(low, left, right), odd[16 * which : 16 * which + 16]]
+                    out[0, :, tile] = jnp.concatenate(parts, 0).astype(BF)
+
+    loop(8, slab)
 
 
 def unpack(wall):
@@ -657,18 +704,17 @@
         unpack_kernel,
         grid=(2, blocks),
         out_shape=tuple(jax.ShapeDtypeStruct(s, BF) for s in shapes),
-        in_specs=[pl.BlockSpec((UNPACK, ROWS // 2, 128), lambda l, i: (i, l, 0))],
+        in_specs=[pl.BlockSpec((UNPACK, 640, 128), functools.partial(lambda third, l, i: (i, 3 * l + third, 0), third)) for third in range(3)],
         out_specs=tuple(pl.BlockSpec((1, s[1] // blocks, s[2]), lambda l, i: (1 - l, i, 0)) for s in shapes),
         cost_estimate=pl.CostEstimate(flops=10**6, bytes_accessed=126 * 10**6, transcendentals=0),
         name="unpack",
-    )(wall)
+    )(wall, wall, wall)
 
 
 def solution(mesh):
     def step(x, dy, *arrays):
-        moments = [jnp.pad(t, ((0, 0), (0, -t.shape[1] % 8), (0, 0))) for t in arrays[3:]]
-        wall, new = whole_step(x[0], dy[0], arrays[:3], moments)
-        return (*unpack(wall.reshape(64, ROWS, 128)), *(t[:, : old.shape[1]] for t, old in zip(new, arrays[3:], strict=True)))
+        wall, moments = whole_step(x[0], dy[0], arrays[:3], arrays[3:])
+        return (*unpack(wall.reshape(64, ROWS, 128)), *moments)
 
     seq, whole, rows = P(("rep", "dp")), P(), P(None, "dp", None)
     return jax.shard_map(

time: 649 us -> 645 us (level)
  no operation moved by 1% of the time
where the time goes in v5:
time: 645 us
  Pallas kernels  626 us (97%)
  local copies, waits for them, and re-layouts  18.7 us (3%)
    pallas_call x1, Pallas kernels, whole_step(): pl.pallas_call(whole_kernel, out_shape=(units, *(jax.ShapeDtypeStruct(t.s...  578 us
    pallas_call x1, Pallas kernels, unpack(): pl.pallas_call(unpack_kernel, grid=(2, blocks), out_shape=tuple((jax.Shap...  47.6 us
    unnamed x18, local copies, waits for them, and re-layouts  18.7 us

profile of v5, /device:TPU:0, one launch (start us, length us, event | category | flops | bytes accessed | tf_op | source)
XLA Modules:
  0.0 645.0 jit_solution(3984735519188077181)
XLA Ops:
  0.6 2.3 copy.20.refs_5_
  3.0 2.3 copy.21.refs_6_
  5.3 2.3 copy.22.refs_8_
  7.7 2.3 copy.23.refs_9_
  10.0 578.0 %whole_step.1 = (bf16[4,4,4,3840,128]{4,3,2,1,0:T(8,128)(2,1)}, f32[2,20,4096]{2,1,0:T(8,128)}, f32[2,20,4096]{2,1,0:T(8,128)}, f32[2,64,1280]{2,1,0:T(8,128)}, ...) custom-call(bf16[1024,1280]{1,0:T(8,128)(2,1)} %bitcast.6, ...), custom_call_target="tpu_custom_call" | custom-call | tf_op jit(solution)/shard_map/whole_step/pallas_call | solution.py:655
  588.0 0.0 copy-start.3
  588.0 0.0 copy-start.2
  588.0 0.0 copy-start.1
  588.0 0.0 copy-start
  588.0 47.6 %unpack.1 = (bf16[2,1280,4096]{2,1,0:T(8,128)(2,1)}, bf16[2,1280,4096]{2,1,0:T(8,128)(2,1)}, bf16[2,4096,1280]{2,1,0:T(8,128)(2,1)}) custom-call(bf16[64,3840,128]{2,1,0:T(8,128)(2,1)} %bitcast.3, bf16[64,3840,128]{2,1,0:T(8,128)(2,1)} %bitcast.4, bf16[64,3840,128]{2,1,0:T(8,128)(2,1)} %bitcast.5), custom_call_target="tpu_custom_call" | custom-call | flops 1000000 | bytes 126000000 | tf_op jit(solution)/shard_map/unpack/pallas_call | solution.py:703
  635.7 0.0 copy-done.3
  635.7 1.3 copy.24
  637.0 0.0 copy-done.2
  637.0 1.3 copy.25
  638.4 0.0 copy-done.1
  638.4 1.3 copy.26
  639.7 0.0 copy-done
  639.7 1.3 copy.27
  641.1 2.0 copy.30
  643.0 2.0 copy.31
Async XLA Ops:
  588.0 47.7 %copy-start.3 = (f32[2,20,4096]{2,1,0:T(8,128)S(1)}, f32[2,20,4096]{2,1,0:T(8,128)}, u32[]{:S(2)}) copy-start(f32[2,20,4096]{2,1,0:T(8,128)} %get-tuple-element.32) | copy-start | bytes 1966084
  588.0 49.0 %copy-start.2 = (f32[2,20,4096]{2,1,0:T(8,128)S(1)}, f32[2,20,4096]{2,1,0:T(8,128)}, u32[]{:S(2)}) copy-start(f32[2,20,4096]{2,1,0:T(8,128)} %get-tuple-element.33) | copy-start | bytes 1966084
  588.0 50.4 %copy-start.1 = (f32[2,20,4096]{2,1,0:T(8,128)S(1)}, f32[2,20,4096]{2,1,0:T(8,128)}, u32[]{:S(2)}) copy-start(f32[2,20,4096]{2,1,0:T(8,128)} %get-tuple-element.35) | copy-start | bytes 1966084
  588.0 51.7 %copy-start = (f32[2,20,4096]{2,1,0:T(8,128)S(1)}, f32[2,20,4096]{2,1,0:T(8,128)}, u32[]{:S(2)}) copy-start(f32[2,20,4096]{2,1,0:T(8,128)} %get-tuple-element.36) | copy-start | bytes 1966084
